TPU v7x, 16 devices: a whole 2x2x2 slice. The times are simulated.
16 devices in a mesh: cp: 4 (over z, y), fsdp: 4 (over x, core).
Axes of the slice: x: 2, y: 2, z: 2, core: 2. Of those that a mesh axis runs over, the one named last changes fastest.
Arguments:
- x_in: bfloat16 [16, 2048, 1152], P('fsdp', 'cp')
- grad_out: bfloat16 [16, 2048, 1152], P('fsdp', 'cp')
- seg_id: int32 [16, 2048], P('fsdp', 'cp')
- seg_pos: int32 [16, 2048], P('fsdp', 'cp')
- norm_scale: float32 [1152], P(('cp', 'fsdp'))
- w_q: float32 [1152, 1024], P(('cp', 'fsdp'))
- w_k: float32 [1152, 256], P(('cp', 'fsdp'))
- w_v: float32 [1152, 256], P(('cp', 'fsdp'))
- w_o: float32 [1024, 1152], P(('cp', 'fsdp'))
- b_o: float32 [1152], P(('cp', 'fsdp'))
- w_up1: float32 [1152, 6912], P(('cp', 'fsdp'))
- b_up1: float32 [6912], P(('cp', 'fsdp'))
- w_up2: float32 [1152, 6912], P(('cp', 'fsdp'))
- b_up2: float32 [6912], P(('cp', 'fsdp'))
- w_down: float32 [6912, 1152], P(('cp', 'fsdp'))
- b_down: float32 [1152], P(('cp', 'fsdp'))
Outputs:
- output 1: bfloat16 [16, 2048, 1152], P('fsdp', 'cp')
- output 2: bfloat16 [16, 2048, 1152], P('fsdp', 'cp')
- output 3: float32 [1152], P(('cp', 'fsdp'))
- output 4: float32 [1152, 1024], P(('cp', 'fsdp'))
- output 5: float32 [1152, 256], P(('cp', 'fsdp'))
- output 6: float32 [1152, 256], P(('cp', 'fsdp'))
- output 7: float32 [1024, 1152], P(('cp', 'fsdp'))
- output 8: float32 [1152], P(('cp', 'fsdp'))
- output 9: float32 [1152, 6912], P(('cp', 'fsdp'))
- output 10: float32 [6912], P(('cp', 'fsdp'))
- output 11: float32 [1152, 6912], P(('cp', 'fsdp'))
- output 12: float32 [6912], P(('cp', 'fsdp'))
- output 13: float32 [6912, 1152], P(('cp', 'fsdp'))
- output 14: float32 [1152], P(('cp', 'fsdp'))
All inputs are finite; a program needn't handle non-finite values.
Results may differ from a plain program's by a relative error of at most 0.0176682.
Values are sent between devices in bfloat16 or wider.
A program may use at most 1 GiB of HBM per device.

v0:
```python
import functools
import jax
import jax.numpy as jnp
from jax import lax
from jax.experimental import pallas as pl
from jax.experimental.pallas import tpu as pltpu
from jax.sharding import Mesh, PartitionSpec as P


ROPE_DIMS = 128
HEAD_DIM = 256
N_HEADS = 4
MASKED = -1.6e31
EXP_SCALE = 1.4426950408889634 / 16.0
CHIPS = ('z', 'y', 'x')
ALL_AXES = ('z', 'y', 'x', 'core')
F32 = jnp.float32
BF16 = jnp.bfloat16


def dot_nn(a, b):
    return lax.dot_general(a, b, (((1,), (0,)), ((), ())), preferred_element_type=F32)


def dot_nt(a, b):
    return lax.dot_general(a, b, (((1,), (1,)), ((), ())), preferred_element_type=F32)


def dot_tn(a, b):
    return lax.dot_general(a, b, (((0,), (0,)), ((), ())), preferred_element_type=F32)


def rotate(values, cos_b, sin_b):
    return values * cos_b + pltpu.roll(values, ROPE_DIMS // 2, axis=1) * sin_b


def attn_kernel(ng_ref, wqkv_ref, wo_ref, cos_ref, sin_ref, cosk_ref, sink_ref, segq_ref, segk_ref, out_ref,
                q_s, do_s, k_s, v_s, kt_s, vt_s, mask_s, s_s, p_s, dk_s, dv_s):
    step = pl.program_id(0)
    n_blocks = pl.num_programs(0)
    rows = ng_ref.shape[0]
    d_model = ng_ref.shape[1] // 2
    qk = N_HEADS * HEAD_DIM
    base = pl.multiple_of(step * rows, rows)
    cos_b = cos_ref[...]
    sin_b = sin_ref[...]
    n_blk = ng_ref[:, :d_model]
    g_blk = ng_ref[:, d_model:]

    @pl.when(step == 0)
    def _():
        dk_s[...] = jnp.zeros_like(dk_s)
        dv_s[...] = jnp.zeros_like(dv_s)

    for h in range(N_HEADS):
        lin = dot_nn(n_blk, wqkv_ref[:, h * HEAD_DIM:(h + 1) * HEAD_DIM])
        q_s[h, :, :ROPE_DIMS] = rotate(lin[:, :ROPE_DIMS], cos_b, sin_b).astype(BF16)
        q_s[h, :, ROPE_DIMS:] = lin[:, ROPE_DIMS:].astype(BF16)
        do_s[h] = dot_nt(g_blk, wo_ref[h * HEAD_DIM:(h + 1) * HEAD_DIM, :]).astype(BF16)
    k_lin = dot_nn(n_blk, wqkv_ref[:, qk:qk + HEAD_DIM])
    k_blk = jnp.concatenate([rotate(k_lin[:, :ROPE_DIMS], cos_b, sin_b), k_lin[:, ROPE_DIMS:]], axis=1)
    v_blk = dot_nn(n_blk, wqkv_ref[:, qk + HEAD_DIM:])
    k_s[pl.ds(base, rows), :] = k_blk.astype(BF16)
    v_s[pl.ds(base, rows), :] = v_blk.astype(BF16)
    kt_s[:, pl.ds(base, rows)] = k_blk.T.astype(BF16)
    vt_s[:, pl.ds(base, rows)] = v_blk.T.astype(BF16)

    def block(blk):
        n_chunk = blk + 1
        seg_q = segq_ref[:, :1]
        for c in range(n_chunk):
            same = seg_q == segk_ref[:1, c * rows:(c + 1) * rows]
            if c == blk:
                r_id = lax.broadcasted_iota(jnp.int32, (rows, rows), 0)
                c_id = lax.broadcasted_iota(jnp.int32, (rows, rows), 1)
                same = same & (c_id <= r_id)
            mask_s[:, c * rows:(c + 1) * rows] = jnp.where(same, 1.0, 0.0)

        def head(h, carry):
            q = q_s[h]
            do = do_s[h]
            m_run = None
            for c in range(n_chunk):
                sl = slice(c * rows, (c + 1) * rows)
                s = jnp.where(mask_s[:, sl] > 0.5, dot_nn(q, kt_s[:, sl]), MASKED)
                s_s[:, sl] = s
                m_c = jnp.max(s, axis=1, keepdims=True)
                m_run = m_c if m_run is None else jnp.maximum(m_run, m_c)
            l_run = None
            for c in range(n_chunk):
                sl = slice(c * rows, (c + 1) * rows)
                e = jnp.exp2((s_s[:, sl] - m_run) * EXP_SCALE)
                s_s[:, sl] = e
                l_c = jnp.sum(e, axis=1, keepdims=True)
                l_run = l_c if l_run is None else l_run + l_c
            inv = 1.0 / l_run
            for c in range(n_chunk):
                sl = slice(c * rows, (c + 1) * rows)
                p = s_s[:, sl] * inv
                s_s[:, sl] = p
                p_s[:, sl] = p.astype(BF16)
            o = dot_nn(p_s[:, :n_chunk * rows], v_s[:n_chunk * rows, :])
            delta = jnp.sum(o * do.astype(F32), axis=1, keepdims=True)
            out_ref[pl.ds(base, rows), pl.ds(pl.multiple_of(qk + 2 * HEAD_DIM + h * HEAD_DIM, HEAD_DIM), HEAD_DIM)] = o.astype(BF16)
            dq = None
            for c in range(n_chunk):
                sl = slice(c * rows, (c + 1) * rows)
                ds = (s_s[:, sl] * (dot_nn(do, vt_s[:, sl]) - delta)).astype(BF16)
                dq_c = dot_nn(ds, k_s[sl, :])
                dq = dq_c if dq is None else dq + dq_c
                dk_s[sl, :] += dot_tn(ds, q)
                dv_s[sl, :] += dot_tn(p_s[:, sl], do)
            dq = dq * 0.0625
            dq = jnp.concatenate([rotate(dq[:, :ROPE_DIMS], cos_b, -sin_b), dq[:, ROPE_DIMS:]], axis=1)
            out_ref[pl.ds(base, rows), pl.ds(pl.multiple_of(h * HEAD_DIM, HEAD_DIM), HEAD_DIM)] = dq.astype(BF16)
            return carry

        lax.fori_loop(0, N_HEADS, head, 0)

    for blk in range(4):
        pl.when(step == blk)(functools.partial(block, blk))

    @pl.when(step == n_blocks - 1)
    def _():
        dk = dk_s[...] * 0.0625
        dk = jnp.concatenate([rotate(dk[:, :ROPE_DIMS], cosk_ref[...], -sink_ref[...]), dk[:, ROPE_DIMS:]], axis=1)
        out_ref[:, qk:qk + HEAD_DIM] = dk.astype(BF16)
        out_ref[:, qk + HEAD_DIM:qk + 2 * HEAD_DIM] = dv_s[...].astype(BF16)


def attention(ng_seq, wqkv, wo, cos_b, sin_b, seg_own):
    t_len, both = ng_seq.shape
    rows = t_len // 4
    qk = N_HEADS * HEAD_DIM
    segq = jnp.broadcast_to(seg_own[:, None], (t_len, 128))
    segk = jnp.broadcast_to(seg_own[None, :], (8, t_len))
    row_spec = lambda width: pl.BlockSpec((rows, width), lambda i: (i, 0))
    full = lambda a: pl.BlockSpec(a.shape, lambda i: (0,) * a.ndim, pipeline_mode=pl.Buffered(1))
    width = 2 * (qk + HEAD_DIM)
    return pl.pallas_call(
        attn_kernel,
        grid=(4,),
        in_specs=[row_spec(both), full(wqkv), full(wo), row_spec(ROPE_DIMS), row_spec(ROPE_DIMS), full(cos_b), full(sin_b), row_spec(128), full(segk)],
        out_specs=pl.BlockSpec((t_len, width), lambda i: (0, 0)),
        out_shape=jax.ShapeDtypeStruct((t_len, width), BF16),
        scratch_shapes=[
            pltpu.VMEM((N_HEADS, rows, HEAD_DIM), BF16), pltpu.VMEM((N_HEADS, rows, HEAD_DIM), BF16),
            pltpu.VMEM((t_len, HEAD_DIM), BF16), pltpu.VMEM((t_len, HEAD_DIM), BF16),
            pltpu.VMEM((HEAD_DIM, t_len), BF16), pltpu.VMEM((HEAD_DIM, t_len), BF16),
            pltpu.VMEM((rows, t_len), F32), pltpu.VMEM((rows, t_len), F32), pltpu.VMEM((rows, t_len), BF16),
            pltpu.VMEM((t_len, HEAD_DIM), F32), pltpu.VMEM((t_len, HEAD_DIM), F32)],
        compiler_params=pltpu.CompilerParams(vmem_limit_bytes=60 * 1024 * 1024, dimension_semantics=('arbitrary',)),
        cost_estimate=pl.CostEstimate(flops=45_000_000_000, bytes_accessed=40_000_000, transcendentals=10_000_000),
        name='attn',
    )(ng_seq, wqkv, wo, cos_b, sin_b, cos_b, sin_b, segq, segk)


def norm_kernel(x_ref, g_ref, scale_ref, out_ref):
    d_model = x_ref.shape[1]
    for part in range(0, x_ref.shape[0], 128):
        sl = slice(part, part + 128)
        x_f = x_ref[sl, :].astype(F32)
        inv = lax.rsqrt(jnp.mean(x_f * x_f, axis=1, keepdims=True) + 1e-6)
        out_ref[sl, :d_model] = (x_f * inv * (1.0 + scale_ref[...])).astype(BF16)
        out_ref[sl, d_model:] = g_ref[sl, :]


def norm_and_grad(x_loc, g_loc, scale_f):
    t_len, d_model = x_loc.shape
    rows = 512
    tile = pl.BlockSpec((rows, d_model), lambda i: (i, 0))
    return pl.pallas_call(
        norm_kernel, grid=(t_len // rows,), name='norm',
        in_specs=[tile, tile, pl.BlockSpec(scale_f.shape, lambda i: (0, 0))],
        out_specs=pl.BlockSpec((rows, 2 * d_model), lambda i: (i, 0)),
        out_shape=jax.ShapeDtypeStruct((t_len, 2 * d_model), BF16),
        cost_estimate=pl.CostEstimate(flops=4_000_000_000, bytes_accessed=19_000_000, transcendentals=2048),
    )(x_loc, g_loc, scale_f)


def order_kernel(x_ref, a_ref, b_ref, c_ref, out_ref):
    cp = lax.axis_index('z') * 2 + lax.axis_index('y')
    rows = a_ref.shape[1]
    for flip, ref in enumerate((x_ref.at[cp], a_ref.at[0], b_ref.at[0], c_ref.at[0])):
        out_ref[pl.ds(pl.multiple_of((cp ^ flip) * rows, rows), rows), :] = ref[...]


def order(values, got):
    n_seq, rows, width = values.shape
    return pl.pallas_call(
        order_kernel, out_shape=jax.ShapeDtypeStruct((n_seq * rows, width), values.dtype), name='order',
        compiler_params=pltpu.CompilerParams(vmem_limit_bytes=40 * 1024 * 1024),
        cost_estimate=pl.CostEstimate(flops=2_000_000_000, bytes_accessed=10_000_000, transcendentals=0),
    )(values, *got)


N_PART = 3
EXTRA_GATHER = 1


def split_kernel(w1_ref, w2_ref, keep_ref, send_ref):
    core = lax.axis_index('core')
    d_model = keep_ref.shape[2] // 2
    sub = d_model // 8
    for part in range(N_PART):
        for i, w_ref in enumerate((w1_ref, w2_ref)):
            even, odd = [
                jnp.concatenate([w_ref[:, ((2 * j + k) * N_PART + part) * sub:((2 * j + k) * N_PART + part + 1) * sub] for j in range(8)], axis=1).astype(BF16)
                for k in range(2)]

            @pl.when(core == 0)
            def _():
                keep_ref[part, :, i * d_model:(i + 1) * d_model] = even
                send_ref[part, :, i * d_model:(i + 1) * d_model] = odd

            @pl.when(core == 1)
            def _():
                keep_ref[part, :, i * d_model:(i + 1) * d_model] = odd
                send_ref[part, :, i * d_model:(i + 1) * d_model] = even


def split_up(w1, w2):
    rows, cols = w1.shape
    out = jax.ShapeDtypeStruct((N_PART, rows, cols // N_PART), BF16)
    return pl.pallas_call(split_kernel, out_shape=[out, out], name='split_up')(w1, w2)


def stack_kernel(keep_ref, recv_ref, wd_ref, extra_ref, *out_refs):
    core = lax.axis_index('core')
    rows, cols = keep_ref.shape[1:]
    d_model = wd_ref.shape[1]
    for part, out_ref in enumerate(out_refs):
        own = pl.multiple_of(core * rows, 8)
        out_ref[pl.ds(own, rows), :cols] = keep_ref[part]
        out_ref[pl.ds(pl.multiple_of(rows - own, 8), rows), :cols] = recv_ref[part]
        out_ref[:, cols:cols + d_model] = wd_ref[part * 2 * rows:(part + 1) * 2 * rows, :].astype(BF16)
        if part == EXTRA_GATHER:
            n_extra = extra_ref.shape[0]
            out_ref[:n_extra, cols + d_model:] = extra_ref[...]
            out_ref[n_extra:, cols + d_model:] = jnp.zeros((2 * rows - n_extra, extra_ref.shape[1]), BF16)


def stack_up(keep, recv, w_down, extra):
    _, rows, cols = keep.shape
    width = cols + w_down.shape[1]
    outs = [jax.ShapeDtypeStruct((2 * rows, width + (extra.shape[1] if part == EXTRA_GATHER else 0)), BF16) for part in range(N_PART)]
    return pl.pallas_call(stack_kernel, out_shape=outs, name='stack_up')(keep, recv, w_down, extra)


def unpack_kernel(own_ref, oth_ref, wqkv_ref, wo_ref):
    core = lax.axis_index('core')
    r_o, r_in = wo_ref.shape[0] // 16, wqkv_ref.shape[0] // 16
    d_model = wo_ref.shape[1]
    rows = own_ref.shape[0] // 8
    for chip in range(8):
        for flip, ref in enumerate((own_ref, oth_ref)):
            dev = 2 * chip + (core ^ flip)
            wo_ref[pl.ds(pl.multiple_of(dev * r_o, 8), r_o), :] = ref[chip * rows:chip * rows + r_o, :d_model]
            wqkv_ref[pl.ds(pl.multiple_of(dev * r_in, 8), r_in), :] = ref[chip * rows + r_o:chip * rows + r_o + r_in, :]


def unpack(own, oth, r_o, r_in, d_model):
    return pl.pallas_call(
        unpack_kernel, name='unpack',
        out_shape=[jax.ShapeDtypeStruct((16 * r_in, own.shape[1]), BF16), jax.ShapeDtypeStruct((16 * r_o, d_model), BF16)],
    )(own, oth)


def join_kernel(*refs):
    own_refs, recv_refs, (w1_ref, w2_ref, wd_ref) = refs[:N_PART], refs[N_PART:2 * N_PART], refs[2 * N_PART:]
    core = lax.axis_index('core')
    rows = w1_ref.shape[0]
    d_model = wd_ref.shape[1]
    sub = d_model // 8

    def put(even_of, odd_of):
        for i, w_ref in enumerate((w1_ref, w2_ref)):
            pieces = []
            for j in range(8):
                for of in (even_of, odd_of):
                    for part in range(N_PART):
                        pieces.append(of(part)[:, i * d_model + j * sub:i * d_model + (j + 1) * sub])
            w_ref[...] = jnp.concatenate(pieces, axis=1)

    pl.when(core == 0)(lambda: put(lambda p: own_refs[p][:rows, :2 * d_model], lambda p: recv_refs[p][...]))
    pl.when(core == 1)(lambda: put(lambda p: recv_refs[p][...], lambda p: own_refs[p][rows:, :2 * d_model]))
    for part in range(N_PART):
        wd_ref[part * 2 * rows:(part + 1) * 2 * rows, :] = own_refs[part][:, 2 * d_model:3 * d_model]


def join_up(owns, recvs):
    rows, cols = recvs[0].shape
    d_model = cols // 2
    up = jax.ShapeDtypeStruct((rows, N_PART * cols), F32)
    return pl.pallas_call(
        join_kernel, out_shape=[up, up, jax.ShapeDtypeStruct((N_PART * 2 * rows, d_model), F32)], name='join_up',
    )(*owns, *recvs)


GELU_C = 0.7978845608028654
GELU_A = 0.044715


def hidden_kernel(own_ref, oth_ref, w_ref, b1_ref, b2_ref, *refs):
    extra_refs = refs[:-10]
    act_ref, dh_ref, dw_ref, db_ref, h_s, da_s, ng_s, acc_s, side_s, sems = refs[-10:]
    step = pl.program_id(0)
    last = pl.num_programs(0) - 1
    rows, d_model = da_s.shape
    own = step < pl.num_programs(0) // 2
    ng_s[...] = jnp.where(own, own_ref[...], oth_ref[...])

    @pl.when(step == 0)
    def _():
        acc_s[...] = jnp.zeros_like(acc_s)
        db_ref[...] = jnp.zeros_like(db_ref)

    n_sub = 2
    sub = rows // n_sub
    w12 = w_ref[:, :2 * d_model]
    for i in range(n_sub):
        sl = slice(i * sub, (i + 1) * sub)
        h_s[sl, :] = dot_nn(ng_s[sl, :d_model], w12)
        da_s[sl, :] = dot_nt(ng_s[sl, d_model:], w_ref[:, 2 * d_model:])
    b1 = b1_ref[...]
    b2 = b2_ref[...]
    for i in range(n_sub):
        sl = slice(i * sub, (i + 1) * sub)
        s1 = None
        s2 = None
        for r in range(i * sub, (i + 1) * sub, 64):
            rs = slice(r, r + 64)
            u = h_s[rs, :d_model] + b1
            v = h_s[rs, d_model:] + b2
            da = da_s[rs, :]
            u2 = u * u
            t = jnp.tanh(u * (GELU_C + (GELU_C * GELU_A) * u2))
            half = 0.5 + 0.5 * t
            gelu = u * half
            slope = half + (half * (1.0 - t)) * (u * (GELU_C + (3.0 * GELU_C * GELU_A) * u2))
            d1 = da * v * slope
            d2 = da * gelu
            act_ref[rs, :] = (gelu * v).astype(BF16)
            dh_ref[rs, :d_model] = d1.astype(BF16)
            dh_ref[rs, d_model:] = d2.astype(BF16)
            p1 = jnp.sum(d1.reshape(8, 8, d_model), axis=0)
            p2 = jnp.sum(d2.reshape(8, 8, d_model), axis=0)
            s1 = p1 if s1 is None else s1 + p1
            s2 = p2 if s2 is None else s2 + p2
        db_ref[:8, :] += s1
        db_ref[8:, :] += s2
        acc_s[:, :2 * d_model] += dot_tn(ng_s[sl, :d_model], dh_ref[sl, :])
        acc_s[:, 2 * d_model:] += dot_tn(act_ref[sl, :], ng_s[sl, d_model:])

    if extra_refs:
        keep_ref, got_ref = extra_refs
        block = side_s.shape[1]
        n_extra = keep_ref.shape[1]
        slot = lax.rem(step, 2)

        def side_copy(at_slot, at_step):
            place = dw_ref.at[pl.ds(pl.multiple_of(at_step * block, 8), block), 3 * d_model:]
            return pltpu.make_async_copy(side_s.at[at_slot], place, sems.at[1 + at_slot])

        @pl.when(step >= 2)
        def _():
            side_copy(slot, step - 2).wait()

        side_s[slot, :n_extra, :] = keep_ref[0] + got_ref[0]
        side_s[slot, n_extra:, :] = jnp.zeros((block - n_extra, keep_ref.shape[2]), F32)
        side_copy(slot, step).start()

        @pl.when(step == last)
        def _():
            side_copy(1 - slot, step - 1).wait()
            side_copy(slot, step).wait()

    @pl.when(step == last)
    def _():
        copy = pltpu.make_async_copy(acc_s, dw_ref.at[:, :3 * d_model], sems.at[0])
        copy.start()
        copy.wait()


def hidden_part(ng_own, ng_oth, w_part, b1, b2, extra=()):
    t_len, both = ng_own.shape
    d_model = both // 2
    rows = 512
    steps = 2 * t_len // rows
    half = steps // 2
    own_spec = pl.BlockSpec((rows, both), lambda i: (jnp.minimum(i, half - 1), 0))
    oth_spec = pl.BlockSpec((rows, both), lambda i: (jnp.maximum(i - half, 0), 0))
    full = lambda a, width: pl.BlockSpec((a.shape[0], width), lambda i: (0, 0), pipeline_mode=pl.Buffered(1))
    row = lambda width: pl.BlockSpec((rows, width), lambda i: (i, 0))
    blk = [pl.BlockSpec((1,) + a.shape[1:], lambda i: (i, 0, 0)) for a in extra]
    side = (2, d_model // 8, extra[0].shape[2]) if extra else (2, 8, 128)
    return pl.pallas_call(
        hidden_kernel,
        grid=(steps,),
        in_specs=[own_spec, oth_spec, full(w_part, 3 * d_model), full(b1, d_model), full(b2, d_model)] + blk,
        out_specs=[row(d_model), row(2 * d_model), pl.BlockSpec(memory_space=pl.ANY), pl.BlockSpec((16, d_model), lambda i: (0, 0))],
        out_shape=[jax.ShapeDtypeStruct((2 * t_len, d_model), BF16), jax.ShapeDtypeStruct((2 * t_len, 2 * d_model), BF16),
                   jax.ShapeDtypeStruct((d_model, 3 * d_model + (extra[0].shape[2] if extra else 0)), F32), jax.ShapeDtypeStruct((16, d_model), F32)],
        scratch_shapes=[pltpu.VMEM((rows, 2 * d_model), F32), pltpu.VMEM((rows, d_model), F32), pltpu.VMEM((rows, both), BF16),
                        pltpu.VMEM((d_model, 3 * d_model), F32), pltpu.VMEM(side, F32), pltpu.SemaphoreType.DMA((3,))],
        compiler_params=pltpu.CompilerParams(vmem_limit_bytes=63 * 1024 * 1024, dimension_semantics=('arbitrary',)),
        cost_estimate=pl.CostEstimate(flops=65_000_000_000, bytes_accessed=70_000_000, transcendentals=4_700_000),
        name='hidden',
    )(ng_own, ng_oth, w_part, b1, b2, *extra)


def attn_grad_kernel(n_ref, dqkv_ref, o_lo_ref, o_hi_ref, g_ref, keep_ref, send_ref):
    step = pl.program_id(0)
    core = lax.axis_index('core')
    r_o, r_in = o_lo_ref.shape[1] // 8, n_ref.shape[1] // 16
    width = dqkv_ref.shape[1]
    d_model = g_ref.shape[1]

    def put(rows, cols, value_of):
        for dev in range(16):
            for ref, flip in ((keep_ref, 0), (send_ref, 1)):
                @pl.when((core ^ flip) == dev % 2)
                def _():
                    ref[dev // 2, rows, cols] = value_of(dev)

    d_wqkv = dot_tn(n_ref[...], dqkv_ref[...])
    put(slice(r_o, r_o + r_in), slice(0, width), lambda dev: d_wqkv[dev * r_in:(dev + 1) * r_in])

    def low(first_col, used):
        g_cols = g_ref[:, first_col:first_col + used]
        d_wo = [dot_tn(o_lo_ref[...], g_cols), dot_tn(o_hi_ref[...], g_cols)]
        put(slice(0, r_o), slice(0, used), lambda dev: d_wo[dev // 8][dev % 8 * r_o:(dev % 8 + 1) * r_o])
        if used < width:
            put(slice(0, r_o), slice(used, width), lambda dev: jnp.zeros((r_o, width - used), F32))

    for i in range(-(-d_model // width)):
        pl.when(step == i)(functools.partial(low, i * width, min(width, d_model - i * width)))


def attn_grad(ng_seq, od_seq, r_o, r_in):
    t_len, both = ng_seq.shape
    d_model = both // 2
    width = 512
    qk = N_HEADS * HEAD_DIM
    total = qk + 2 * HEAD_DIM
    out = jax.ShapeDtypeStruct((8, r_o + r_in, total), F32)
    out_spec = pl.BlockSpec((8, r_o + r_in, width), lambda i: (0, 0, i))
    one = pl.Buffered(1)
    return pl.pallas_call(
        attn_grad_kernel,
        grid=(total // width,),
        in_specs=[pl.BlockSpec((t_len, d_model), lambda i: (0, 0), pipeline_mode=one), pl.BlockSpec((t_len, width), lambda i: (0, i)),
                  pl.BlockSpec((t_len, width), lambda i: (0, total // width), pipeline_mode=one), pl.BlockSpec((t_len, width), lambda i: (0, total // width + 1), pipeline_mode=one),
                  pl.BlockSpec((t_len, d_model), lambda i: (0, 1), pipeline_mode=one)],
        out_specs=[out_spec, out_spec],
        out_shape=[out, out],
        compiler_params=pltpu.CompilerParams(vmem_limit_bytes=60 * 1024 * 1024, dimension_semantics=('arbitrary',)),
        cost_estimate=pl.CostEstimate(flops=12_000_000_000, bytes_accessed=33_000_000, transcendentals=0),
        name='attn_grad',
    )(ng_seq, od_seq, od_seq, od_seq, ng_seq)


def out_products(act_refs, dh_refs, w_refs):
    d_model = act_refs[0].shape[1]
    out = None
    d_n = None
    for act_ref, dh_ref, w_ref in zip(act_refs, dh_refs, w_refs):
        o_part = dot_nn(act_ref[...], w_ref[:, 2 * d_model:3 * d_model])
        n_part = dot_nt(dh_ref[...], w_ref[:, :2 * d_model])
        out = o_part if out is None else out + o_part
        d_n = n_part if d_n is None else d_n + n_part
    return out, d_n


def out_other_kernel(*refs):
    out, d_n = out_products(refs[:3], refs[3:6], refs[6:9])
    refs[9][...] = out
    refs[10][...] = d_n


def out_specs_of(rows, d_model, first_block):
    tile = lambda width: pl.BlockSpec((rows, width), lambda i: (i + first_block, 0))
    full = pl.BlockSpec((d_model, 3 * d_model), lambda i: (0, 0), pipeline_mode=pl.Buffered(1))
    return [tile(d_model)] * 3 + [tile(2 * d_model)] * 3 + [full] * 3


def out_other(acts, dhs, w_parts):
    t_len, d_model = acts[0].shape[0] // 2, acts[0].shape[1]
    rows = 256
    tile = pl.BlockSpec((rows, d_model), lambda i: (i, 0))
    out = jax.ShapeDtypeStruct((t_len, d_model), F32)
    return pl.pallas_call(
        out_other_kernel,
        grid=(t_len // rows,),
        in_specs=out_specs_of(rows, d_model, t_len // rows),
        out_specs=[tile, tile],
        out_shape=[out, out],
        compiler_params=pltpu.CompilerParams(vmem_limit_bytes=60 * 1024 * 1024, dimension_semantics=('arbitrary',)),
        cost_estimate=pl.CostEstimate(flops=49_000_000_000, bytes_accessed=86_000_000, transcendentals=0),
        name='out_other',
    )(*acts, *dhs, *w_parts)


def out_own_kernel(*refs):
    (od_ref, wo_ref, wqkv_ref, x_ref, g_ref, got_o_ref, got_n_ref, scale_ref, bias_ref, x_out_ref, d_x_ref, sums_ref) = refs[9:]
    d_model = x_ref.shape[1]

    @pl.when(pl.program_id(0) == 0)
    def _():
        sums_ref[...] = jnp.zeros_like(sums_ref)

    out, d_n = out_products(refs[:3], refs[3:6], refs[6:9])
    split = wqkv_ref.shape[1]
    out = out + dot_nn(od_ref[:, split:], wo_ref[...])
    d_n = d_n + dot_nt(od_ref[:, :split], wqkv_ref[...])
    x_f = x_ref[...].astype(F32)
    g_f = g_ref[...].astype(F32)
    x_out_ref[...] = (x_f + out + got_o_ref[...] + bias_ref[...]).astype(BF16)
    d_n = d_n + got_n_ref[...]
    inv = lax.rsqrt(jnp.mean(x_f * x_f, axis=1, keepdims=True) + 1e-6)
    scaled = d_n * (1.0 + scale_ref[...])
    xn = x_f * inv
    proj = jnp.mean(scaled * xn, axis=1, keepdims=True)
    d_x_ref[...] = (g_f + inv * (scaled - xn * proj)).astype(BF16)
    rows = x_f.shape[0]
    sums_ref[:8, :] += jnp.sum((d_n * xn).reshape(rows // 8, 8, d_model), axis=0)
    sums_ref[8:, :] += jnp.sum(g_f.reshape(rows // 8, 8, d_model), axis=0)


def out_own(acts, dhs, w_parts, od_loc, wo, wqkv, x_loc, ng_own, got_o, got_n, scale_f, bias_f):
    t_len, d_model = x_loc.shape
    rows = 256
    tile = lambda width: pl.BlockSpec((rows, width), lambda i: (i, 0))
    full = lambda a: pl.BlockSpec(a.shape, lambda i: (0, 0), pipeline_mode=pl.Buffered(1))
    out = jax.ShapeDtypeStruct((t_len, d_model), BF16)
    return pl.pallas_call(
        out_own_kernel,
        grid=(t_len // rows,),
        in_specs=out_specs_of(rows, d_model, 0) + [tile(od_loc.shape[1]), full(wo), full(wqkv), tile(d_model), pl.BlockSpec((rows, d_model), lambda i: (i, 1))]
                 + [tile(d_model)] * 2 + [full(scale_f), full(bias_f)],
        out_specs=[tile(d_model), tile(d_model), pl.BlockSpec((16, d_model), lambda i: (0, 0))],
        out_shape=[out, out, jax.ShapeDtypeStruct((16, d_model), F32)],
        compiler_params=pltpu.CompilerParams(vmem_limit_bytes=63 * 1024 * 1024, dimension_semantics=('arbitrary',)),
        cost_estimate=pl.CostEstimate(flops=61_000_000_000, bytes_accessed=125_000_000, transcendentals=0),
        name='out_own',
    )(*acts, *dhs, *w_parts, od_loc, wo, wqkv, x_loc, ng_own, got_o, got_n, scale_f, bias_f)


def pack_kernel(wq_ref, wk_ref, wv_ref, wo_ref, out_ref):
    r_o, d_model = wo_ref.shape
    qk = wq_ref.shape[1]
    out_ref[:r_o, :d_model] = wo_ref[...].astype(BF16)
    out_ref[:r_o, d_model:] = jnp.zeros((r_o, out_ref.shape[1] - d_model), BF16)
    out_ref[r_o:, :qk] = wq_ref[...].astype(BF16)
    out_ref[r_o:, qk:qk + HEAD_DIM] = wk_ref[...].astype(BF16)
    out_ref[r_o:, qk + HEAD_DIM:] = wv_ref[...].astype(BF16)


def pack(w_q, w_k, w_v, w_o):
    out = jax.ShapeDtypeStruct((w_o.shape[0] + w_q.shape[0], w_q.shape[1] + 2 * HEAD_DIM), BF16)
    return pl.pallas_call(pack_kernel, out_shape=out, name='pack')(w_q, w_k, w_v, w_o)


def vector_kernel(scale_ref, bo_ref, bd_ref, b1_ref, b2_ref, out_ref, side_s):
    side_s[...] = jnp.zeros_like(side_s)
    for row, ref in enumerate((scale_ref, bo_ref, bd_ref, b1_ref, b2_ref)):
        side_s[row:row + 1, :ref.shape[1]] = ref[...]
    out_ref[...] = side_s[...].astype(BF16)


def vectors(*parts):
    width = -(-max(part.shape[0] for part in parts) // 128) * 128
    return pl.pallas_call(
        vector_kernel, out_shape=jax.ShapeDtypeStruct((8, width), BF16), scratch_shapes=[pltpu.VMEM((8, width), F32)], name='vectors',
    )(*[part[None] for part in parts])


def solution(mesh):
    mesh4 = Mesh(mesh.devices.reshape(2, 2, 2, 2), ALL_AXES)
    tok_spec = P(('x', 'core'), ('z', 'y'), None)
    pos_spec = P(('x', 'core'), ('z', 'y'))
    vec_spec = P(ALL_AXES)
    mat_spec = P(ALL_AXES, None)
    param_specs = (vec_spec, mat_spec, mat_spec, mat_spec, mat_spec, vec_spec, mat_spec, vec_spec, mat_spec, vec_spec, mat_spec, vec_spec)

    def swap_core(values):
        return lax.ppermute(values, 'core', [(0, 1), (1, 0)])

    def send_blocks(values, cp_index):
        got = []
        for flip in (1, 2, 3):
            sent = lax.dynamic_index_in_dim(values, cp_index ^ flip, 0, keepdims=True)
            got.append(lax.ppermute(sent, ('z', 'y'), [(i, i ^ flip) for i in range(4)]))
        return got

    def local_step(x_in, grad_out, seg_id, seg_pos, norm_scale, w_q, w_k, w_v, w_o, b_o, w_up1, b_up1, w_up2, b_up2, w_down, b_down):
        n_seq, piece, d_model = x_in.shape
        t_len = n_seq * piece
        core = lax.axis_index('core')
        cp_index = lax.axis_index('z') * 2 + lax.axis_index('y')
        first = core == 0
        r_in = w_q.shape[0]
        r_o = w_o.shape[0]
        f_blk = b_up1.shape[0]
        sub = f_blk // N_PART
        qk = N_HEADS * HEAD_DIM

        def after(value, *deps):
            return lax.optimization_barrier((value,) + deps)[0]

        keep, send = split_up(w_up1, w_up2)
        shards = stack_up(keep, swap_core(send), w_down, pack(w_q, w_k, w_v, w_o))

        def gather(shard):
            return lax.all_gather(shard, CHIPS, axis=0, tiled=True)

        w_parts = [gather(shards[0])]

        vec_all = lax.all_gather(vectors(norm_scale, b_o, b_down, b_up1, b_up2), ALL_AXES, axis=0)
        scale_f, bo_f, bd_f = [vec_all[:, i, :r_in].reshape(1, d_model).astype(F32) for i in range(3)]
        b_ups = []
        for row in (3, 4):
            both = vec_all[:, row, :f_blk].reshape(8, 2, N_PART, sub)
            mine = jnp.where(first, both[:, 0], both[:, 1]).astype(F32)
            b_ups.append([mine[:, part].reshape(1, d_model) for part in range(N_PART)])

        x_loc = x_in.reshape(t_len, d_model)
        g_loc = grad_out.reshape(t_len, d_model)
        ng_own = norm_and_grad(x_loc, g_loc, scale_f)
        ng_oth = swap_core(ng_own)
        w_parts.append(gather(shards[1]))
        w_parts.append(gather(shards[2]))

        seg_pack = jnp.stack([seg_id, seg_pos], axis=1)
        seg_got = send_blocks(seg_pack, cp_index)
        seg_all = jnp.zeros_like(seg_pack)
        for flip, got in enumerate([lax.dynamic_index_in_dim(seg_pack, cp_index, 0, keepdims=True)] + seg_got):
            seg_all = lax.dynamic_update_slice_in_dim(seg_all, got, cp_index ^ flip, 0)
        seg_own = seg_all[:, 0].reshape(t_len)
        pos_own = seg_all[:, 1].reshape(t_len)
        half = ROPE_DIMS // 2
        inv_freq = 10000.0 ** (-jnp.arange(half, dtype=F32) / half)
        angle = pos_own.astype(F32)[:, None] * inv_freq
        cos_a = jnp.cos(angle)
        sin_a = jnp.sin(angle)
        cos_b = jnp.concatenate([cos_a, cos_a], axis=1)
        sin_b = jnp.concatenate([-sin_a, sin_a], axis=1)
        ng_blocks = ng_own.reshape(n_seq, piece, 2 * d_model)
        ng_seq = order(ng_blocks, send_blocks(after(ng_blocks, w_parts[0]), cp_index))

        acts, dhs, dbs, owns, recvs = [], [], [], [], []

        def third(part, ng_in, extra=()):
            act, dh, d_w, db = hidden_part(ng_in, ng_oth, w_parts[part], b_ups[0][part], b_ups[1][part], extra)
            own = lax.psum_scatter(d_w, CHIPS, scatter_dimension=0, tiled=True)
            recvs.append(swap_core(jnp.where(first, own[r_in:, :2 * d_model], own[:r_in, :2 * d_model])))
            acts.append(act)
            dhs.append(dh)
            dbs.append(jnp.sum(db.reshape(2, 8, d_model), axis=1).reshape(2, 8, sub))
            owns.append(own)

        third(0, ng_own)
        third(1, after(ng_own, dbs[0]))
        extra_own = w_parts[1][:, 3 * d_model:]
        wqkv, wo = unpack(extra_own, swap_core(extra_own), r_o, r_in, d_model)
        od_seq = attention(after(ng_seq, dbs[1]), wqkv, wo, cos_b, sin_b, seg_own)
        d_keep, d_send = attn_grad(ng_seq, od_seq, r_o, r_in)
        third(2, ng_own, (d_keep, swap_core(d_send)))
        od_blocks = od_seq.reshape(n_seq, piece, -1)
        od_loc = order(od_blocks, send_blocks(od_blocks, cp_index))

        out_oth, dn_oth = out_other(acts, dhs, w_parts)
        x_out, d_x, sums = out_own(acts, dhs, w_parts, od_loc, wo, wqkv, x_loc, ng_own, swap_core(out_oth), swap_core(dn_oth), scale_f, bo_f + bd_f)
        x_out = x_out.reshape(n_seq, piece, d_model)
        d_x = d_x.reshape(n_seq, piece, d_model)

        sums = jnp.sum(sums.reshape(2, 8, d_model), axis=1).reshape(2, 16, r_in)
        db = jnp.stack(dbs, axis=2).reshape(2, 8, f_blk)
        zero = jnp.zeros_like(db)
        db = jnp.where(first, jnp.stack([db, zero], axis=2), jnp.stack([zero, db], axis=2)).reshape(2, 16, f_blk)
        small = jnp.concatenate([sums[0], sums[1], db[0], db[1]], axis=1)
        small = lax.psum(small, ALL_AXES)
        small = lax.dynamic_index_in_dim(small, lax.axis_index(ALL_AXES), 0, keepdims=False)
        g_scale, g_bias, g_b1, g_b2 = small[:r_in], small[r_in:2 * r_in], small[2 * r_in:2 * r_in + f_blk], small[2 * r_in + f_blk:]

        g_w1, g_w2, g_wd = join_up(owns, recvs)
        g_attn = owns[2][:r_o + r_in, 3 * d_model:]
        g_wo, g_wq, g_wk, g_wv = g_attn[:r_o, :d_model], g_attn[r_o:, :qk], g_attn[r_o:, qk:qk + HEAD_DIM], g_attn[r_o:, qk + HEAD_DIM:]
        return (x_out, d_x, g_scale, g_wq, g_wk, g_wv, g_wo, g_bias, g_w1, g_b1, g_w2, g_b2, g_wd, g_bias)

    in_specs = (tok_spec, tok_spec, pos_spec, pos_spec) + param_specs
    out_specs = (tok_spec, tok_spec) + param_specs
    return jax.shard_map(local_step, mesh=mesh4, in_specs=in_specs, out_specs=out_specs, check_vma=False)
```

profile of v0, /device:TPU:0, one launch (start us, length us, event | category | flops | bytes accessed | tf_op | source)
XLA Modules:
  0.0 1099.0 jit_solution(4849850353086228386)
XLA Ops:
  7.2 4.8 split_up.1
  12.0 0.7 collective-permute-start.1
  12.8 1.9 pack.1.extra_ref
  15.2 0.9 copy-done
  16.1 4.1 stack_up.1
  20.3 0.7 all-gather.7.cloned.1.call-update
  21.1 1.4 vectors.1
  22.5 15.1 %all-gather = bf16[128,512]{1,0:T(8,128)(2,1)S(1)} all-gather(bf16[8,512]{1,0:T(8,128)(2,1)} %vectors.1), channel_id=2, replica_groups=mesh['z'=2,'y'=2,'x'=2,'core'=2] {'z','y','x','core'}, dimensions={0}, use_global_device_ids=true | all-gather | bytes 139264 | tf_op jit(solution)/shard_map/all_gather | solution.py:619
  37.5 0.6 fusion.12
  38.2 0.7 reshape.151.scale_ref.refs_16_
  38.9 8.7 norm.1.own_ref.refs_13_
  48.5 0.6 slice_reduce_fusion
  49.1 0.7 reshape_squeeze.31.b2_ref
  49.8 0.6 slice_reduce_fusion.1
  50.4 0.7 reshape_squeeze.29.b1_ref
  51.1 11.4 %collective-permute-done.oth_ref = bf16[2048,2304]{1,0:T(8,128)(2,1)} collective-permute-done((bf16[2048,2304]{1,0:T(8,128)(2,1)}, bf16[2048,2304]{1,0:T(8,128)(2,1)}, u32[]{:S(2)}, u32[]{:S(2)}) %collective-permute-start) | collective-permute-done | bytes 9437216 | tf_op jit(solution)/shard_map/ppermute | solution.py:587
  62.5 32.1 %all-gather.5.cloned.1.call-done.w_ref.refs_6_ = bf16[1152,3456]{1,0:T(8,128)(2,1)} async-done(((bf16[144,3456]{1,0:T(8,128)(2,1)}), bf16[1152,3456]{1,0:T(8,128)(2,1)}) %all-gather.5.cloned.1.call-update) | async-done | bytes 7962640 | tf_op jit(solution)/shard_map/all_gather | solution.py:615
  94.6 93.0 %hidden.3 = (bf16[4096,1152]{1,0:T(8,128)(2,1)}, bf16[4096,2304]{1,0:T(8,128)(2,1)}, f32[1152,3456]{1,0:T(8,128)}, f32[16,1152]{1,0:T(8,128)}) custom-call(bf16[2048,2304]{1,0:T(8,128)(2,1)} %norm.1.own_ref.refs_13_, bf16[2048,2304]{1,0:T(8,128)(2,1)} %collective-permute-done.oth_ref, bf16[1152,3456]{1,0:T(8,128)(2,1)} %all-gather.5.cloned.1.call-done.w_ref.refs_6_, ...), custom_call_target="tpu_custom_call" | custom-call | flops 65000001536 | bytes 70000000 | tf_op jit(solution)/shard_map/hidden/pallas_call | solution.py:397
  188.1 0.7 reshape_squeeze.33.b2_ref
  188.8 0.7 reshape_squeeze.32.b1_ref
  189.5 1.8 all-gather.7.cloned.1.call-done.w_ref.refs_7_
  191.3 93.3 %hidden.4 = (bf16[4096,1152]{1,0:T(8,128)(2,1)}, bf16[4096,2304]{1,0:T(8,128)(2,1)}, f32[1152,3456]{1,0:T(8,128)}, f32[16,1152]{1,0:T(8,128)}) custom-call(bf16[2048,2304]{1,0:T(8,128)(2,1)} %norm.1.own_ref.refs_13_, bf16[2048,2304]{1,0:T(8,128)(2,1)} %collective-permute-done.oth_ref, bf16[1152,4992]{1,0:T(8,128)(2,1)} %all-gather.7.cloned.1.call-done.w_ref.refs_7_, ...), custom_call_target="tpu_custom_call" | custom-call | flops 65000001536 | bytes 70000000 | tf_op jit(solution)/shard_map/hidden/pallas_call | solution.py:397
  284.7 4.2 slice.182.own_ref
  288.9 6.5 constant_dynamic-slice_fusion.4
  295.4 2.4 collective-permute-start.4
  297.7 0.6 collective-permute-start.3
  298.9 1.5 collective-permute-start.6
  300.4 144.3 %collective-permute-done.6 = s32[1,2,512]{2,0,1:T(1,128)S(1)} collective-permute-done((s32[1,2,512]{2,0,1:T(1,128)S(1)}, s32[1,2,512]{2,0,1:T(1,128)S(1)}, u32[]{:S(2)}, u32[]{:S(2)}) %collective-permute-start.6) | collective-permute-done | bytes 4128 | tf_op jit(solution)/shard_map/ppermute | solution.py:593
  444.7 1.5 collective-permute-start.7
  446.1 2.3 collective-permute-done.7
  448.5 1.5 collective-permute-start.8
  450.1 3.1 collective-permute-done.8
  453.3 3.7 fusion
  457.0 1.9 pad_maximum_fusion
  459.0 9.7 order.2.ng_ref.n_ref.g_ref
  468.6 6.0 unpack.1
  474.6 0.6 broadcast_in_dim.40.segk_ref
  475.3 1.3 broadcast_in_dim.39.segq_ref
  476.6 84.8 %attn.1.dqkv_ref.o_lo_ref.o_hi_ref = bf16[2048,2560]{1,0:T(8,128)(2,1)} custom-call(bf16[2048,2304]{1,0:T(8,128)(2,1)} %order.2.ng_ref.n_ref.g_ref, bf16[1152,1536]{1,0:T(8,128)(2,1)} %get-tuple-element.52.wqkv_ref.refs_11_, bf16[1024,1152]{1,0:T(8,128)(2,1)} %get-tuple-element.53.wo_ref.refs_10_, f32[2048,128]{1,0:T(8,128)} %get-tuple-element.112.cos_ref.cosk_ref, ...), custom_call_target="tpu_custom_call" | custom-call | flops 44999999488 | bytes 40000000 | tf_op jit(solution)/shard_map/attn/pallas_call | solution.py:140
  561.4 23.7 %attn_grad.1 = (f32[8,136,1536]{2,1,0:T(8,128)}, f32[8,136,1536]{2,1,0:T(8,128)}) custom-call(bf16[2048,2304]{1,0:T(8,128)(2,1)} %order.2.ng_ref.n_ref.g_ref, bf16[2048,2560]{1,0:T(8,128)(2,1)} %attn.1.dqkv_ref.o_lo_ref.o_hi_ref, bf16[2048,2560]{1,0:T(8,128)(2,1)} %attn.1.dqkv_ref.o_lo_ref.o_hi_ref, bf16[2048,2560]{1,0:T(8,128)(2,1)} %attn.1.dqkv_ref.o_lo_ref.o_hi_ref, ...), custom_call_target="tpu_custom_call" | custom-call | flops 12000000000 | bytes 33000000 | tf_op jit(solution)/shard_map/attn_grad/pallas_call | solution.py:449
  585.1 0.7 reshape_squeeze.35.b2_ref
  585.8 0.7 reshape_squeeze.34.b1_ref
  586.5 9.7 collective-permute-done.9.refs_1_
  596.2 95.8 %hidden.5 = (bf16[4096,1152]{1,0:T(8,128)(2,1)}, bf16[4096,2304]{1,0:T(8,128)(2,1)}, f32[1152,4992]{1,0:T(8,128)}, f32[16,1152]{1,0:T(8,128)}) custom-call(bf16[2048,2304]{1,0:T(8,128)(2,1)} %norm.1.own_ref.refs_13_, bf16[2048,2304]{1,0:T(8,128)(2,1)} %collective-permute-done.oth_ref, bf16[1152,3456]{1,0:T(8,128)(2,1)} %all-gather.9.cloned.1.call-done.w_ref.refs_8_, ...), custom_call_target="tpu_custom_call" | custom-call | flops 65000001536 | bytes 70000000 | tf_op jit(solution)/shard_map/hidden/pallas_call | solution.py:397
  692.0 70.8 %out_other.1 = (f32[2048,1152]{1,0:T(8,128)}, f32[2048,1152]{1,0:T(8,128)}) custom-call(bf16[4096,1152]{1,0:T(8,128)(2,1)} %get-tuple-element.47.refs_0_, bf16[4096,1152]{1,0:T(8,128)(2,1)} %get-tuple-element.49.refs_1_, bf16[4096,1152]{1,0:T(8,128)(2,1)} %get-tuple-element.56.refs_2_, bf16[4096,2304]{1,0:T(8,128)(2,1)} %get-tuple-element.57.refs_3_, ...), custom_call_target="tpu_custom_call" | custom-call | flops 49000001536 | bytes 86000000 | tf_op jit(solution)/shard_map/out_other/pallas_call | solution.py:492
  763.3 7.2 constant_dynamic-slice_fusion
  770.5 1.7 collective-permute-start.12
  772.6 1.4 collective-permute-start.10
  774.0 0.7 add.64.refs_17_
  775.0 64.2 %collective-permute-done.12.c_ref = bf16[1,512,2560]{2,1,0:T(8,128)(2,1)S(1)} collective-permute-done((bf16[1,512,2560]{2,1,0:T(8,128)(2,1)}, bf16[1,512,2560]{2,1,0:T(8,128)(2,1)S(1)}, u32[]{:S(2)}, u32[]{:S(2)}) %collective-permute-start.12) | collective-permute-done | bytes 2621472 | tf_op jit(solution)/shard_map/ppermute | solution.py:593
  839.2 96.3 %collective-permute-done.11.b_ref = bf16[1,512,2560]{2,1,0:T(8,128)(2,1)} collective-permute-done((bf16[1,512,2560]{2,1,0:T(8,128)(2,1)}, bf16[1,512,2560]{2,1,0:T(8,128)(2,1)}, u32[]{:S(2)}, u32[]{:S(2)}) %collective-permute-start.11) | collective-permute-done | bytes 2621472 | tf_op jit(solution)/shard_map/ppermute | solution.py:593
  935.5 10.9 order.3.refs_9_
  946.9 91.6 %out_own.1 = (bf16[2048,1152]{1,0:T(8,128)(2,1)}, bf16[2048,1152]{1,0:T(8,128)(2,1)}, f32[16,1152]{1,0:T(8,128)}) custom-call(bf16[4096,1152]{1,0:T(8,128)(2,1)} %get-tuple-element.47.refs_0_, bf16[4096,1152]{1,0:T(8,128)(2,1)} %get-tuple-element.49.refs_1_, bf16[4096,1152]{1,0:T(8,128)(2,1)} %get-tuple-element.56.refs_2_, ...), custom_call_target="tpu_custom_call" | custom-call | flops 60999999488 | bytes 125000000 | tf_op jit(solution)/shard_map/out_own/pallas_call | solution.py:536
  1038.5 0.9 bitcast_reduce_fusion.3
  1039.4 1.4 slice_select_fusion.2
  1040.9 1.4 slice_select_fusion.1
  1042.7 1.4 slice_select_fusion
  1044.5 31.9 %psum.7 = f32[16,1008]{1,0:T(8,128)S(1)} all-reduce(f32[16,1008]{1,0:T(8,128)S(1)} %pad_maximum_fusion.3), channel_id=1, replica_groups=mesh['z'=2,'y'=2,'x'=2,'core'=2] {'z','y','x','core'}, use_global_device_ids=true, to_apply=%region_4.5 | all-reduce | flops 16128 | bytes 129024 | tf_op jit(solution)/shard_map/psum | solution.py:682
  1076.9 0.7 fusion.14
  1077.6 1.7 slice.194
  1079.3 1.7 slice.191
  1081.0 1.6 fusion.11
  1082.6 0.8 copy-done.1
  1083.6 7.7 join_up.1
  (98 shorter events, 6.8 us)
Async XLA Ops:
  7.2 87.5 %all-gather.5.cloned.1.call-start = ((), (), s32[]{:S(2)}) async-start(), calls=%async_computation.3 | async-start | bytes 8957952 | tf_op jit(solution)/shard_map/all_gather | solution.py:615
  12.0 3.2 collective-permute-start.1
  15.2 0.9 copy-start
  20.3 171.0 %all-gather.7.cloned.1.call-start = ((), (), s32[]{:S(2)}) async-start(), calls=%async_computation.4 | async-start | bytes 12939264 | tf_op jit(solution)/shard_map/all_gather | solution.py:615
  21.0 565.4 %all-gather.9.cloned.1.call-start = ((), (), s32[]{:S(2)}) async-start(), calls=%async_computation.5 | async-start | bytes 8957952 | tf_op jit(solution)/shard_map/all_gather | solution.py:615
  47.5 15.0 %collective-permute-start = (bf16[2048,2304]{1,0:T(8,128)(2,1)}, bf16[2048,2304]{1,0:T(8,128)(2,1)}, u32[]{:S(2)}, u32[]{:S(2)}) collective-permute-start(bf16[2048,2304]{1,0:T(8,128)(2,1)} %norm.1.own_ref.refs_13_), channel_id=1, source_target_pairs={{0,1},{1,0},{2,3},{3,2},{4,5},{5,4},{6,7},{7,6},{8,9},{9,8},{10,11... | collective-permute-start | bytes 28311560 | tf_op jit(solution)/shard_map/ppermute | solution.py:587
  47.9 991.5 %reduce-scatter.6.cloned.1.call-start = ((), (), s32[]{:S(2)}) async-start(), calls=%async_computation.7 | async-start | bytes 17915904 | tf_op jit(solution)/shard_map/reduce_scatter | solution.py:655
  187.7 853.2 %reduce-scatter.8.cloned.1.call-start = ((), (), s32[]{:S(2)}) async-start(), calls=%async_computation.8 | async-start | bytes 17915904 | tf_op jit(solution)/shard_map/reduce_scatter | solution.py:655
  284.6 758.1 %reduce-scatter.4.cloned.1.call-start = ((), (), s32[]{:S(2)}) async-start(), calls=%async_computation.6 | async-start | bytes 25878528 | tf_op jit(solution)/shard_map/reduce_scatter | solution.py:655
  288.9 179.7 %collective-permute-start.5 = (bf16[1152,1536]{1,0:T(8,128)(2,1)}, bf16[1152,1536]{1,0:T(8,128)(2,1)}, u32[]{:S(2)}, u32[]{:S(2)}) collective-permute-start(bf16[1152,1536]{1,0:T(8,128)(2,1)} %slice.182.own_ref), channel_id=1, source_target_pairs={{0,1},{1,0},{2,3},{3,2},{4,5},{5,4},{6,7},{7,6},{8,9},{9,8},{10,11... | collective-permute-start | bytes 10616840 | tf_op jit(solution)/shard_map/ppermute | solution.py:587
  288.9 10.0 copy-start.10
  288.9 10.0 copy-start.11
  295.4 163.6 %collective-permute-start.4 = (bf16[1,512,2304]{2,1,0:T(8,128)(2,1)}, bf16[1,512,2304]{2,1,0:T(8,128)(2,1)S(1)}, u32[]{:S(2)}, u32[]{:S(2)}) collective-permute-start(bf16[1,512,2304]{2,1,0:T(8,128)(2,1)} %get-tuple-element.85), channel_id=1, source_target_pairs={{0,12},{4,8},{8,4},{12,0},{1,13},{5,9},{9,5},{13,1},{2,14},{6,10},... | collective-permute-start | bytes 7077896 | tf_op jit(solution)/shard_map/ppermute | solution.py:593
  297.7 161.2 %collective-permute-start.3 = (bf16[1,512,2304]{2,1,0:T(8,128)(2,1)}, bf16[1,512,2304]{2,1,0:T(8,128)(2,1)}, u32[]{:S(2)}, u32[]{:S(2)}) collective-permute-start(bf16[1,512,2304]{2,1,0:T(8,128)(2,1)} %get-tuple-element.86), channel_id=1, source_target_pairs={{0,8},{4,12},{8,0},{12,4},{1,9},{5,13},{9,1},{13,5},{2,10},{6,14},... | collective-permute-start | bytes 7077896 | tf_op jit(solution)/shard_map/ppermute | solution.py:593
  298.3 160.6 %collective-permute-start.2 = (bf16[1,512,2304]{2,1,0:T(8,128)(2,1)}, bf16[1,512,2304]{2,1,0:T(8,128)(2,1)}, u32[]{:S(2)}, u32[]{:S(2)}) collective-permute-start(bf16[1,512,2304]{2,1,0:T(8,128)(2,1)} %get-tuple-element.87), channel_id=1, source_target_pairs={{0,4},{4,0},{8,12},{12,8},{1,5},{5,1},{9,13},{13,9},{2,6},{6,2},{1... | collective-permute-start | bytes 7077896 | tf_op jit(solution)/shard_map/ppermute | solution.py:593
  298.9 145.8 %collective-permute-start.6 = (s32[1,2,512]{2,0,1:T(1,128)S(1)}, s32[1,2,512]{2,0,1:T(1,128)S(1)}, u32[]{:S(2)}, u32[]{:S(2)}) collective-permute-start(s32[1,2,512]{2,0,1:T(1,128)S(1)} %get-tuple-element.105), channel_id=1, source_target_pairs={{0,4},{4,0},{8,12},{12,8},{1,5},{5,1},{9,13},{13,9},{2,6},{6,2},{1... | collective-permute-start | bytes 12296 | tf_op jit(solution)/shard_map/ppermute | solution.py:593
  444.7 3.8 collective-permute-start.7
  448.5 4.7 collective-permute-start.8
  561.4 23.7 %copy-start.8 = (f32[8,144]{1,0:T(8,128)S(1)}, f32[8,144]{1,0:T(8,128)}, u32[]{:S(2)}) copy-start(f32[8,144]{1,0:T(8,128)} %get-tuple-element.74) | copy-start | bytes 13828
  561.4 24.4 %copy-start.9 = (f32[8,144]{1,0:T(8,128)S(1)}, f32[8,144]{1,0:T(8,128)}, u32[]{:S(2)}) copy-start(f32[8,144]{1,0:T(8,128)} %get-tuple-element.77) | copy-start | bytes 13828
  585.1 11.1 %collective-permute-start.9 = (f32[8,136,1536]{2,1,0:T(8,128)}, f32[8,136,1536]{2,1,0:T(8,128)}, u32[]{:S(2)}, u32[]{:S(2)}) collective-permute-start(f32[8,136,1536]{2,1,0:T(8,128)} %get-tuple-element.55), channel_id=1, source_target_pairs={{0,1},{1,0},{2,3},{3,2},{4,5},{5,4},{6,7},{7,6},{8,9},{9,8},{10,11... | collective-permute-start | bytes 20054024 | tf_op jit(solution)/shard_map/ppermute | solution.py:587
  762.8 184.1 %collective-permute-start.13 = (f32[2048,1152]{1,0:T(8,128)}, f32[2048,1152]{1,0:T(8,128)}, u32[]{:S(2)}, u32[]{:S(2)}) collective-permute-start(f32[2048,1152]{1,0:T(8,128)} %get-tuple-element.60), channel_id=1, source_target_pairs={{0,1},{1,0},{2,3},{3,2},{4,5},{5,4},{6,7},{7,6},{8,9},{9,8},{10,11... | collective-permute-start | bytes 28311560 | tf_op jit(solution)/shard_map/ppermute | solution.py:587
  763.2 183.7 %collective-permute-start.14 = (f32[2048,1152]{1,0:T(8,128)}, f32[2048,1152]{1,0:T(8,128)}, u32[]{:S(2)}, u32[]{:S(2)}) collective-permute-start(f32[2048,1152]{1,0:T(8,128)} %get-tuple-element.61), channel_id=1, source_target_pairs={{0,1},{1,0},{2,3},{3,2},{4,5},{5,4},{6,7},{7,6},{8,9},{9,8},{10,11... | collective-permute-start | bytes 28311560 | tf_op jit(solution)/shard_map/ppermute | solution.py:587
  763.3 10.7 copy-start.6
  763.3 10.7 copy-start.7
  763.3 11.4 %copy-start.3 = (f32[16,1152]{1,0:T(8,128)S(1)}, f32[16,1152]{1,0:T(8,128)}, u32[]{:S(2)}) copy-start(f32[16,1152]{1,0:T(8,128)} %get-tuple-element.65) | copy-start | bytes 221188
  763.3 11.5 %copy-start.4 = (f32[16,1152]{1,0:T(8,128)S(1)}, f32[16,1152]{1,0:T(8,128)}, u32[]{:S(2)}) copy-start(f32[16,1152]{1,0:T(8,128)} %get-tuple-element.66) | copy-start | bytes 221188
  770.5 68.7 %collective-permute-start.12 = (bf16[1,512,2560]{2,1,0:T(8,128)(2,1)}, bf16[1,512,2560]{2,1,0:T(8,128)(2,1)S(1)}, u32[]{:S(2)}, u32[]{:S(2)}) collective-permute-start(bf16[1,512,2560]{2,1,0:T(8,128)(2,1)} %get-tuple-element.82), channel_id=1, source_target_pairs={{0,12},{4,8},{8,4},{12,0},{1,13},{5,9},{9,5},{13,1},{2,14},{6,10},... | collective-permute-start | bytes 7864328 | tf_op jit(solution)/shard_map/ppermute | solution.py:593
  772.2 163.3 %collective-permute-start.11 = (bf16[1,512,2560]{2,1,0:T(8,128)(2,1)}, bf16[1,512,2560]{2,1,0:T(8,128)(2,1)}, u32[]{:S(2)}, u32[]{:S(2)}) collective-permute-start(bf16[1,512,2560]{2,1,0:T(8,128)(2,1)} %get-tuple-element.83), channel_id=1, source_target_pairs={{0,8},{4,12},{8,0},{12,4},{1,9},{5,13},{9,1},{13,5},{2,10},{6,14},... | collective-permute-start | bytes 7864328 | tf_op jit(solution)/shard_map/ppermute | solution.py:593
  772.6 162.9 %collective-permute-start.10 = (bf16[1,512,2560]{2,1,0:T(8,128)(2,1)}, bf16[1,512,2560]{2,1,0:T(8,128)(2,1)}, u32[]{:S(2)}, u32[]{:S(2)}) collective-permute-start(bf16[1,512,2560]{2,1,0:T(8,128)(2,1)} %get-tuple-element.84), channel_id=1, source_target_pairs={{0,4},{4,0},{8,12},{12,8},{1,5},{5,1},{9,13},{13,9},{2,6},{6,2},{1... | collective-permute-start | bytes 7864328 | tf_op jit(solution)/shard_map/ppermute | solution.py:593
  774.9 171.5 %copy-start.5 = (f32[16,1152]{1,0:T(8,128)S(1)}, f32[16,1152]{1,0:T(8,128)}, u32[]{:S(2)}) copy-start(f32[16,1152]{1,0:T(8,128)} %get-tuple-element.67) | copy-start | bytes 221188
  1040.8 41.7 %collective-permute-start.15 = (f32[72,2304]{1,0:T(8,128)S(1)}, f32[72,2304]{1,0:T(8,128)S(1)}, u32[]{:S(2)}, u32[]{:S(2)}) collective-permute-start(f32[72,2304]{1,0:T(8,128)S(1)} %slice_select_fusion.2), channel_id=1, source_target_pairs={{0,1},{1,0},{2,3},{3,2},{4,5},{5,4},{6,7},{7,6},{8,9},{9,8},{10,11... | collective-permute-start | bytes 1990664 | tf_op jit(solution)/shard_map/ppermute | solution.py:587
  1042.2 40.3 %collective-permute-start.16 = (f32[72,2304]{1,0:T(8,128)S(1)}, f32[72,2304]{1,0:T(8,128)S(1)}, u32[]{:S(2)}, u32[]{:S(2)}) collective-permute-start(f32[72,2304]{1,0:T(8,128)S(1)} %slice_select_fusion.1), channel_id=1, source_target_pairs={{0,1},{1,0},{2,3},{3,2},{4,5},{5,4},{6,7},{7,6},{8,9},{9,8},{10,11... | collective-permute-start | bytes 1990664 | tf_op jit(solution)/shard_map/ppermute | solution.py:587
  1044.1 38.5 %collective-permute-start.17 = (f32[72,2304]{1,0:T(8,128)S(1)}, f32[72,2304]{1,0:T(8,128)}, u32[]{:S(2)}, u32[]{:S(2)}) collective-permute-start(f32[72,2304]{1,0:T(8,128)S(1)} %slice_select_fusion), channel_id=1, source_target_pairs={{0,1},{1,0},{2,3},{3,2},{4,5},{5,4},{6,7},{7,6},{8,9},{9,8},{10,11... | collective-permute-start | bytes 1990664 | tf_op jit(solution)/shard_map/ppermute | solution.py:587
  1076.9 14.5 %copy-start.12 = (f32[72]{0:T(128)}, f32[72]{0:T(128)S(1)}, u32[]{:S(2)}) copy-start(f32[72]{0:T(128)S(1)} %get-tuple-element.141) | copy-start | bytes 868
  1082.5 0.8 copy-start.1
  1082.6 1.1 copy-start.2
Sparse Core Ops, SparseCore 0:
  20.4 74.1 all-gather.4
  97.3 93.9 all-gather.6
  193.5 71.2 all-gather.8
  269.0 216.6 reduce-scatter.5
  489.8 122.3 reduce-scatter.7
  692.1 272.6 reduce-scatter.3
where the time goes:
time: 1100 us
  Pallas kernels  608 us (55%)
  waiting for transfers between devices  367 us (33%)
  blocking collectives  47 us (4%)
  local copies, waits for them, and re-layouts  37 us (3%)
  between operations  14.8 us (1%)
  starting transfers between devices  14.5 us (1%)
  other arithmetic  11 us (1%)
    ppermute x9, waiting for transfers between devices, send_blocks(): lax.ppermute(sent, ('z', 'y'), [(i, i ^ flip) for i in range(4)])  310 us
    pallas_call x3, Pallas kernels, hidden_part(): pl.pallas_call(hidden_kernel, grid=(steps,), in_specs=[own_spec, oth_spec...  282 us
    pallas_call x1, Pallas kernels, out_own(): pl.pallas_call(out_own_kernel, grid=(t_len // rows,), in_specs=out_specs_...  91.6 us
    pallas_call x1, Pallas kernels, attention(): pl.pallas_call(attn_kernel, grid=(4,), in_specs=[row_spec(both), full(wqk...  84.8 us
    pallas_call x1, Pallas kernels, out_other(): pl.pallas_call(out_other_kernel, grid=(t_len // rows,), in_specs=out_spec...  70.8 us
    all_gather x3, waiting for transfers between devices, gather(): return lax.all_gather(shard, CHIPS, axis=0, tiled=True)  33.9 us
    psum x1, blocking collectives, local_step(): small = lax.psum(small, ALL_AXES)  31.9 us
    pallas_call x1, Pallas kernels, attn_grad(): pl.pallas_call(attn_grad_kernel, grid=(total // width,), in_specs=[pl.Blo...  23.7 us
  transfers between devices with their start and end apart: 24, of which 10 were waited for; matrix products, arithmetic and copies ran while one was open for 4% of the time, Pallas kernels for 54%

commit v1 on v0

--- a/solution.py
+++ b/solution.py
@@ -34,18 +34,30 @@
     return values * cos_b + pltpu.roll(values, ROPE_DIMS // 2, axis=1) * sin_b
 
 
-def attn_kernel(ng_ref, wqkv_ref, wo_ref, cos_ref, sin_ref, cosk_ref, sink_ref, segq_ref, segk_ref, out_ref,
-                q_s, do_s, k_s, v_s, kt_s, vt_s, mask_s, s_s, p_s, dk_s, dv_s):
+def attn_kernel(cp_ref, own_ref, n1_ref, n2_ref, n3_ref, g1_ref, g2_ref, g3_ref, wqkv_ref, wo_ref, cos_ref, sin_ref, cosk_ref, sink_ref, segq_ref, segk_ref, out_ref,
+                n_s, g_s, q_s, do_s, k_s, v_s, kt_s, vt_s, mask_s, s_s, p_s, dk_s, dv_s):
     step = pl.program_id(0)
     n_blocks = pl.num_programs(0)
-    rows = ng_ref.shape[0]
-    d_model = ng_ref.shape[1] // 2
+    rows, d_model = n_s.shape
     qk = N_HEADS * HEAD_DIM
     base = pl.multiple_of(step * rows, rows)
     cos_b = cos_ref[...]
     sin_b = sin_ref[...]
-    n_blk = ng_ref[:, :d_model]
-    g_blk = ng_ref[:, d_model:]
+    flip = step ^ cp_ref[0]
+
+    @pl.when(flip == 0)
+    def _():
+        n_s[...] = own_ref[0, :, :d_model]
+        g_s[...] = own_ref[0, :, d_model:]
+
+    for i, (n_ref, g_ref) in enumerate(((n1_ref, g1_ref), (n2_ref, g2_ref), (n3_ref, g3_ref))):
+        @pl.when(flip == i + 1)
+        def _():
+            n_s[...] = n_ref[0]
+            g_s[...] = g_ref[0]
+
+    n_blk = n_s[...]
+    g_blk = g_s[...]
 
     @pl.when(step == 0)
     def _():
@@ -128,31 +140,35 @@
         out_ref[:, qk + HEAD_DIM:qk + 2 * HEAD_DIM] = dv_s[...].astype(BF16)
 
 
-def attention(ng_seq, wqkv, wo, cos_b, sin_b, seg_own):
-    t_len, both = ng_seq.shape
-    rows = t_len // 4
+def attention(cp_index, ng_blocks, n_got, g_got, wqkv, wo, cos_b, sin_b, seg_own):
+    _, rows, both = ng_blocks.shape
+    t_len = 4 * rows
     qk = N_HEADS * HEAD_DIM
     segq = jnp.broadcast_to(seg_own[:, None], (t_len, 128))
     segk = jnp.broadcast_to(seg_own[None, :], (8, t_len))
-    row_spec = lambda width: pl.BlockSpec((rows, width), lambda i: (i, 0))
-    full = lambda a: pl.BlockSpec(a.shape, lambda i: (0,) * a.ndim, pipeline_mode=pl.Buffered(1))
+    row_spec = lambda width: pl.BlockSpec((rows, width), lambda i, cp: (i, 0))
+    full = lambda a: pl.BlockSpec(a.shape, lambda i, cp: (0,) * a.ndim, pipeline_mode=pl.Buffered(1))
+    own_spec = pl.BlockSpec((1, rows, both), lambda i, cp: (cp[0], 0, 0), pipeline_mode=pl.Buffered(1))
     width = 2 * (qk + HEAD_DIM)
     return pl.pallas_call(
         attn_kernel,
-        grid=(4,),
-        in_specs=[row_spec(both), full(wqkv), full(wo), row_spec(ROPE_DIMS), row_spec(ROPE_DIMS), full(cos_b), full(sin_b), row_spec(128), full(segk)],
-        out_specs=pl.BlockSpec((t_len, width), lambda i: (0, 0)),
+        grid_spec=pltpu.PrefetchScalarGridSpec(
+            num_scalar_prefetch=1,
+            grid=(4,),
+            in_specs=[own_spec] + [full(a) for a in n_got + g_got] + [full(wqkv), full(wo), row_spec(ROPE_DIMS), row_spec(ROPE_DIMS), full(cos_b), full(sin_b), row_spec(128), full(segk)],
+            out_specs=pl.BlockSpec((t_len, width), lambda i, cp: (0, 0)),
+            scratch_shapes=[
+                pltpu.VMEM((rows, both // 2), BF16), pltpu.VMEM((rows, both // 2), BF16),
+                pltpu.VMEM((N_HEADS, rows, HEAD_DIM), BF16), pltpu.VMEM((N_HEADS, rows, HEAD_DIM), BF16),
+                pltpu.VMEM((t_len, HEAD_DIM), BF16), pltpu.VMEM((t_len, HEAD_DIM), BF16),
+                pltpu.VMEM((HEAD_DIM, t_len), BF16), pltpu.VMEM((HEAD_DIM, t_len), BF16),
+                pltpu.VMEM((rows, t_len), F32), pltpu.VMEM((rows, t_len), F32), pltpu.VMEM((rows, t_len), BF16),
+                pltpu.VMEM((t_len, HEAD_DIM), F32), pltpu.VMEM((t_len, HEAD_DIM), F32)]),
         out_shape=jax.ShapeDtypeStruct((t_len, width), BF16),
-        scratch_shapes=[
-            pltpu.VMEM((N_HEADS, rows, HEAD_DIM), BF16), pltpu.VMEM((N_HEADS, rows, HEAD_DIM), BF16),
-            pltpu.VMEM((t_len, HEAD_DIM), BF16), pltpu.VMEM((t_len, HEAD_DIM), BF16),
-            pltpu.VMEM((HEAD_DIM, t_len), BF16), pltpu.VMEM((HEAD_DIM, t_len), BF16),
-            pltpu.VMEM((rows, t_len), F32), pltpu.VMEM((rows, t_len), F32), pltpu.VMEM((rows, t_len), BF16),
-            pltpu.VMEM((t_len, HEAD_DIM), F32), pltpu.VMEM((t_len, HEAD_DIM), F32)],
-        compiler_params=pltpu.CompilerParams(vmem_limit_bytes=60 * 1024 * 1024, dimension_semantics=('arbitrary',)),
+        compiler_params=pltpu.CompilerParams(vmem_limit_bytes=62 * 1024 * 1024, dimension_semantics=('arbitrary',)),
         cost_estimate=pl.CostEstimate(flops=45_000_000_000, bytes_accessed=40_000_000, transcendentals=10_000_000),
         name='attn',
-    )(ng_seq, wqkv, wo, cos_b, sin_b, cos_b, sin_b, segq, segk)
+    )(cp_index[None], ng_blocks, *n_got, *g_got, wqkv, wo, cos_b, sin_b, cos_b, sin_b, segq, segk)
 
 
 def norm_kernel(x_ref, g_ref, scale_ref, out_ref):
@@ -178,24 +194,7 @@
     )(x_loc, g_loc, scale_f)
 
 
-def order_kernel(x_ref, a_ref, b_ref, c_ref, out_ref):
-    cp = lax.axis_index('z') * 2 + lax.axis_index('y')
-    rows = a_ref.shape[1]
-    for flip, ref in enumerate((x_ref.at[cp], a_ref.at[0], b_ref.at[0], c_ref.at[0])):
-        out_ref[pl.ds(pl.multiple_of((cp ^ flip) * rows, rows), rows), :] = ref[...]
-
-
-def order(values, got):
-    n_seq, rows, width = values.shape
-    return pl.pallas_call(
-        order_kernel, out_shape=jax.ShapeDtypeStruct((n_seq * rows, width), values.dtype), name='order',
-        compiler_params=pltpu.CompilerParams(vmem_limit_bytes=40 * 1024 * 1024),
-        cost_estimate=pl.CostEstimate(flops=2_000_000_000, bytes_accessed=10_000_000, transcendentals=0),
-    )(values, *got)
-
-
 N_PART = 3
-EXTRA_GATHER = 1
 
 
 def split_kernel(w1_ref, w2_ref, keep_ref, send_ref):
@@ -225,25 +224,26 @@
     return pl.pallas_call(split_kernel, out_shape=[out, out], name='split_up')(w1, w2)
 
 
-def stack_kernel(keep_ref, recv_ref, wd_ref, extra_ref, *out_refs):
+def stack_kernel(keep_ref, recv_ref, wd_ref, extra_ref, first_ref, rest_ref):
     core = lax.axis_index('core')
     rows, cols = keep_ref.shape[1:]
     d_model = wd_ref.shape[1]
-    for part, out_ref in enumerate(out_refs):
-        own = pl.multiple_of(core * rows, 8)
-        out_ref[pl.ds(own, rows), :cols] = keep_ref[part]
-        out_ref[pl.ds(pl.multiple_of(rows - own, 8), rows), :cols] = recv_ref[part]
-        out_ref[:, cols:cols + d_model] = wd_ref[part * 2 * rows:(part + 1) * 2 * rows, :].astype(BF16)
-        if part == EXTRA_GATHER:
-            n_extra = extra_ref.shape[0]
-            out_ref[:n_extra, cols + d_model:] = extra_ref[...]
-            out_ref[n_extra:, cols + d_model:] = jnp.zeros((2 * rows - n_extra, extra_ref.shape[1]), BF16)
+    own = pl.multiple_of(core * rows, 8)
+    oth = pl.multiple_of(rows - own, 8)
+    for part in range(N_PART):
+        out_ref, base = (first_ref, 0) if part == 0 else (rest_ref, (part - 1) * (cols + d_model))
+        out_ref[pl.ds(own, rows), base:base + cols] = keep_ref[part]
+        out_ref[pl.ds(oth, rows), base:base + cols] = recv_ref[part]
+        out_ref[:, base + cols:base + cols + d_model] = wd_ref[part * 2 * rows:(part + 1) * 2 * rows, :].astype(BF16)
+    n_extra = extra_ref.shape[0]
+    first_ref[:n_extra, cols + d_model:] = extra_ref[...]
+    first_ref[n_extra:, cols + d_model:] = jnp.zeros((2 * rows - n_extra, extra_ref.shape[1]), BF16)
 
 
 def stack_up(keep, recv, w_down, extra):
     _, rows, cols = keep.shape
     width = cols + w_down.shape[1]
-    outs = [jax.ShapeDtypeStruct((2 * rows, width + (extra.shape[1] if part == EXTRA_GATHER else 0)), BF16) for part in range(N_PART)]
+    outs = [jax.ShapeDtypeStruct((2 * rows, width + extra.shape[1]), BF16), jax.ShapeDtypeStruct((2 * rows, (N_PART - 1) * width), BF16)]
     return pl.pallas_call(stack_kernel, out_shape=outs, name='stack_up')(keep, recv, w_down, extra)
 
 
@@ -382,7 +382,8 @@
         copy.wait()
 
 
-def hidden_part(ng_own, ng_oth, w_part, b1, b2, extra=()):
+def hidden_part(ng_own, ng_oth, weight, b1, b2, extra=()):
+    w_part, w_col = weight
     t_len, both = ng_own.shape
     d_model = both // 2
     rows = 512
@@ -390,14 +391,14 @@
     half = steps // 2
     own_spec = pl.BlockSpec((rows, both), lambda i: (jnp.minimum(i, half - 1), 0))
     oth_spec = pl.BlockSpec((rows, both), lambda i: (jnp.maximum(i - half, 0), 0))
-    full = lambda a, width: pl.BlockSpec((a.shape[0], width), lambda i: (0, 0), pipeline_mode=pl.Buffered(1))
+    full = lambda a, width, col=0: pl.BlockSpec((a.shape[0], width), lambda i: (0, col), pipeline_mode=pl.Buffered(1))
     row = lambda width: pl.BlockSpec((rows, width), lambda i: (i, 0))
     blk = [pl.BlockSpec((1,) + a.shape[1:], lambda i: (i, 0, 0)) for a in extra]
     side = (2, d_model // 8, extra[0].shape[2]) if extra else (2, 8, 128)
     return pl.pallas_call(
         hidden_kernel,
         grid=(steps,),
-        in_specs=[own_spec, oth_spec, full(w_part, 3 * d_model), full(b1, d_model), full(b2, d_model)] + blk,
+        in_specs=[own_spec, oth_spec, full(w_part, 3 * d_model, w_col), full(b1, d_model), full(b2, d_model)] + blk,
         out_specs=[row(d_model), row(2 * d_model), pl.BlockSpec(memory_space=pl.ANY), pl.BlockSpec((16, d_model), lambda i: (0, 0))],
         out_shape=[jax.ShapeDtypeStruct((2 * t_len, d_model), BF16), jax.ShapeDtypeStruct((2 * t_len, 2 * d_model), BF16),
                    jax.ShapeDtypeStruct((d_model, 3 * d_model + (extra[0].shape[2] if extra else 0)), F32), jax.ShapeDtypeStruct((16, d_model), F32)],
@@ -409,26 +410,34 @@
     )(ng_own, ng_oth, w_part, b1, b2, *extra)
 
 
-def attn_grad_kernel(n_ref, dqkv_ref, o_lo_ref, o_hi_ref, g_ref, keep_ref, send_ref):
+def attn_grad_kernel(cp_ref, own_ref, n1_ref, n2_ref, n3_ref, g1_ref, g2_ref, g3_ref, dqkv_ref, o_lo_ref, o_hi_ref, keep_ref, send_ref):
     step = pl.program_id(0)
     core = lax.axis_index('core')
-    r_o, r_in = o_lo_ref.shape[1] // 8, n_ref.shape[1] // 16
+    d_model = own_ref.shape[2] // 2
+    r_o, r_in = o_lo_ref.shape[1] // 8, d_model // 16
     width = dqkv_ref.shape[1]
-    d_model = g_ref.shape[1]
-
-    def put(rows, cols, value_of):
+    rows = own_ref.shape[1]
+    place = [pl.ds(pl.multiple_of((cp_ref[0] ^ flip) * rows, rows), rows) for flip in range(4)]
+
+    def put(at, cols, value_of):
         for dev in range(16):
             for ref, flip in ((keep_ref, 0), (send_ref, 1)):
                 @pl.when((core ^ flip) == dev % 2)
                 def _():
-                    ref[dev // 2, rows, cols] = value_of(dev)
-
-    d_wqkv = dot_tn(n_ref[...], dqkv_ref[...])
+                    ref[dev // 2, at, cols] = value_of(dev)
+
+    d_wqkv = dot_tn(own_ref[0, :, :d_model], dqkv_ref[place[0], :])
+    for flip, n_ref in ((1, n1_ref), (2, n2_ref), (3, n3_ref)):
+        d_wqkv = d_wqkv + dot_tn(n_ref[0], dqkv_ref[place[flip], :])
     put(slice(r_o, r_o + r_in), slice(0, width), lambda dev: d_wqkv[dev * r_in:(dev + 1) * r_in])
 
     def low(first_col, used):
-        g_cols = g_ref[:, first_col:first_col + used]
-        d_wo = [dot_tn(o_lo_ref[...], g_cols), dot_tn(o_hi_ref[...], g_cols)]
+        d_wo = []
+        for o_ref in (o_lo_ref, o_hi_ref):
+            total = dot_tn(o_ref[place[0], :], own_ref[0, :, d_model + first_col:d_model + first_col + used])
+            for flip, g_ref in ((1, g1_ref), (2, g2_ref), (3, g3_ref)):
+                total = total + dot_tn(o_ref[place[flip], :], g_ref[0, :, first_col:first_col + used])
+            d_wo.append(total)
         put(slice(0, r_o), slice(0, used), lambda dev: d_wo[dev // 8][dev % 8 * r_o:(dev % 8 + 1) * r_o])
         if used < width:
             put(slice(0, r_o), slice(used, width), lambda dev: jnp.zeros((r_o, width - used), F32))
@@ -437,113 +446,134 @@
         pl.when(step == i)(functools.partial(low, i * width, min(width, d_model - i * width)))
 
 
-def attn_grad(ng_seq, od_seq, r_o, r_in):
-    t_len, both = ng_seq.shape
-    d_model = both // 2
+def attn_grad(cp_index, ng_blocks, n_got, g_got, od_seq, r_o, r_in):
+    _, rows, both = ng_blocks.shape
+    t_len = od_seq.shape[0]
     width = 512
-    qk = N_HEADS * HEAD_DIM
-    total = qk + 2 * HEAD_DIM
+    total = (N_HEADS + 2) * HEAD_DIM
     out = jax.ShapeDtypeStruct((8, r_o + r_in, total), F32)
-    out_spec = pl.BlockSpec((8, r_o + r_in, width), lambda i: (0, 0, i))
+    out_spec = pl.BlockSpec((8, r_o + r_in, width), lambda i, cp: (0, 0, i))
     one = pl.Buffered(1)
+    full = lambda a: pl.BlockSpec(a.shape, lambda i, cp: (0, 0, 0), pipeline_mode=one)
     return pl.pallas_call(
         attn_grad_kernel,
-        grid=(total // width,),
-        in_specs=[pl.BlockSpec((t_len, d_model), lambda i: (0, 0), pipeline_mode=one), pl.BlockSpec((t_len, width), lambda i: (0, i)),
-                  pl.BlockSpec((t_len, width), lambda i: (0, total // width), pipeline_mode=one), pl.BlockSpec((t_len, width), lambda i: (0, total // width + 1), pipeline_mode=one),
-                  pl.BlockSpec((t_len, d_model), lambda i: (0, 1), pipeline_mode=one)],
-        out_specs=[out_spec, out_spec],
+        grid_spec=pltpu.PrefetchScalarGridSpec(
+            num_scalar_prefetch=1,
+            grid=(total // width,),
+            in_specs=[pl.BlockSpec((1, rows, both), lambda i, cp: (cp[0], 0, 0), pipeline_mode=one)] + [full(a) for a in n_got + g_got]
+                     + [pl.BlockSpec((t_len, width), lambda i, cp: (0, i)),
+                        pl.BlockSpec((t_len, width), lambda i, cp: (0, total // width), pipeline_mode=one),
+                        pl.BlockSpec((t_len, width), lambda i, cp: (0, total // width + 1), pipeline_mode=one)],
+            out_specs=[out_spec, out_spec]),
         out_shape=[out, out],
         compiler_params=pltpu.CompilerParams(vmem_limit_bytes=60 * 1024 * 1024, dimension_semantics=('arbitrary',)),
         cost_estimate=pl.CostEstimate(flops=12_000_000_000, bytes_accessed=33_000_000, transcendentals=0),
         name='attn_grad',
-    )(ng_seq, od_seq, od_seq, od_seq, ng_seq)
-
-
-def out_products(act_refs, dh_refs, w_refs):
-    d_model = act_refs[0].shape[1]
-    out = None
-    d_n = None
-    for act_ref, dh_ref, w_ref in zip(act_refs, dh_refs, w_refs):
-        o_part = dot_nn(act_ref[...], w_ref[:, 2 * d_model:3 * d_model])
-        n_part = dot_nt(dh_ref[...], w_ref[:, :2 * d_model])
-        out = o_part if out is None else out + o_part
-        d_n = n_part if d_n is None else d_n + n_part
-    return out, d_n
-
-
-def out_other_kernel(*refs):
-    out, d_n = out_products(refs[:3], refs[3:6], refs[6:9])
-    refs[9][...] = out
-    refs[10][...] = d_n
-
-
-def out_specs_of(rows, d_model, first_block):
-    tile = lambda width: pl.BlockSpec((rows, width), lambda i: (i + first_block, 0))
-    full = pl.BlockSpec((d_model, 3 * d_model), lambda i: (0, 0), pipeline_mode=pl.Buffered(1))
-    return [tile(d_model)] * 3 + [tile(2 * d_model)] * 3 + [full] * 3
-
-
-def out_other(acts, dhs, w_parts):
-    t_len, d_model = acts[0].shape[0] // 2, acts[0].shape[1]
-    rows = 256
-    tile = pl.BlockSpec((rows, d_model), lambda i: (i, 0))
-    out = jax.ShapeDtypeStruct((t_len, d_model), F32)
-    return pl.pallas_call(
-        out_other_kernel,
-        grid=(t_len // rows,),
-        in_specs=out_specs_of(rows, d_model, t_len // rows),
-        out_specs=[tile, tile],
-        out_shape=[out, out],
+    )(cp_index[None], ng_blocks, *n_got, *g_got, od_seq, od_seq, od_seq)
+
+
+def fwd_product(act_refs, w_refs):
+    out = dot_nn(act_refs[0][...], w_refs[0][...])
+    for act_ref, w_ref in zip(act_refs[1:], w_refs[1:]):
+        out = out + dot_nn(act_ref[...], w_ref[...])
+    return out
+
+
+def bwd_product(dh_refs, w_refs):
+    out = dot_nt(dh_refs[0][...], w_refs[0][:, :dh_refs[0].shape[1]])
+    for dh_ref, w_ref in zip(dh_refs[1:], w_refs[1:]):
+        out = out + dot_nt(dh_ref[...], w_ref[:, :dh_ref.shape[1]])
+    return out
+
+
+def other_kernel(product, *refs):
+    refs[-1][...] = product(refs[:N_PART], refs[N_PART:2 * N_PART])
+
+
+OUT_ROWS = 256
+
+
+def out_specs_of(width, weights, w_width, w_off, first_block):
+    tile = pl.BlockSpec((OUT_ROWS, width), lambda i, *_: (i + first_block, 0))
+    specs = [tile] * N_PART
+    for array, col in weights:
+        specs.append(pl.BlockSpec((array.shape[0], w_width), lambda i, *_, at=w_off(col): (0, at), pipeline_mode=pl.Buffered(1)))
+    return specs
+
+
+def out_other(parts, weights, product, w_width, w_off):
+    t_len, width = parts[0].shape[0] // 2, parts[0].shape[1]
+    d_model = weights[0][0].shape[0]
+    return pl.pallas_call(
+        functools.partial(other_kernel, product),
+        grid=(t_len // OUT_ROWS,),
+        in_specs=out_specs_of(width, weights, w_width, w_off, t_len // OUT_ROWS),
+        out_specs=pl.BlockSpec((OUT_ROWS, d_model), lambda i: (i, 0)),
+        out_shape=jax.ShapeDtypeStruct((t_len, d_model), F32),
         compiler_params=pltpu.CompilerParams(vmem_limit_bytes=60 * 1024 * 1024, dimension_semantics=('arbitrary',)),
-        cost_estimate=pl.CostEstimate(flops=49_000_000_000, bytes_accessed=86_000_000, transcendentals=0),
-        name='out_other',
-    )(*acts, *dhs, *w_parts)
-
-
-def out_own_kernel(*refs):
-    (od_ref, wo_ref, wqkv_ref, x_ref, g_ref, got_o_ref, got_n_ref, scale_ref, bias_ref, x_out_ref, d_x_ref, sums_ref) = refs[9:]
-    d_model = x_ref.shape[1]
+        cost_estimate=pl.CostEstimate(flops=2 * t_len * d_model * width * N_PART, bytes_accessed=50_000_000, transcendentals=0),
+    )(*parts, *[array for array, _ in weights])
+
+
+def fwd_own_kernel(cp_ref, *refs):
+    o_refs = refs[2 * N_PART:2 * N_PART + 8]
+    wo_ref, x_ref, got_ref, bias_ref, out_ref, o_s = refs[2 * N_PART + 8:]
+    flip = (pl.program_id(0) // 2) ^ cp_ref[0]
+    half = o_s.shape[1] // 2
+    for i in range(4):
+        @pl.when(flip == i)
+        def _():
+            o_s[:, :half] = o_refs[2 * i][0]
+            o_s[:, half:] = o_refs[2 * i + 1][0]
+    out = fwd_product(refs[:N_PART], refs[N_PART:2 * N_PART]) + dot_nn(o_s[...], wo_ref[...])
+    out_ref[...] = (x_ref[...].astype(F32) + out + got_ref[...] + bias_ref[...]).astype(BF16)
+
+
+def bwd_own_kernel(cp_ref, *refs):
+    d_refs = refs[2 * N_PART:2 * N_PART + 4]
+    wqkv_ref, x_ref, g_ref, got_ref, scale_ref, d_x_ref, sums_ref, d_s = refs[2 * N_PART + 4:]
+    flip = (pl.program_id(0) // 2) ^ cp_ref[0]
+    for i in range(4):
+        @pl.when(flip == i)
+        def _():
+            d_s[...] = d_refs[i][0]
 
     @pl.when(pl.program_id(0) == 0)
     def _():
         sums_ref[...] = jnp.zeros_like(sums_ref)
 
-    out, d_n = out_products(refs[:3], refs[3:6], refs[6:9])
-    split = wqkv_ref.shape[1]
-    out = out + dot_nn(od_ref[:, split:], wo_ref[...])
-    d_n = d_n + dot_nt(od_ref[:, :split], wqkv_ref[...])
+    d_n = bwd_product(refs[:N_PART], refs[N_PART:2 * N_PART]) + dot_nt(d_s[...], wqkv_ref[...]) + got_ref[...]
     x_f = x_ref[...].astype(F32)
     g_f = g_ref[...].astype(F32)
-    x_out_ref[...] = (x_f + out + got_o_ref[...] + bias_ref[...]).astype(BF16)
-    d_n = d_n + got_n_ref[...]
     inv = lax.rsqrt(jnp.mean(x_f * x_f, axis=1, keepdims=True) + 1e-6)
     scaled = d_n * (1.0 + scale_ref[...])
     xn = x_f * inv
     proj = jnp.mean(scaled * xn, axis=1, keepdims=True)
     d_x_ref[...] = (g_f + inv * (scaled - xn * proj)).astype(BF16)
-    rows = x_f.shape[0]
+    rows, d_model = x_f.shape
     sums_ref[:8, :] += jnp.sum((d_n * xn).reshape(rows // 8, 8, d_model), axis=0)
     sums_ref[8:, :] += jnp.sum(g_f.reshape(rows // 8, 8, d_model), axis=0)
 
 
-def out_own(acts, dhs, w_parts, od_loc, wo, wqkv, x_loc, ng_own, got_o, got_n, scale_f, bias_f):
-    t_len, d_model = x_loc.shape
-    rows = 256
-    tile = lambda width: pl.BlockSpec((rows, width), lambda i: (i, 0))
-    full = lambda a: pl.BlockSpec(a.shape, lambda i: (0, 0), pipeline_mode=pl.Buffered(1))
-    out = jax.ShapeDtypeStruct((t_len, d_model), BF16)
-    return pl.pallas_call(
-        out_own_kernel,
-        grid=(t_len // rows,),
-        in_specs=out_specs_of(rows, d_model, 0) + [tile(od_loc.shape[1]), full(wo), full(wqkv), tile(d_model), pl.BlockSpec((rows, d_model), lambda i: (i, 1))]
-                 + [tile(d_model)] * 2 + [full(scale_f), full(bias_f)],
-        out_specs=[tile(d_model), tile(d_model), pl.BlockSpec((16, d_model), lambda i: (0, 0))],
-        out_shape=[out, out, jax.ShapeDtypeStruct((16, d_model), F32)],
-        compiler_params=pltpu.CompilerParams(vmem_limit_bytes=63 * 1024 * 1024, dimension_semantics=('arbitrary',)),
-        cost_estimate=pl.CostEstimate(flops=61_000_000_000, bytes_accessed=125_000_000, transcendentals=0),
-        name='out_own',
-    )(*acts, *dhs, *w_parts, od_loc, wo, wqkv, x_loc, ng_own, got_o, got_n, scale_f, bias_f)
+def own_call(kernel, cp_index, parts, weights, w_width, w_off, od_blocks, od_got, od_cols, od_width, rest, rest_specs, out_specs, out_shape, scratch):
+    t_len, width = parts[0].shape[0] // 2, parts[0].shape[1]
+    specs = out_specs_of(width, weights, w_width, w_off, 0)
+    args = list(parts) + [array for array, _ in weights]
+    for i, source in enumerate([od_blocks] + od_got):
+        for col in od_cols:
+            if i == 0:
+                specs.append(pl.BlockSpec((1, OUT_ROWS, od_width), lambda j, cp, col=col: (cp[0], j % 2, col)))
+            else:
+                specs.append(pl.BlockSpec((1, OUT_ROWS, od_width), lambda j, cp, col=col: (0, j % 2, col)))
+            args.append(source)
+    return pl.pallas_call(
+        kernel,
+        grid_spec=pltpu.PrefetchScalarGridSpec(
+            num_scalar_prefetch=1, grid=(t_len // OUT_ROWS,), in_specs=specs + rest_specs, out_specs=out_specs, scratch_shapes=scratch),
+        out_shape=out_shape,
+        compiler_params=pltpu.CompilerParams(vmem_limit_bytes=62 * 1024 * 1024, dimension_semantics=('arbitrary',)),
+        cost_estimate=pl.CostEstimate(flops=2 * t_len * weights[0][0].shape[0] * (width * N_PART + 1024), bytes_accessed=80_000_000, transcendentals=0),
+    )(cp_index[None], *args, *rest)
 
 
 def pack_kernel(wq_ref, wk_ref, wv_ref, wo_ref, out_ref):
@@ -586,10 +616,10 @@
     def swap_core(values):
         return lax.ppermute(values, 'core', [(0, 1), (1, 0)])
 
-    def send_blocks(values, cp_index):
+    def send_blocks(values, cp_index, width=None):
         got = []
         for flip in (1, 2, 3):
-            sent = lax.dynamic_index_in_dim(values, cp_index ^ flip, 0, keepdims=True)
+            sent = lax.dynamic_index_in_dim(values, cp_index ^ flip, 0, keepdims=True)[..., :width]
             got.append(lax.ppermute(sent, ('z', 'y'), [(i, i ^ flip) for i in range(4)]))
         return got
 
@@ -608,13 +638,18 @@
         def after(value, *deps):
             return lax.optimization_barrier((value,) + deps)[0]
 
+        seg_pack = jnp.stack([seg_id, seg_pos], axis=1)
+        seg_got = send_blocks(seg_pack, cp_index)
+        g_got = send_blocks(grad_out, cp_index)
+
         keep, send = split_up(w_up1, w_up2)
         shards = stack_up(keep, swap_core(send), w_down, pack(w_q, w_k, w_v, w_o))
 
         def gather(shard):
             return lax.all_gather(shard, CHIPS, axis=0, tiled=True)
 
-        w_parts = [gather(shards[0])]
+        whole = [gather(shards[0]), gather(shards[1])]
+        weights = [(whole[0], 0), (whole[1], 0), (whole[1], 1)]
 
         vec_all = lax.all_gather(vectors(norm_scale, b_o, b_down, b_up1, b_up2), ALL_AXES, axis=0)
         scale_f, bo_f, bd_f = [vec_all[:, i, :r_in].reshape(1, d_model).astype(F32) for i in range(3)]
@@ -625,14 +660,11 @@
             b_ups.append([mine[:, part].reshape(1, d_model) for part in range(N_PART)])
 
         x_loc = x_in.reshape(t_len, d_model)
-        g_loc = grad_out.reshape(t_len, d_model)
-        ng_own = norm_and_grad(x_loc, g_loc, scale_f)
+        ng_own = norm_and_grad(x_loc, grad_out.reshape(t_len, d_model), scale_f)
         ng_oth = swap_core(ng_own)
-        w_parts.append(gather(shards[1]))
-        w_parts.append(gather(shards[2]))
-
-        seg_pack = jnp.stack([seg_id, seg_pos], axis=1)
-        seg_got = send_blocks(seg_pack, cp_index)
+        ng_blocks = ng_own.reshape(n_seq, piece, 2 * d_model)
+        n_got = send_blocks(ng_blocks, cp_index, d_model)
+
         seg_all = jnp.zeros_like(seg_pack)
         for flip, got in enumerate([lax.dynamic_index_in_dim(seg_pack, cp_index, 0, keepdims=True)] + seg_got):
             seg_all = lax.dynamic_update_slice_in_dim(seg_all, got, cp_index ^ flip, 0)
@@ -645,13 +677,11 @@
         sin_a = jnp.sin(angle)
         cos_b = jnp.concatenate([cos_a, cos_a], axis=1)
         sin_b = jnp.concatenate([-sin_a, sin_a], axis=1)
-        ng_blocks = ng_own.reshape(n_seq, piece, 2 * d_model)
-        ng_seq = order(ng_blocks, send_blocks(after(ng_blocks, w_parts[0]), cp_index))
 
         acts, dhs, dbs, owns, recvs = [], [], [], [], []
 
         def third(part, ng_in, extra=()):
-            act, dh, d_w, db = hidden_part(ng_in, ng_oth, w_parts[part], b_ups[0][part], b_ups[1][part], extra)
+            act, dh, d_w, db = hidden_part(ng_in, ng_oth, weights[part], b_ups[0][part], b_ups[1][part], extra)
             own = lax.psum_scatter(d_w, CHIPS, scatter_dimension=0, tiled=True)
             recvs.append(swap_core(jnp.where(first, own[r_in:, :2 * d_model], own[:r_in, :2 * d_model])))
             acts.append(act)
@@ -660,17 +690,31 @@
             owns.append(own)
 
         third(0, ng_own)
-        third(1, after(ng_own, dbs[0]))
-        extra_own = w_parts[1][:, 3 * d_model:]
+        extra_own = whole[0][:, 3 * d_model:]
         wqkv, wo = unpack(extra_own, swap_core(extra_own), r_o, r_in, d_model)
-        od_seq = attention(after(ng_seq, dbs[1]), wqkv, wo, cos_b, sin_b, seg_own)
-        d_keep, d_send = attn_grad(ng_seq, od_seq, r_o, r_in)
-        third(2, ng_own, (d_keep, swap_core(d_send)))
+        od_seq = attention(cp_index, after(ng_blocks, dbs[0]), n_got, g_got, wqkv, wo, cos_b, sin_b, seg_own)
+        d_keep, d_send = attn_grad(cp_index, ng_blocks, n_got, g_got, od_seq, r_o, r_in)
         od_blocks = od_seq.reshape(n_seq, piece, -1)
-        od_loc = order(od_blocks, send_blocks(od_blocks, cp_index))
-
-        out_oth, dn_oth = out_other(acts, dhs, w_parts)
-        x_out, d_x, sums = out_own(acts, dhs, w_parts, od_loc, wo, wqkv, x_loc, ng_own, swap_core(out_oth), swap_core(dn_oth), scale_f, bo_f + bd_f)
+        od_got = send_blocks(od_blocks, cp_index)
+        third(1, ng_own, (d_keep, swap_core(d_send)))
+        third(2, after(ng_own, dbs[1]))
+
+        wd_off = lambda col: 3 * col + 2
+        w12_off = lambda col: col
+        tile = lambda width, col=0: pl.BlockSpec((OUT_ROWS, width), lambda i, *_: (i, col))
+        full = lambda a: pl.BlockSpec(a.shape, lambda i, *_: (0, 0), pipeline_mode=pl.Buffered(1))
+        out_oth = out_other(acts, weights, fwd_product, d_model, wd_off)
+        dn_oth = out_other(after(tuple(dhs), out_oth), weights, bwd_product, 3 * d_model, w12_off)
+        bias_f = bo_f + bd_f
+        x_out = own_call(fwd_own_kernel, cp_index, after(tuple(acts), dn_oth), weights, d_model, wd_off, od_blocks, od_got, (3, 4), 512,
+                         [wo, x_loc, swap_core(out_oth), bias_f], [full(wo), tile(d_model), tile(d_model), full(bias_f)],
+                         tile(d_model), jax.ShapeDtypeStruct((t_len, d_model), BF16), [pltpu.VMEM((OUT_ROWS, qk), BF16)])
+        d_x, sums = own_call(bwd_own_kernel, cp_index, after(tuple(dhs), x_out), weights, 3 * d_model, w12_off, od_blocks, od_got, (0,), qk + 2 * HEAD_DIM,
+                             [wqkv, x_loc, ng_own, swap_core(dn_oth), scale_f],
+                             [full(wqkv), tile(d_model), tile(d_model, 1), tile(d_model), full(scale_f)],
+                             [tile(d_model), pl.BlockSpec((16, d_model), lambda i, *_: (0, 0))],
+                             [jax.ShapeDtypeStruct((t_len, d_model), BF16), jax.ShapeDtypeStruct((16, d_model), F32)],
+                             [pltpu.VMEM((OUT_ROWS, qk + 2 * HEAD_DIM), BF16)])
         x_out = x_out.reshape(n_seq, piece, d_model)
         d_x = d_x.reshape(n_seq, piece, d_model)
 
@@ -684,7 +728,7 @@
         g_scale, g_bias, g_b1, g_b2 = small[:r_in], small[r_in:2 * r_in], small[2 * r_in:2 * r_in + f_blk], small[2 * r_in + f_blk:]
 
         g_w1, g_w2, g_wd = join_up(owns, recvs)
-        g_attn = owns[2][:r_o + r_in, 3 * d_model:]
+        g_attn = owns[1][:r_o + r_in, 3 * d_model:]
         g_wo, g_wq, g_wk, g_wv = g_attn[:r_o, :d_model], g_attn[r_o:, :qk], g_attn[r_o:, qk:qk + HEAD_DIM], g_attn[r_o:, qk + HEAD_DIM:]
         return (x_out, d_x, g_scale, g_wq, g_wk, g_wv, g_wo, g_bias, g_w1, g_b1, g_w2, g_b2, g_wd, g_bias)
 

time: 1100 us -> 1180 us (1.073)
  waiting for transfers between devices: 367 us -> 450 us
    all_gather x3 -> x2, waiting for transfers between devices: 33.9 us -> 85.5 us  [gather(): return lax.all_gather(shard, CHIPS, axis=0, tiled=True)]
    ppermute x9 -> x12, waiting for transfers between devices: 310 us -> 342 us  [send_blocks(): lax.ppermute(sent, ('z', 'y'), [(i, i ^ flip) for i in range(4)])]
  transfers between devices with their start and end apart: 24 -> 26, of which waited for: 10 -> 11; matrix products, arithmetic and copies ran while one was open for 4% -> 4% of each run, Pallas kernels for 54% -> 49%
where the time goes in v1:
time: 1180 us
  Pallas kernels  601 us (51%)
  waiting for transfers between devices  450 us (38%)
  blocking collectives  47.3 us (4%)
  local copies, waits for them, and re-layouts  38 us (3%)
  starting transfers between devices  18.1 us (2%)
  between operations  14.5 us (1%)
  other arithmetic  11.8 us (1%)
    ppermute x12, waiting for transfers between devices, send_blocks(): lax.ppermute(sent, ('z', 'y'), [(i, i ^ flip) for i in range(4)])  342 us
    pallas_call x3, Pallas kernels, hidden_part(): pl.pallas_call(hidden_kernel, grid=(steps,), in_specs=[own_spec, oth_spec...  282 us
    pallas_call x2, Pallas kernels, own_call(): pl.pallas_call(kernel, grid_spec=pltpu.PrefetchScalarGridSpec(num_scalar_...  98.3 us
    pallas_call x1, Pallas kernels, attention(): pl.pallas_call(attn_kernel, grid_spec=pltpu.PrefetchScalarGridSpec(num_sc...  86.4 us
    all_gather x2, waiting for transfers between devices, gather(): return lax.all_gather(shard, CHIPS, axis=0, tiled=True)  85.5 us
    pallas_call x2, Pallas kernels, out_other(): pl.pallas_call(functools.partial(other_kernel, product), grid=(t_len // O...  76.7 us
    psum x1, blocking collectives, local_step(): small = lax.psum(small, ALL_AXES)  32.2 us
  transfers between devices with their start and end apart: 26, of which 11 were waited for; matrix products, arithmetic and copies ran while one was open for 4% of the time, Pallas kernels for 49%

profile of v1, /device:TPU:0, one launch (start us, length us, event | category | flops | bytes accessed | tf_op | source)
XLA Modules:
  0.0 1181.2 jit_solution(8944085892273056706)
XLA Ops:
  7.2 4.8 split_up.1
  12.0 0.7 collective-permute-start.1
  12.8 1.9 pack.1.extra_ref
  15.2 0.9 copy-done.2
  16.1 4.2 stack_up.1
  20.4 0.7 all-gather.6.cloned.1.call-update
  21.1 1.4 vectors.1
  22.5 15.1 %all-gather = bf16[128,512]{1,0:T(8,128)(2,1)S(1)} all-gather(bf16[8,512]{1,0:T(8,128)(2,1)} %vectors.1), channel_id=2, replica_groups=mesh['z'=2,'y'=2,'x'=2,'core'=2] {'z','y','x','core'}, dimensions={0}, use_global_device_ids=true | all-gather | bytes 139264 | tf_op jit(solution)/shard_map/all_gather | solution.py:654
  38.2 0.7 reshape.151.scale_ref.refs_14_
  38.9 8.4 norm.1.own_ref.refs_12_
  48.6 0.7 reshape_squeeze.29.b1_ref
  49.9 0.7 reshape_squeeze.31.b2_ref
  50.6 11.7 collective-permute-done.oth_ref
  62.3 54.9 %all-gather.4.cloned.1.call-done.w_ref.refs_3_ = bf16[1152,4992]{1,0:T(8,128)(2,1)} async-done(((bf16[144,4992]{1,0:T(8,128)(2,1)}), bf16[1152,4992]{1,0:T(8,128)(2,1)}) %all-gather.4.cloned.1.call-update) | async-done | bytes 11501584 | tf_op jit(solution)/shard_map/all_gather | solution.py:649
  117.2 93.0 %hidden.3 = (bf16[4096,1152]{1,0:T(8,128)(2,1)}, bf16[4096,2304]{1,0:T(8,128)(2,1)}, f32[1152,3456]{1,0:T(8,128)}, f32[16,1152]{1,0:T(8,128)}) custom-call(bf16[2048,2304]{1,0:T(8,128)(2,1)} %norm.1.own_ref.refs_12_, bf16[2048,2304]{1,0:T(8,128)(2,1)} %collective-permute-done.oth_ref, bf16[1152,4992]{1,0:T(8,128)(2,1)} %all-gather.4.cloned.1.call-done.w_ref.refs_3_, ...), custom_call_target="tpu_custom_call" | custom-call | flops 65000001536 | bytes 70000000 | tf_op jit(solution)/shard_map/hidden/pallas_call | solution.py:398
  210.3 0.7 reshape_squeeze.34.b1_ref
  211.0 0.7 reshape_squeeze.35.b2_ref
  211.7 30.6 %all-gather.6.cloned.1.call-done.w_ref.refs_4_.refs_5_ = bf16[1152,6912]{1,0:T(8,128)(2,1)} async-done(((bf16[144,6912]{1,0:T(8,128)(2,1)}), bf16[1152,6912]{1,0:T(8,128)(2,1)}) %all-gather.6.cloned.1.call-update) | async-done | bytes 15925264 | tf_op jit(solution)/shard_map/all_gather | solution.py:649
  242.2 93.8 %hidden.5 = (bf16[4096,1152]{1,0:T(8,128)(2,1)}, bf16[4096,2304]{1,0:T(8,128)(2,1)}, f32[1152,3456]{1,0:T(8,128)}, f32[16,1152]{1,0:T(8,128)}) custom-call(bf16[2048,2304]{1,0:T(8,128)(2,1)} %norm.1.own_ref.refs_12_, bf16[2048,2304]{1,0:T(8,128)(2,1)} %collective-permute-done.oth_ref, bf16[1152,6912]{1,0:T(8,128)(2,1)} %all-gather.6.cloned.1.call-done.w_ref.refs_4_.refs_5_, ...), custom_call_target="tpu_custom_call" | custom-call | flops 65000001536 | bytes 70000000 | tf_op jit(solution)/shard_map/hidden/pallas_call | solution.py:398
  336.6 2.4 slice.192.own_ref
  339.2 5.2 constant_dynamic-slice_fusion.7
  344.3 1.5 collective-permute-start.2
  345.8 0.9 fusion.6
  347.3 1.5 collective-permute-start.10
  348.7 1.5 collective-permute-start.11
  350.2 4.5 constant_dynamic-slice_fusion.4
  354.7 31.6 %collective-permute-done.9 = s32[1,2,512]{2,0,1:T(1,128)S(1)} collective-permute-done((s32[1,2,512]{2,0,1:T(1,128)S(1)}, s32[1,2,512]{2,0,1:T(1,128)S(1)}, u32[]{:S(2)}, u32[]{:S(2)}) %collective-permute-start.9) | collective-permute-done | bytes 4128 | tf_op jit(solution)/shard_map/ppermute | solution.py:623
  386.3 1.5 collective-permute-start.3
  387.8 1.5 collective-permute-start.4
  389.8 1.5 collective-permute-start.6
  391.3 1.5 collective-permute-start.7
  393.0 3.7 fusion
  396.7 1.9 pad_maximum_fusion
  398.7 6.1 unpack.1
  404.7 61.1 %collective-permute-done.3.n2_ref = bf16[1,512,1152]{2,1,0:T(8,128)(2,1)} collective-permute-done((bf16[1,512,1152]{2,1,0:T(8,128)(2,1)}, bf16[1,512,1152]{2,1,0:T(8,128)(2,1)}, u32[]{:S(2)}, u32[]{:S(2)}) %collective-permute-start.3) | collective-permute-done | bytes 1179680 | tf_op jit(solution)/shard_map/ppermute | solution.py:623
  465.9 10.1 collective-permute-done.5.g1_ref
  476.0 63.5 %collective-permute-done.6.g2_ref = bf16[1,512,1152]{2,1,0:T(8,128)(2,1)} collective-permute-done((bf16[1,512,1152]{2,1,0:T(8,128)(2,1)}, bf16[1,512,1152]{2,1,0:T(8,128)(2,1)}, u32[]{:S(2)}, u32[]{:S(2)}) %collective-permute-start.6) | collective-permute-done | bytes 1179680 | tf_op jit(solution)/shard_map/ppermute | solution.py:623
  539.5 1.4 broadcast_in_dim.46.segq_ref
  541.5 86.4 %attn.1.dqkv_ref.o_lo_ref.o_hi_ref = bf16[2048,2560]{1,0:T(8,128)(2,1)} custom-call(s32[1]{0:T(128)} %bitcast.cp_ref, bf16[4,512,2304]{2,1,0:T(8,128)(2,1)} %bitcast.60, bf16[1,512,1152]{2,1,0:T(8,128)(2,1)} %collective-permute-done.2.n1_ref, bf16[1,512,1152]{2,1,0:T(8,128)(2,1)} %collective-permute-done.3.n2_ref, ...), custom_call_target="tpu_custom_call" | custom-call | flops 44999999488 | bytes 40000000 | tf_op jit(solution)/shard_map/attn/pallas_call | solution.py:153
  627.9 23.1 %attn_grad.1 = (f32[8,136,1536]{2,1,0:T(8,128)}, f32[8,136,1536]{2,1,0:T(8,128)}) custom-call(s32[1]{0:T(128)} %bitcast.cp_ref, bf16[4,512,2304]{2,1,0:T(8,128)(2,1)} %bitcast.61, bf16[1,512,1152]{2,1,0:T(8,128)(2,1)} %collective-permute-done.2.n1_ref, bf16[1,512,1152]{2,1,0:T(8,128)(2,1)} %collective-permute-done.3.n2_ref, ...), custom_call_target="tpu_custom_call" | custom-call | flops 12000000000 | bytes 33000000 | tf_op jit(solution)/shard_map/attn_grad/pallas_call | solution.py:458
  651.1 0.7 reshape_squeeze.32.b1_ref
  651.8 0.7 reshape_squeeze.33.b2_ref
  652.4 9.7 collective-permute-done.12.refs_1_
  662.1 95.5 %hidden.4 = (bf16[4096,1152]{1,0:T(8,128)(2,1)}, bf16[4096,2304]{1,0:T(8,128)(2,1)}, f32[1152,4992]{1,0:T(8,128)}, f32[16,1152]{1,0:T(8,128)}) custom-call(bf16[2048,2304]{1,0:T(8,128)(2,1)} %norm.1.own_ref.refs_12_, bf16[2048,2304]{1,0:T(8,128)(2,1)} %collective-permute-done.oth_ref, bf16[1152,6912]{1,0:T(8,128)(2,1)} %all-gather.6.cloned.1.call-done.w_ref.refs_4_.refs_5_, ...), custom_call_target="tpu_custom_call" | custom-call | flops 65000001536 | bytes 70000000 | tf_op jit(solution)/shard_map/hidden/pallas_call | solution.py:398
  757.6 27.0 %shard_map.263 = f32[2048,1152]{1,0:T(8,128)} custom-call(bf16[4096,1152]{1,0:T(8,128)(2,1)} %get-tuple-element.65.refs_0_, bf16[4096,1152]{1,0:T(8,128)(2,1)} %get-tuple-element.66.refs_1_, bf16[4096,1152]{1,0:T(8,128)(2,1)} %get-tuple-element.67.refs_2_, bf16[1152,4992]{1,0:T(8,128)(2,1)} %all-gather.4.cloned.1.call-done.w_ref.refs_3_, ...), custom_call_target="tpu_custom_call" | custom-call | flops 16307453952 | bytes 50000000 | tf_op jit(solution)/shard_map/pallas_call | solution.py:507
  784.7 49.8 %shard_map.264 = f32[2048,1152]{1,0:T(8,128)} custom-call(bf16[4096,2304]{1,0:T(8,128)(2,1)} %get-tuple-element.68.refs_0_, bf16[4096,2304]{1,0:T(8,128)(2,1)} %get-tuple-element.69.refs_1_, bf16[4096,2304]{1,0:T(8,128)(2,1)} %get-tuple-element.70.refs_2_, bf16[1152,4992]{1,0:T(8,128)(2,1)} %all-gather.4.cloned.1.call-done.w_ref.refs_3_, ...), custom_call_target="tpu_custom_call" | custom-call | flops 32614907904 | bytes 50000000 | tf_op jit(solution)/shard_map/pallas_call | solution.py:507
  835.2 6.6 constant_dynamic-slice_fusion.1
  841.8 1.5 collective-permute-start.13
  843.3 1.4 collective-permute-start.14
  845.3 0.7 add.68.refs_17_
  846.8 98.0 %collective-permute-done.13.refs_8_.refs_9_.refs_7_ = bf16[1,512,2560]{2,1,0:T(8,128)(2,1)} collective-permute-done((bf16[1,512,2560]{2,1,0:T(8,128)(2,1)}, bf16[1,512,2560]{2,1,0:T(8,128)(2,1)}, u32[]{:S(2)}, u32[]{:S(2)}) %collective-permute-start.13) | collective-permute-done | bytes 2621472 | tf_op jit(solution)/shard_map/ppermute | solution.py:623
  944.8 77.4 %collective-permute-done.15.refs_12_.refs_13_.refs_9_ = bf16[1,512,2560]{2,1,0:T(8,128)(2,1)} collective-permute-done((bf16[1,512,2560]{2,1,0:T(8,128)(2,1)S(1)}, bf16[1,512,2560]{2,1,0:T(8,128)(2,1)}, u32[]{:S(2)}, u32[]{:S(2)}) %collective-permute-start.15) | collective-permute-done | bytes 2621472 | tf_op jit(solution)/shard_map/ppermute | solution.py:623
  1022.2 34.7 %shard_map.265 = bf16[2048,1152]{1,0:T(8,128)(2,1)} custom-call(s32[1]{0:T(128)} %bitcast.cp_ref, bf16[4096,1152]{1,0:T(8,128)(2,1)} %get-tuple-element.65.refs_0_, bf16[4096,1152]{1,0:T(8,128)(2,1)} %get-tuple-element.66.refs_1_, bf16[4096,1152]{1,0:T(8,128)(2,1)} %get-tuple-element.67.refs_2_, ...), custom_call_target="tpu_custom_call" | custom-call | flops 21139292160 | bytes 80000000 | tf_op jit(solution)/shard_map/pallas_call | solution.py:569
  1056.9 63.6 %shard_map.266 = (bf16[2048,1152]{1,0:T(8,128)(2,1)}, f32[16,1152]{1,0:T(8,128)}) custom-call(s32[1]{0:T(128)} %bitcast.cp_ref, bf16[4096,2304]{1,0:T(8,128)(2,1)} %get-tuple-element.68.refs_0_, bf16[4096,2304]{1,0:T(8,128)(2,1)} %get-tuple-element.69.refs_1_, bf16[4096,2304]{1,0:T(8,128)(2,1)} %get-tuple-element.70.refs_2_, ...), custom_call_target="tpu_custom_call" | custom-call | flops 37446746112 | bytes 80000000 | tf_op jit(solution)/shard_map/pallas_call | solution.py:569
  1120.5 0.9 bitcast_reduce_fusion.3
  1121.5 1.4 slice_select_fusion.2
  1122.9 1.4 slice_select_fusion
  1124.8 1.4 slice_select_fusion.1
  1126.5 32.2 %psum.7 = f32[16,1008]{1,0:T(8,128)S(1)} all-reduce(f32[16,1008]{1,0:T(8,128)S(1)} %pad_maximum_fusion.3), channel_id=1, replica_groups=mesh['z'=2,'y'=2,'x'=2,'core'=2] {'z','y','x','core'}, use_global_device_ids=true, to_apply=%region_4.5 | all-reduce | flops 16128 | bytes 129024 | tf_op jit(solution)/shard_map/psum | solution.py:726
  1159.9 1.7 slice.203
  1161.6 1.7 slice.206
  1163.3 1.6 fusion.11
  1164.9 0.8 copy-done.3
  1166.0 7.9 join_up.1
  (104 shorter events, 10.9 us)
Async XLA Ops:
  7.2 110.1 %all-gather.4.cloned.1.call-start = ((), (), s32[]{:S(2)}) async-start(), calls=%async_computation.3 | async-start | bytes 12939264 | tf_op jit(solution)/shard_map/all_gather | solution.py:649
  12.0 3.2 collective-permute-start.1
  15.2 0.9 copy-start.2
  20.3 221.9 %all-gather.6.cloned.1.call-start = ((), (), s32[]{:S(2)}) async-start(), calls=%async_computation.4 | async-start | bytes 17915904 | tf_op jit(solution)/shard_map/all_gather | solution.py:649
  21.1 1100.4 %reduce-scatter.6.cloned.1.call-start = ((), (), s32[]{:S(2)}) async-start(), calls=%async_computation.6 | async-start | bytes 17915904 | tf_op jit(solution)/shard_map/reduce_scatter | solution.py:685
  47.3 15.0 %collective-permute-start = (bf16[2048,2304]{1,0:T(8,128)(2,1)}, bf16[2048,2304]{1,0:T(8,128)(2,1)}, u32[]{:S(2)}, u32[]{:S(2)}) collective-permute-start(bf16[2048,2304]{1,0:T(8,128)(2,1)} %norm.1.own_ref.refs_12_), channel_id=1, source_target_pairs={{0,1},{1,0},{2,3},{3,2},{4,5},{5,4},{6,7},{7,6},{8,9},{9,8},{10,11... | collective-permute-start | bytes 28311560 | tf_op jit(solution)/shard_map/ppermute | solution.py:617
  210.3 912.6 %reduce-scatter.8.cloned.1.call-start = ((), (), s32[]{:S(2)}) async-start(), calls=%async_computation.7 | async-start | bytes 17915904 | tf_op jit(solution)/shard_map/reduce_scatter | solution.py:685
  336.1 788.7 %reduce-scatter.4.cloned.1.call-start = ((), (), s32[]{:S(2)}) async-start(), calls=%async_computation.5 | async-start | bytes 25878528 | tf_op jit(solution)/shard_map/reduce_scatter | solution.py:685
  339.1 5.3 copy-start
  339.1 52.2 %collective-permute-start.8 = (bf16[1152,1536]{1,0:T(8,128)(2,1)S(1)}, bf16[1152,1536]{1,0:T(8,128)(2,1)}, u32[]{:S(2)}, u32[]{:S(2)}) collective-permute-start(bf16[1152,1536]{1,0:T(8,128)(2,1)S(1)} %slice.192.own_ref), channel_id=1, source_target_pairs={{0,1},{1,0},{2,3},{3,2},{4,5},{5,4},{6,7},{7,6},{8,9},{9,8},{10,11... | collective-permute-start | bytes 10616840 | tf_op jit(solution)/shard_map/ppermute | solution.py:617
  339.2 6.6 copy-start.12
  344.3 45.5 %collective-permute-start.2 = (bf16[1,512,1152]{2,1,0:T(8,128)(2,1)}, bf16[1,512,1152]{2,1,0:T(8,128)(2,1)}, u32[]{:S(2)}, u32[]{:S(2)}) collective-permute-start(bf16[1,512,1152]{2,1,0:T(8,128)(2,1)} %get-tuple-element.95), channel_id=1, source_target_pairs={{0,4},{4,0},{8,12},{12,8},{1,5},{5,1},{9,13},{13,9},{2,6},{6,2},{1... | collective-permute-start | bytes 3538952 | tf_op jit(solution)/shard_map/ppermute | solution.py:623
  346.7 39.7 %collective-permute-start.9 = (s32[1,2,512]{2,0,1:T(1,128)S(1)}, s32[1,2,512]{2,0,1:T(1,128)S(1)}, u32[]{:S(2)}, u32[]{:S(2)}) collective-permute-start(s32[1,2,512]{2,0,1:T(1,128)S(1)} %get-tuple-element.116), channel_id=1, source_target_pairs={{0,4},{4,0},{8,12},{12,8},{1,5},{5,1},{9,13},{13,9},{2,6},{6,2},{1... | collective-permute-start | bytes 12296 | tf_op jit(solution)/shard_map/ppermute | solution.py:623
  347.3 40.5 %collective-permute-start.10 = (s32[1,2,512]{2,0,1:T(1,128)S(1)}, s32[1,2,512]{2,0,1:T(1,128)S(1)}, u32[]{:S(2)}, u32[]{:S(2)}) collective-permute-start(s32[1,2,512]{2,0,1:T(1,128)S(1)} %get-tuple-element.117), channel_id=1, source_target_pairs={{0,8},{4,12},{8,0},{12,4},{1,9},{5,13},{9,1},{13,5},{2,10},{6,14},... | collective-permute-start | bytes 12296 | tf_op jit(solution)/shard_map/ppermute | solution.py:623
  348.7 40.5 %collective-permute-start.11 = (s32[1,2,512]{2,0,1:T(1,128)S(1)}, s32[1,2,512]{2,0,1:T(1,128)S(1)}, u32[]{:S(2)}, u32[]{:S(2)}) collective-permute-start(s32[1,2,512]{2,0,1:T(1,128)S(1)} %get-tuple-element.114), channel_id=1, source_target_pairs={{0,12},{4,8},{8,4},{12,0},{1,13},{5,9},{9,5},{13,1},{2,14},{6,10},... | collective-permute-start | bytes 12296 | tf_op jit(solution)/shard_map/ppermute | solution.py:623
  386.3 79.6 %collective-permute-start.3 = (bf16[1,512,1152]{2,1,0:T(8,128)(2,1)}, bf16[1,512,1152]{2,1,0:T(8,128)(2,1)}, u32[]{:S(2)}, u32[]{:S(2)}) collective-permute-start(bf16[1,512,1152]{2,1,0:T(8,128)(2,1)} %get-tuple-element.94), channel_id=1, source_target_pairs={{0,8},{4,12},{8,0},{12,4},{1,9},{5,13},{9,1},{13,5},{2,10},{6,14},... | collective-permute-start | bytes 3538952 | tf_op jit(solution)/shard_map/ppermute | solution.py:623
  387.8 78.1 %collective-permute-start.4 = (bf16[1,512,1152]{2,1,0:T(8,128)(2,1)}, bf16[1,512,1152]{2,1,0:T(8,128)(2,1)}, u32[]{:S(2)}, u32[]{:S(2)}) collective-permute-start(bf16[1,512,1152]{2,1,0:T(8,128)(2,1)} %get-tuple-element.93), channel_id=1, source_target_pairs={{0,12},{4,8},{8,4},{12,0},{1,13},{5,9},{9,5},{13,1},{2,14},{6,10},... | collective-permute-start | bytes 3538952 | tf_op jit(solution)/shard_map/ppermute | solution.py:623
  389.2 86.7 %collective-permute-start.5 = (bf16[1,512,1152]{2,1,0:T(8,128)(2,1)}, bf16[1,512,1152]{2,1,0:T(8,128)(2,1)}, u32[]{:S(2)}, u32[]{:S(2)}) collective-permute-start(bf16[1,512,1152]{2,1,0:T(8,128)(2,1)} %get-tuple-element.97), channel_id=1, source_target_pairs={{0,4},{4,0},{8,12},{12,8},{1,5},{5,1},{9,13},{13,9},{2,6},{6,2},{1... | collective-permute-start | bytes 3538952 | tf_op jit(solution)/shard_map/ppermute | solution.py:623
  389.8 149.7 %collective-permute-start.6 = (bf16[1,512,1152]{2,1,0:T(8,128)(2,1)}, bf16[1,512,1152]{2,1,0:T(8,128)(2,1)}, u32[]{:S(2)}, u32[]{:S(2)}) collective-permute-start(bf16[1,512,1152]{2,1,0:T(8,128)(2,1)} %get-tuple-element.98), channel_id=1, source_target_pairs={{0,8},{4,12},{8,0},{12,4},{1,9},{5,13},{9,1},{13,5},{2,10},{6,14},... | collective-permute-start | bytes 3538952 | tf_op jit(solution)/shard_map/ppermute | solution.py:623
  391.3 148.2 %collective-permute-start.7 = (bf16[1,512,1152]{2,1,0:T(8,128)(2,1)}, bf16[1,512,1152]{2,1,0:T(8,128)(2,1)S(1)}, u32[]{:S(2)}, u32[]{:S(2)}) collective-permute-start(bf16[1,512,1152]{2,1,0:T(8,128)(2,1)} %get-tuple-element.96), channel_id=1, source_target_pairs={{0,12},{4,8},{8,4},{12,0},{1,13},{5,9},{9,5},{13,1},{2,14},{6,10},... | collective-permute-start | bytes 3538952 | tf_op jit(solution)/shard_map/ppermute | solution.py:623
  539.5 2.0 copy-start.1
  627.9 23.1 %copy-start.10 = (f32[8,144]{1,0:T(8,128)S(1)}, f32[8,144]{1,0:T(8,128)}, u32[]{:S(2)}) copy-start(f32[8,144]{1,0:T(8,128)} %get-tuple-element.86) | copy-start | bytes 13828
  627.9 23.8 %copy-start.11 = (f32[8,144]{1,0:T(8,128)S(1)}, f32[8,144]{1,0:T(8,128)}, u32[]{:S(2)}) copy-start(f32[8,144]{1,0:T(8,128)} %get-tuple-element.83) | copy-start | bytes 13828
  651.0 11.1 collective-permute-start.12
  784.6 237.6 %collective-permute-start.16 = (f32[2048,1152]{1,0:T(8,128)}, f32[2048,1152]{1,0:T(8,128)}, u32[]{:S(2)}, u32[]{:S(2)}) collective-permute-start(f32[2048,1152]{1,0:T(8,128)} %shard_map.263), channel_id=1, source_target_pairs={{0,1},{1,0},{2,3},{3,2},{4,5},{5,4},{6,7},{7,6},{8,9},{9,8},{10,11... | collective-permute-start | bytes 28311560 | tf_op jit(solution)/shard_map/ppermute | solution.py:617
  834.5 222.4 %collective-permute-start.17 = (f32[2048,1152]{1,0:T(8,128)}, f32[2048,1152]{1,0:T(8,128)}, u32[]{:S(2)}, u32[]{:S(2)}) collective-permute-start(f32[2048,1152]{1,0:T(8,128)} %shard_map.264), channel_id=1, source_target_pairs={{0,1},{1,0},{2,3},{3,2},{4,5},{5,4},{6,7},{7,6},{8,9},{9,8},{10,11... | collective-permute-start | bytes 28311560 | tf_op jit(solution)/shard_map/ppermute | solution.py:617
  835.2 10.1 copy-start.8
  835.2 10.1 copy-start.9
  835.2 10.8 copy-start.5
  835.2 11.0 copy-start.6
  835.2 11.1 copy-start.7
  841.8 103.0 %collective-permute-start.13 = (bf16[1,512,2560]{2,1,0:T(8,128)(2,1)}, bf16[1,512,2560]{2,1,0:T(8,128)(2,1)}, u32[]{:S(2)}, u32[]{:S(2)}) collective-permute-start(bf16[1,512,2560]{2,1,0:T(8,128)(2,1)} %get-tuple-element.92), channel_id=1, source_target_pairs={{0,4},{4,0},{8,12},{12,8},{1,5},{5,1},{9,13},{13,9},{2,6},{6,2},{1... | collective-permute-start | bytes 7864328 | tf_op jit(solution)/shard_map/ppermute | solution.py:623
  843.3 101.5 %collective-permute-start.14 = (bf16[1,512,2560]{2,1,0:T(8,128)(2,1)}, bf16[1,512,2560]{2,1,0:T(8,128)(2,1)}, u32[]{:S(2)}, u32[]{:S(2)}) collective-permute-start(bf16[1,512,2560]{2,1,0:T(8,128)(2,1)} %get-tuple-element.91), channel_id=1, source_target_pairs={{0,8},{4,12},{8,0},{12,4},{1,9},{5,13},{9,1},{13,5},{2,10},{6,14},... | collective-permute-start | bytes 7864328 | tf_op jit(solution)/shard_map/ppermute | solution.py:623
  844.7 177.5 %collective-permute-start.15 = (bf16[1,512,2560]{2,1,0:T(8,128)(2,1)S(1)}, bf16[1,512,2560]{2,1,0:T(8,128)(2,1)}, u32[]{:S(2)}, u32[]{:S(2)}) collective-permute-start(bf16[1,512,2560]{2,1,0:T(8,128)(2,1)S(1)} %get-tuple-element.90), channel_id=1, source_target_pairs={{0,12},{4,8},{8,4},{12,0},{1,13},{5,9},{9,5},{13,1},{2,14},{6,10},... | collective-permute-start | bytes 7864328 | tf_op jit(solution)/shard_map/ppermute | solution.py:623
  1122.8 42.1 %collective-permute-start.18 = (f32[72,2304]{1,0:T(8,128)S(1)}, f32[72,2304]{1,0:T(8,128)S(1)}, u32[]{:S(2)}, u32[]{:S(2)}) collective-permute-start(f32[72,2304]{1,0:T(8,128)S(1)} %slice_select_fusion.2), channel_id=1, source_target_pairs={{0,1},{1,0},{2,3},{3,2},{4,5},{5,4},{6,7},{7,6},{8,9},{9,8},{10,11... | collective-permute-start | bytes 1990664 | tf_op jit(solution)/shard_map/ppermute | solution.py:617
  1124.3 40.6 %collective-permute-start.20 = (f32[72,2304]{1,0:T(8,128)S(1)}, f32[72,2304]{1,0:T(8,128)S(1)}, u32[]{:S(2)}, u32[]{:S(2)}) collective-permute-start(f32[72,2304]{1,0:T(8,128)S(1)} %slice_select_fusion), channel_id=1, source_target_pairs={{0,1},{1,0},{2,3},{3,2},{4,5},{5,4},{6,7},{7,6},{8,9},{9,8},{10,11... | collective-permute-start | bytes 1990664 | tf_op jit(solution)/shard_map/ppermute | solution.py:617
  1126.1 38.8 %collective-permute-start.19 = (f32[72,2304]{1,0:T(8,128)S(1)}, f32[72,2304]{1,0:T(8,128)}, u32[]{:S(2)}, u32[]{:S(2)}) collective-permute-start(f32[72,2304]{1,0:T(8,128)S(1)} %slice_select_fusion.1), channel_id=1, source_target_pairs={{0,1},{1,0},{2,3},{3,2},{4,5},{5,4},{6,7},{7,6},{8,9},{9,8},{10,11... | collective-permute-start | bytes 1990664 | tf_op jit(solution)/shard_map/ppermute | solution.py:617
  1159.3 14.6 %copy-start.13 = (f32[72]{0:T(128)}, f32[72]{0:T(128)S(1)}, u32[]{:S(2)}) copy-start(f32[72]{0:T(128)S(1)} %get-tuple-element.152) | copy-start | bytes 868
  1164.9 0.9 copy-start.3
  1164.9 1.1 copy-start.4
Sparse Core Ops, SparseCore 0:
  20.5 96.7 all-gather.3
  120.0 122.2 all-gather.5
  246.5 136.6 reduce-scatter.5
  387.4 216.4 reduce-scatter.7
  757.8 232.3 reduce-scatter.3

commit v2 on v1

--- a/solution.py
+++ b/solution.py
@@ -35,29 +35,33 @@
 
 
 def attn_kernel(cp_ref, own_ref, n1_ref, n2_ref, n3_ref, g1_ref, g2_ref, g3_ref, wqkv_ref, wo_ref, cos_ref, sin_ref, cosk_ref, sink_ref, segq_ref, segk_ref, out_ref,
-                n_s, g_s, q_s, do_s, k_s, v_s, kt_s, vt_s, mask_s, s_s, p_s, dk_s, dv_s):
+                n_buf, g_buf, sems, q_s, do_s, k_s, v_s, kt_s, vt_s, mask_s, s_s, p_s, dk_s, dv_s):
     step = pl.program_id(0)
     n_blocks = pl.num_programs(0)
-    rows, d_model = n_s.shape
+    rows, d_model = n_buf.shape[1:]
     qk = N_HEADS * HEAD_DIM
     base = pl.multiple_of(step * rows, rows)
     cos_b = cos_ref[...]
     sin_b = sin_ref[...]
-    flip = step ^ cp_ref[0]
-
-    @pl.when(flip == 0)
-    def _():
-        n_s[...] = own_ref[0, :, :d_model]
-        g_s[...] = own_ref[0, :, d_model:]
-
-    for i, (n_ref, g_ref) in enumerate(((n1_ref, g1_ref), (n2_ref, g2_ref), (n3_ref, g3_ref))):
-        @pl.when(flip == i + 1)
-        def _():
-            n_s[...] = n_ref[0]
-            g_s[...] = g_ref[0]
-
-    n_blk = n_s[...]
-    g_blk = g_s[...]
+    slot = lax.rem(step, 2)
+
+    def fetch(at_step):
+        flip = at_step ^ cp_ref[0]
+        to = lax.rem(at_step, 2)
+        own = own_ref.at[cp_ref[0]]
+        sources = ((own.at[:, :d_model], own.at[:, d_model:]), (n1_ref.at[0], g1_ref.at[0]), (n2_ref.at[0], g2_ref.at[0]), (n3_ref.at[0], g3_ref.at[0]))
+        for i, (n_src, g_src) in enumerate(sources):
+            @pl.when(flip == i)
+            def _():
+                pltpu.make_async_copy(n_src, n_buf.at[to], sems.at[0, to]).start()
+                pltpu.make_async_copy(g_src, g_buf.at[to], sems.at[1, to]).start()
+
+    pl.when(step == 0)(lambda: fetch(step))
+    pl.when(step + 1 < n_blocks)(lambda: fetch(step + 1))
+    pltpu.make_async_copy(n1_ref.at[0], n_buf.at[slot], sems.at[0, slot]).wait()
+    pltpu.make_async_copy(g1_ref.at[0], g_buf.at[slot], sems.at[1, slot]).wait()
+    n_blk = n_buf[slot]
+    g_blk = g_buf[slot]
 
     @pl.when(step == 0)
     def _():
@@ -148,17 +152,17 @@
     segk = jnp.broadcast_to(seg_own[None, :], (8, t_len))
     row_spec = lambda width: pl.BlockSpec((rows, width), lambda i, cp: (i, 0))
     full = lambda a: pl.BlockSpec(a.shape, lambda i, cp: (0,) * a.ndim, pipeline_mode=pl.Buffered(1))
-    own_spec = pl.BlockSpec((1, rows, both), lambda i, cp: (cp[0], 0, 0), pipeline_mode=pl.Buffered(1))
+    anywhere = pl.BlockSpec(memory_space=pl.ANY)
     width = 2 * (qk + HEAD_DIM)
     return pl.pallas_call(
         attn_kernel,
         grid_spec=pltpu.PrefetchScalarGridSpec(
             num_scalar_prefetch=1,
             grid=(4,),
-            in_specs=[own_spec] + [full(a) for a in n_got + g_got] + [full(wqkv), full(wo), row_spec(ROPE_DIMS), row_spec(ROPE_DIMS), full(cos_b), full(sin_b), row_spec(128), full(segk)],
+            in_specs=[anywhere] * 7 + [full(wqkv), full(wo), row_spec(ROPE_DIMS), row_spec(ROPE_DIMS), full(cos_b), full(sin_b), row_spec(128), full(segk)],
             out_specs=pl.BlockSpec((t_len, width), lambda i, cp: (0, 0)),
             scratch_shapes=[
-                pltpu.VMEM((rows, both // 2), BF16), pltpu.VMEM((rows, both // 2), BF16),
+                pltpu.VMEM((2, rows, both // 2), BF16), pltpu.VMEM((2, rows, both // 2), BF16), pltpu.SemaphoreType.DMA((2, 2)),
                 pltpu.VMEM((N_HEADS, rows, HEAD_DIM), BF16), pltpu.VMEM((N_HEADS, rows, HEAD_DIM), BF16),
                 pltpu.VMEM((t_len, HEAD_DIM), BF16), pltpu.VMEM((t_len, HEAD_DIM), BF16),
                 pltpu.VMEM((HEAD_DIM, t_len), BF16), pltpu.VMEM((HEAD_DIM, t_len), BF16),
@@ -301,9 +305,10 @@
 GELU_A = 0.044715
 
 
-def hidden_kernel(own_ref, oth_ref, w_ref, b1_ref, b2_ref, *refs):
-    extra_refs = refs[:-10]
-    act_ref, dh_ref, dw_ref, db_ref, h_s, da_s, ng_s, acc_s, side_s, sems = refs[-10:]
+def hidden_kernel(mode, own_ref, oth_ref, w_ref, b1_ref, b2_ref, *refs):
+    extra_refs = refs[:2] if mode == 'extra' else ()
+    act_ref, dh_ref, *dw_refs, db_ref, h_s, da_s, ng_s, acc_s, side_s, sems = refs[len(extra_refs):]
+    dw_ref = dw_refs[0]
     step = pl.program_id(0)
     last = pl.num_programs(0) - 1
     rows, d_model = da_s.shape
@@ -377,12 +382,26 @@
 
     @pl.when(step == last)
     def _():
-        copy = pltpu.make_async_copy(acc_s, dw_ref.at[:, :3 * d_model], sems.at[0])
-        copy.start()
-        copy.wait()
-
-
-def hidden_part(ng_own, ng_oth, weight, b1, b2, extra=()):
+        if mode != 'halves':
+            copy = pltpu.make_async_copy(acc_s, dw_ref.at[:, :3 * d_model], sems.at[0])
+            copy.start()
+            copy.wait()
+            return
+        x_index = lax.axis_index('x')
+        block = d_model // 8
+
+        def each(act):
+            for chip in range(8):
+                for ref, flip in zip(dw_refs, (0, 1)):
+                    @pl.when((x_index ^ flip) == chip % 2)
+                    def _():
+                        act(pltpu.make_async_copy(acc_s.at[chip * block:(chip + 1) * block, :], ref.at[chip // 2], sems.at[0]))
+
+        each(lambda copy: copy.start())
+        each(lambda copy: copy.wait())
+
+
+def hidden_part(ng_own, ng_oth, weight, b1, b2, extra=(), halves=False):
     w_part, w_col = weight
     t_len, both = ng_own.shape
     d_model = both // 2
@@ -395,19 +414,82 @@
     row = lambda width: pl.BlockSpec((rows, width), lambda i: (i, 0))
     blk = [pl.BlockSpec((1,) + a.shape[1:], lambda i: (i, 0, 0)) for a in extra]
     side = (2, d_model // 8, extra[0].shape[2]) if extra else (2, 8, 128)
-    return pl.pallas_call(
-        hidden_kernel,
+    mode = 'halves' if halves else 'extra' if extra else 'plain'
+    if halves:
+        grads = [jax.ShapeDtypeStruct((4, d_model // 8, 3 * d_model), F32)] * 2
+    else:
+        grads = [jax.ShapeDtypeStruct((d_model, 3 * d_model + (extra[0].shape[2] if extra else 0)), F32)]
+    return pl.pallas_call(
+        functools.partial(hidden_kernel, mode),
         grid=(steps,),
         in_specs=[own_spec, oth_spec, full(w_part, 3 * d_model, w_col), full(b1, d_model), full(b2, d_model)] + blk,
-        out_specs=[row(d_model), row(2 * d_model), pl.BlockSpec(memory_space=pl.ANY), pl.BlockSpec((16, d_model), lambda i: (0, 0))],
+        out_specs=[row(d_model), row(2 * d_model)] + [pl.BlockSpec(memory_space=pl.ANY)] * len(grads) + [pl.BlockSpec((16, d_model), lambda i: (0, 0))],
         out_shape=[jax.ShapeDtypeStruct((2 * t_len, d_model), BF16), jax.ShapeDtypeStruct((2 * t_len, 2 * d_model), BF16),
-                   jax.ShapeDtypeStruct((d_model, 3 * d_model + (extra[0].shape[2] if extra else 0)), F32), jax.ShapeDtypeStruct((16, d_model), F32)],
+                   *grads, jax.ShapeDtypeStruct((16, d_model), F32)],
         scratch_shapes=[pltpu.VMEM((rows, 2 * d_model), F32), pltpu.VMEM((rows, d_model), F32), pltpu.VMEM((rows, both), BF16),
                         pltpu.VMEM((d_model, 3 * d_model), F32), pltpu.VMEM(side, F32), pltpu.SemaphoreType.DMA((3,))],
         compiler_params=pltpu.CompilerParams(vmem_limit_bytes=63 * 1024 * 1024, dimension_semantics=('arbitrary',)),
         cost_estimate=pl.CostEstimate(flops=65_000_000_000, bytes_accessed=70_000_000, transcendentals=4_700_000),
         name='hidden',
     )(ng_own, ng_oth, w_part, b1, b2, *extra)
+
+
+A_SHARE = 14
+
+
+def fold_first_kernel(keep_ref, got_ref, keep_a, send_a, keep_b, send_b):
+    z_at, y_at = pl.program_id(0) // 2, lax.rem(pl.program_id(0), 2)
+    cols = keep_a.shape[2]
+    a = keep_ref[0, :, :cols] + got_ref[0, :, :cols]
+    b = keep_ref[0, :, cols:] + got_ref[0, :, cols:]
+    z_own = z_at == lax.axis_index('z')
+    y_own = y_at == lax.axis_index('y')
+    for ref, hit, at, value in ((keep_a, z_own, y_at, a), (send_a, jnp.logical_not(z_own), y_at, a), (keep_b, y_own, z_at, b), (send_b, jnp.logical_not(y_own), z_at, b)):
+        @pl.when(hit)
+        def _():
+            ref[at] = value
+
+
+def fold_first(keep, got):
+    _, rows, width = keep.shape
+    cols = A_SHARE * 128
+    block = pl.BlockSpec((1, rows, width), lambda i: (i, 0, 0))
+    shapes = [(2, rows, cols)] * 2 + [(2, rows, width - cols)] * 2
+    return pl.pallas_call(
+        fold_first_kernel, grid=(4,), in_specs=[block, block], name='fold_first',
+        out_specs=[pl.BlockSpec(shape, lambda i: (0, 0, 0)) for shape in shapes],
+        out_shape=[jax.ShapeDtypeStruct(shape, F32) for shape in shapes],
+        compiler_params=pltpu.CompilerParams(vmem_limit_bytes=48 * 1024 * 1024, dimension_semantics=('arbitrary',)),
+        cost_estimate=pl.CostEstimate(flops=6_000_000_000, bytes_accessed=24_000_000, transcendentals=0),
+    )(keep, got)
+
+
+def fold_second_kernel(a_ref, got_a_ref, b_ref, got_b_ref, keep_a, send_a, keep_b, send_b):
+    for ref, got_ref, keep, send, own in ((a_ref, got_a_ref, keep_a, send_a, lax.axis_index('y')), (b_ref, got_b_ref, keep_b, send_b, lax.axis_index('z'))):
+        keep[...] = ref[own] + got_ref[own]
+        send[...] = ref[1 - own] + got_ref[1 - own]
+
+
+def fold_second(*parts):
+    shapes = [part.shape[1:] for part in parts]
+    return pl.pallas_call(
+        fold_second_kernel, out_shape=[jax.ShapeDtypeStruct(shape, F32) for shape in shapes], name='fold_second',
+        compiler_params=pltpu.CompilerParams(vmem_limit_bytes=48 * 1024 * 1024),
+        cost_estimate=pl.CostEstimate(flops=3_000_000_000, bytes_accessed=12_000_000, transcendentals=0),
+    )(*parts)
+
+
+def fold_third_kernel(a_ref, got_a_ref, b_ref, got_b_ref, out_ref):
+    cols = a_ref.shape[1]
+    out_ref[:, :cols] = a_ref[...] + got_a_ref[...]
+    out_ref[:, cols:] = b_ref[...] + got_b_ref[...]
+
+
+def fold_third(a, got_a, b, got_b):
+    return pl.pallas_call(
+        fold_third_kernel, out_shape=jax.ShapeDtypeStruct((a.shape[0], a.shape[1] + b.shape[1]), F32), name='fold_third',
+        cost_estimate=pl.CostEstimate(flops=2_000_000_000, bytes_accessed=6_000_000, transcendentals=0),
+    )(a, got_a, b, got_b)
 
 
 def attn_grad_kernel(cp_ref, own_ref, n1_ref, n2_ref, n3_ref, g1_ref, g2_ref, g3_ref, dqkv_ref, o_lo_ref, o_hi_ref, keep_ref, send_ref):
@@ -562,9 +644,9 @@
     for i, source in enumerate([od_blocks] + od_got):
         for col in od_cols:
             if i == 0:
-                specs.append(pl.BlockSpec((1, OUT_ROWS, od_width), lambda j, cp, col=col: (cp[0], j % 2, col)))
+                specs.append(pl.BlockSpec((1, OUT_ROWS, od_width), lambda j, cp, col=col: (cp[0], jnp.clip(j - 2 * cp[0], 0, 1), col)))
             else:
-                specs.append(pl.BlockSpec((1, OUT_ROWS, od_width), lambda j, cp, col=col: (0, j % 2, col)))
+                specs.append(pl.BlockSpec((1, OUT_ROWS, od_width), lambda j, cp, col=col, i=i: (0, jnp.clip(j - 2 * (cp[0] ^ i), 0, 1), col)))
             args.append(source)
     return pl.pallas_call(
         kernel,
@@ -615,6 +697,17 @@
 
     def swap_core(values):
         return lax.ppermute(values, 'core', [(0, 1), (1, 0)])
+
+    def scatter_by_hand(keep, send):
+        def shift(values, axis):
+            return lax.ppermute(values, axis, [(0, 1), (1, 0)])
+
+        keep_a, send_a, keep_b, send_b = fold_first(keep, shift(send, 'x'))
+        keep_a, send_a, keep_b, send_b = fold_second(keep_a, shift(send_a, 'z'), keep_b, shift(send_b, 'y'))
+        return fold_third(keep_a, shift(send_a, 'y'), keep_b, shift(send_b, 'z'))
+
+    def after(value, *deps):
+        return lax.optimization_barrier((value,) + deps)[0]
 
     def send_blocks(values, cp_index, width=None):
         got = []
@@ -634,9 +727,6 @@
         f_blk = b_up1.shape[0]
         sub = f_blk // N_PART
         qk = N_HEADS * HEAD_DIM
-
-        def after(value, *deps):
-            return lax.optimization_barrier((value,) + deps)[0]
 
         seg_pack = jnp.stack([seg_id, seg_pos], axis=1)
         seg_got = send_blocks(seg_pack, cp_index)
@@ -681,8 +771,11 @@
         acts, dhs, dbs, owns, recvs = [], [], [], [], []
 
         def third(part, ng_in, extra=()):
-            act, dh, d_w, db = hidden_part(ng_in, ng_oth, weights[part], b_ups[0][part], b_ups[1][part], extra)
-            own = lax.psum_scatter(d_w, CHIPS, scatter_dimension=0, tiled=True)
+            act, dh, *d_w, db = hidden_part(ng_in, ng_oth, weights[part], b_ups[0][part], b_ups[1][part], extra, halves=part == 0)
+            if part == 0:
+                own = scatter_by_hand(*d_w)
+            else:
+                own = lax.psum_scatter(d_w[0], CHIPS, scatter_dimension=0, tiled=True)
             recvs.append(swap_core(jnp.where(first, own[r_in:, :2 * d_model], own[:r_in, :2 * d_model])))
             acts.append(act)
             dhs.append(dh)
@@ -692,12 +785,12 @@
         third(0, ng_own)
         extra_own = whole[0][:, 3 * d_model:]
         wqkv, wo = unpack(extra_own, swap_core(extra_own), r_o, r_in, d_model)
-        od_seq = attention(cp_index, after(ng_blocks, dbs[0]), n_got, g_got, wqkv, wo, cos_b, sin_b, seg_own)
+        od_seq = attention(cp_index, ng_blocks, n_got, g_got, wqkv, wo, cos_b, sin_b, seg_own)
+        third(1, ng_own)
         d_keep, d_send = attn_grad(cp_index, ng_blocks, n_got, g_got, od_seq, r_o, r_in)
         od_blocks = od_seq.reshape(n_seq, piece, -1)
         od_got = send_blocks(od_blocks, cp_index)
-        third(1, ng_own, (d_keep, swap_core(d_send)))
-        third(2, after(ng_own, dbs[1]))
+        third(2, ng_own, (d_keep, swap_core(d_send)))
 
         wd_off = lambda col: 3 * col + 2
         w12_off = lambda col: col
@@ -728,7 +821,7 @@
         g_scale, g_bias, g_b1, g_b2 = small[:r_in], small[r_in:2 * r_in], small[2 * r_in:2 * r_in + f_blk], small[2 * r_in + f_blk:]
 
         g_w1, g_w2, g_wd = join_up(owns, recvs)
-        g_attn = owns[1][:r_o + r_in, 3 * d_model:]
+        g_attn = owns[2][:r_o + r_in, 3 * d_model:]
         g_wo, g_wq, g_wk, g_wv = g_attn[:r_o, :d_model], g_attn[r_o:, :qk], g_attn[r_o:, qk:qk + HEAD_DIM], g_attn[r_o:, qk + HEAD_DIM:]
         return (x_out, d_x, g_scale, g_wq, g_wk, g_wv, g_wo, g_bias, g_w1, g_b1, g_w2, g_b2, g_wd, g_bias)
 

time: 1180 us -> 1360 us (1.15)
  waiting for transfers between devices: 450 us -> 599 us
  Pallas kernels: 601 us -> 615 us
    ppermute x0 -> x5, waiting for transfers between devices: none -> 217 us  [shift(): return lax.ppermute(values, axis, [(0, 1), (1, 0)])]
    ppermute x12, waiting for transfers between devices: 342 us -> 274 us  [send_blocks(): lax.ppermute(sent, ('z', 'y'), [(i, i ^ flip) for i in range(4)])]
    pallas_call x3 -> x6, Pallas kernels: 282 us -> 298 us  [the longest x3 283 us: hidden_part(): pl.pallas_call(functools.partial(hidden_kernel, mode), grid=(steps,), in_...]
  transfers between devices with their start and end apart: 26 -> 30, of which waited for: 11 -> 16; matrix products, arithmetic and copies ran while one was open for 4% -> 3% of each run, Pallas kernels for 49% -> 44%
where the time goes in v2:
time: 1360 us; the launch traced here: 1350 us
  Pallas kernels  615 us (45%)
  waiting for transfers between devices  599 us (44%)
  blocking collectives  47.1 us (3%)
  local copies, waits for them, and re-layouts  41.5 us (3%)
  starting transfers between devices  25.3 us (2%)
  between operations  14.5 us (1%)
    pallas_call x3, Pallas kernels, hidden_part(): pl.pallas_call(functools.partial(hidden_kernel, mode), grid=(steps,), in_...  283 us
    ppermute x12, waiting for transfers between devices, send_blocks(): lax.ppermute(sent, ('z', 'y'), [(i, i ^ flip) for i in range(4)])  274 us
    ppermute x5, waiting for transfers between devices, shift(): return lax.ppermute(values, axis, [(0, 1), (1, 0)])  217 us
    pallas_call x2, Pallas kernels, own_call(): pl.pallas_call(kernel, grid_spec=pltpu.PrefetchScalarGridSpec(num_scalar_...  98.1 us
    all_gather x2, waiting for transfers between devices, gather(): return lax.all_gather(shard, CHIPS, axis=0, tiled=True)  86 us
    pallas_call x1, Pallas kernels, attention(): pl.pallas_call(attn_kernel, grid_spec=pltpu.PrefetchScalarGridSpec(num_sc...  84.3 us
    pallas_call x2, Pallas kernels, out_other(): pl.pallas_call(functools.partial(other_kernel, product), grid=(t_len // O...  76.5 us
    psum x1, blocking collectives, local_step(): small = lax.psum(small, ALL_AXES)  32.1 us
  transfers between devices with their start and end apart: 30, of which 16 were waited for; matrix products, arithmetic and copies ran while one was open for 3% of the time, Pallas kernels for 44%

profile of v2, /device:TPU:0, one launch (start us, length us, event | category | flops | bytes accessed | tf_op | source)
XLA Modules:
  0.0 1354.5 jit_solution(6744233403254164496)
XLA Ops:
  7.2 4.8 split_up.1
  12.8 1.9 pack.1.extra_ref
  16.1 4.2 stack_up.1
  21.1 1.4 vectors.1
  22.5 15.1 %all-gather = bf16[128,512]{1,0:T(8,128)(2,1)S(1)} all-gather(bf16[8,512]{1,0:T(8,128)(2,1)} %vectors.1), channel_id=2, replica_groups=mesh['z'=2,'y'=2,'x'=2,'core'=2] {'z','y','x','core'}, dimensions={0}, use_global_device_ids=true | all-gather | bytes 139264 | tf_op jit(solution)/shard_map/all_gather | solution.py:744
  38.9 8.5 norm.1.own_ref.refs_12_
  50.8 11.7 collective-permute-done.oth_ref
  62.4 82.9 %all-gather.6.cloned.1.call-done.w_ref.refs_4_.refs_5_ = bf16[1152,6912]{1,0:T(8,128)(2,1)} async-done(((bf16[144,6912]{1,0:T(8,128)(2,1)}), bf16[1152,6912]{1,0:T(8,128)(2,1)}) %all-gather.6.cloned.1.call-update) | async-done | bytes 15925264 | tf_op jit(solution)/shard_map/all_gather | solution.py:739
  145.3 92.9 %hidden.4 = (bf16[4096,1152]{1,0:T(8,128)(2,1)}, bf16[4096,2304]{1,0:T(8,128)(2,1)}, f32[1152,3456]{1,0:T(8,128)}, f32[16,1152]{1,0:T(8,128)}) custom-call(bf16[2048,2304]{1,0:T(8,128)(2,1)} %norm.1.own_ref.refs_12_, bf16[2048,2304]{1,0:T(8,128)(2,1)} %collective-permute-done.oth_ref, bf16[1152,6912]{1,0:T(8,128)(2,1)} %all-gather.6.cloned.1.call-done.w_ref.refs_4_.refs_5_, ...), custom_call_target="tpu_custom_call" | custom-call | flops 65000001536 | bytes 70000000 | tf_op jit(solution)/shard_map/hidden/pallas_call | solution.py:422
  238.9 3.1 all-gather.4.cloned.1.call-done.w_ref.refs_3_
  242.0 2.2 slice.194.own_ref
  244.3 5.1 constant_dynamic-slice_fusion.7
  249.4 1.5 collective-permute-start.2
  250.9 1.5 fusion.6
  252.9 1.5 collective-permute-start.10
  254.4 1.6 collective-permute-start.11
  255.9 3.9 constant_dynamic-slice_fusion.4
  259.8 42.3 %collective-permute-done.9 = s32[1,2,512]{2,0,1:T(1,128)S(1)} collective-permute-done((s32[1,2,512]{2,0,1:T(1,128)S(1)}, s32[1,2,512]{2,0,1:T(1,128)S(1)}, u32[]{:S(2)}, u32[]{:S(2)}) %collective-permute-start.9) | collective-permute-done | bytes 4128 | tf_op jit(solution)/shard_map/ppermute | solution.py:716
  302.1 1.4 collective-permute-start.3
  303.6 2.3 collective-permute-start.4
  305.8 1.3 collective-permute-start.6
  307.2 2.1 collective-permute-start.7
  312.3 3.7 fusion
  316.1 1.9 pad_maximum_fusion
  318.0 6.0 unpack.1
  324.0 57.3 %collective-permute-done.3.n2_ref = bf16[1,512,1152]{2,1,0:T(8,128)(2,1)} collective-permute-done((bf16[1,512,1152]{2,1,0:T(8,128)(2,1)}, bf16[1,512,1152]{2,1,0:T(8,128)(2,1)}, u32[]{:S(2)}, u32[]{:S(2)}) %collective-permute-start.3) | collective-permute-done | bytes 1179680 | tf_op jit(solution)/shard_map/ppermute | solution.py:716
  381.3 4.8 collective-permute-done.5.g1_ref
  386.1 68.0 %collective-permute-done.6.g2_ref = bf16[1,512,1152]{2,1,0:T(8,128)(2,1)} collective-permute-done((bf16[1,512,1152]{2,1,0:T(8,128)(2,1)}, bf16[1,512,1152]{2,1,0:T(8,128)(2,1)}, u32[]{:S(2)}, u32[]{:S(2)}) %collective-permute-start.6) | collective-permute-done | bytes 1179680 | tf_op jit(solution)/shard_map/ppermute | solution.py:716
  454.1 1.4 broadcast_in_dim.46.segq_ref
  456.1 84.3 %attn.1.dqkv_ref.o_lo_ref.o_hi_ref = bf16[2048,2560]{1,0:T(8,128)(2,1)} custom-call(s32[1]{0:T(128)} %bitcast.cp_ref, bf16[4,512,2304]{2,1,0:T(8,128)(2,1)} %bitcast.62, bf16[1,512,1152]{2,1,0:T(8,128)(2,1)} %collective-permute-done.2.n1_ref, bf16[1,512,1152]{2,1,0:T(8,128)(2,1)} %collective-permute-done.3.n2_ref, ...), custom_call_target="tpu_custom_call" | custom-call | flops 44999999488 | bytes 40000000 | tf_op jit(solution)/shard_map/attn/pallas_call | solution.py:157
  540.4 23.2 %attn_grad.1 = (f32[8,136,1536]{2,1,0:T(8,128)}, f32[8,136,1536]{2,1,0:T(8,128)}) custom-call(s32[1]{0:T(128)} %bitcast.cp_ref, bf16[4,512,2304]{2,1,0:T(8,128)(2,1)} %bitcast.63, bf16[1,512,1152]{2,1,0:T(8,128)(2,1)} %collective-permute-done.2.n1_ref, bf16[1,512,1152]{2,1,0:T(8,128)(2,1)} %collective-permute-done.3.n2_ref, ...), custom_call_target="tpu_custom_call" | custom-call | flops 12000000000 | bytes 33000000 | tf_op jit(solution)/shard_map/attn_grad/pallas_call | solution.py:540
  565.0 9.7 collective-permute-done.12.refs_1_
  574.7 95.5 %hidden.5 = (bf16[4096,1152]{1,0:T(8,128)(2,1)}, bf16[4096,2304]{1,0:T(8,128)(2,1)}, f32[1152,4992]{1,0:T(8,128)}, f32[16,1152]{1,0:T(8,128)}) custom-call(bf16[2048,2304]{1,0:T(8,128)(2,1)} %norm.1.own_ref.refs_12_, bf16[2048,2304]{1,0:T(8,128)(2,1)} %collective-permute-done.oth_ref, bf16[1152,6912]{1,0:T(8,128)(2,1)} %all-gather.6.cloned.1.call-done.w_ref.refs_4_.refs_5_, ...), custom_call_target="tpu_custom_call" | custom-call | flops 65000001536 | bytes 70000000 | tf_op jit(solution)/shard_map/hidden/pallas_call | solution.py:422
  672.2 94.3 %hidden.3 = (bf16[4096,1152]{1,0:T(8,128)(2,1)}, bf16[4096,2304]{1,0:T(8,128)(2,1)}, f32[4,144,3456]{2,1,0:T(8,128)}, f32[4,144,3456]{2,1,0:T(8,128)}, f32[16,1152]{1,0:T(8,128)}) custom-call(bf16[2048,2304]{1,0:T(8,128)(2,1)} %norm.1.own_ref.refs_12_, bf16[2048,2304]{1,0:T(8,128)(2,1)} %collective-permute-done.oth_ref, ...), custom_call_target="tpu_custom_call" | custom-call | flops 65000001536 | bytes 70000000 | tf_op jit(solution)/shard_map/hidden/pallas_call | solution.py:422
  766.9 27.2 %shard_map.263 = f32[2048,1152]{1,0:T(8,128)} custom-call(bf16[4096,1152]{1,0:T(8,128)(2,1)} %get-tuple-element.74.refs_0_, bf16[4096,1152]{1,0:T(8,128)(2,1)} %get-tuple-element.75.refs_1_, bf16[4096,1152]{1,0:T(8,128)(2,1)} %get-tuple-element.76.refs_2_, bf16[1152,4992]{1,0:T(8,128)(2,1)} %all-gather.4.cloned.1.call-done.w_ref.refs_3_, ...), custom_call_target="tpu_custom_call" | custom-call | flops 16307453952 | bytes 50000000 | tf_op jit(solution)/shard_map/pallas_call | solution.py:589
  794.2 49.4 %shard_map.264 = f32[2048,1152]{1,0:T(8,128)} custom-call(bf16[4096,2304]{1,0:T(8,128)(2,1)} %get-tuple-element.77.refs_0_, bf16[4096,2304]{1,0:T(8,128)(2,1)} %get-tuple-element.78.refs_1_, bf16[4096,2304]{1,0:T(8,128)(2,1)} %get-tuple-element.79.refs_2_, bf16[1152,4992]{1,0:T(8,128)(2,1)} %all-gather.4.cloned.1.call-done.w_ref.refs_3_, ...), custom_call_target="tpu_custom_call" | custom-call | flops 32614907904 | bytes 50000000 | tf_op jit(solution)/shard_map/pallas_call | solution.py:589
  843.9 155.2 %collective-permute-done.18.got_ref = f32[4,144,3456]{2,1,0:T(8,128)} collective-permute-done((f32[4,144,3456]{2,1,0:T(8,128)}, f32[4,144,3456]{2,1,0:T(8,128)}, u32[]{:S(2)}, u32[]{:S(2)}) %collective-permute-start.18) | collective-permute-done | bytes 7962656 | tf_op jit(solution)/shard_map/ppermute | solution.py:703
  999.1 8.4 fold_first.1
  1007.5 1.3 copy-done.2
  1008.8 1.5 collective-permute-start.19
  1010.3 1.5 collective-permute-start.20
  1011.7 41.8 %collective-permute-done.20.got_b_ref = f32[2,144,1664]{2,1,0:T(8,128)S(1)} collective-permute-done((f32[2,144,1664]{2,1,0:T(8,128)S(1)}, f32[2,144,1664]{2,1,0:T(8,128)S(1)}, u32[]{:S(2)}, u32[]{:S(2)}) %collective-permute-start.20) | collective-permute-done | bytes 1916960 | tf_op jit(solution)/shard_map/ppermute | solution.py:703
  1053.5 2.2 collective-permute-done.19.got_a_ref
  1055.7 1.3 copy-done.20
  1057.0 3.3 fold_second.1
  1060.4 1.5 collective-permute-start.21
  1061.9 1.4 collective-permute-start.22
  1063.3 3.4 constant_dynamic-slice_fusion.1
  1067.4 16.4 %collective-permute-done.22.got_b_ref = f32[144,1664]{1,0:T(8,128)S(1)} collective-permute-done((f32[144,1664]{1,0:T(8,128)S(1)}, f32[144,1664]{1,0:T(8,128)S(1)}, u32[]{:S(2)}, u32[]{:S(2)}) %collective-permute-start.22) | collective-permute-done | bytes 958496 | tf_op jit(solution)/shard_map/ppermute | solution.py:703
  1083.8 1.3 collective-permute-start.14
  1087.1 2.3 collective-permute-start.15
  1091.4 3.6 fold_third.1.refs_0_
  1095.0 1.4 slice_select_fusion.2
  1096.4 46.0 %collective-permute-done.13.refs_8_.refs_9_.refs_7_ = bf16[1,512,2560]{2,1,0:T(8,128)(2,1)} collective-permute-done((bf16[1,512,2560]{2,1,0:T(8,128)(2,1)}, bf16[1,512,2560]{2,1,0:T(8,128)(2,1)}, u32[]{:S(2)}, u32[]{:S(2)}) %collective-permute-start.13) | collective-permute-done | bytes 2621472 | tf_op jit(solution)/shard_map/ppermute | solution.py:716
  1142.4 55.1 %collective-permute-done.15.refs_12_.refs_13_.refs_9_ = bf16[1,512,2560]{2,1,0:T(8,128)(2,1)} collective-permute-done((bf16[1,512,2560]{2,1,0:T(8,128)(2,1)}, bf16[1,512,2560]{2,1,0:T(8,128)(2,1)}, u32[]{:S(2)}, u32[]{:S(2)}) %collective-permute-start.15) | collective-permute-done | bytes 2621472 | tf_op jit(solution)/shard_map/ppermute | solution.py:716
  1197.5 35.2 %shard_map.265 = bf16[2048,1152]{1,0:T(8,128)(2,1)} custom-call(s32[1]{0:T(128)} %bitcast.cp_ref, bf16[4096,1152]{1,0:T(8,128)(2,1)} %get-tuple-element.74.refs_0_, bf16[4096,1152]{1,0:T(8,128)(2,1)} %get-tuple-element.75.refs_1_, bf16[4096,1152]{1,0:T(8,128)(2,1)} %get-tuple-element.76.refs_2_, ...), custom_call_target="tpu_custom_call" | custom-call | flops 21139292160 | bytes 80000000 | tf_op jit(solution)/shard_map/pallas_call | solution.py:651
  1232.7 62.9 %shard_map.266 = (bf16[2048,1152]{1,0:T(8,128)(2,1)}, f32[16,1152]{1,0:T(8,128)}) custom-call(s32[1]{0:T(128)} %bitcast.cp_ref, bf16[4096,2304]{1,0:T(8,128)(2,1)} %get-tuple-element.77.refs_0_, bf16[4096,2304]{1,0:T(8,128)(2,1)} %get-tuple-element.78.refs_1_, bf16[4096,2304]{1,0:T(8,128)(2,1)} %get-tuple-element.79.refs_2_, ...), custom_call_target="tpu_custom_call" | custom-call | flops 37446746112 | bytes 80000000 | tf_op jit(solution)/shard_map/pallas_call | solution.py:651
  1296.6 1.4 slice_select_fusion.1
  1298.0 1.4 slice_select_fusion
  1300.2 32.1 %psum.7 = f32[16,1008]{1,0:T(8,128)S(1)} all-reduce(f32[16,1008]{1,0:T(8,128)S(1)} %pad_maximum_fusion.3), channel_id=1, replica_groups=mesh['z'=2,'y'=2,'x'=2,'core'=2] {'z','y','x','core'}, use_global_device_ids=true, to_apply=%region_4.5 | all-reduce | flops 16128 | bytes 129024 | tf_op jit(solution)/shard_map/psum | solution.py:819
  1333.5 1.7 slice.203
  1335.2 1.7 slice.206
  1336.9 1.6 fusion.11
  1339.5 7.8 join_up.1
  (141 shorter events, 25.9 us)
Async XLA Ops:
  7.2 138.2 %all-gather.6.cloned.1.call-start = ((), (), s32[]{:S(2)}) async-start(), calls=%async_computation.3 | async-start | bytes 17915904 | tf_op jit(solution)/shard_map/all_gather | solution.py:739
  12.0 3.2 collective-permute-start.1
  15.2 0.9 copy-start.5
  20.3 221.7 %all-gather.4.cloned.1.call-start = ((), (), s32[]{:S(2)}) async-start(), calls=%async_computation.2 | async-start | bytes 12939264 | tf_op jit(solution)/shard_map/all_gather | solution.py:739
  21.1 1275.5 %reduce-scatter.5.cloned.1.call-start = ((), (), s32[]{:S(2)}) async-start(), calls=%async_computation.5 | async-start | bytes 17915904 | tf_op jit(solution)/shard_map/reduce_scatter | solution.py:778
  47.4 15.0 %collective-permute-start = (bf16[2048,2304]{1,0:T(8,128)(2,1)}, bf16[2048,2304]{1,0:T(8,128)(2,1)}, u32[]{:S(2)}, u32[]{:S(2)}) collective-permute-start(bf16[2048,2304]{1,0:T(8,128)(2,1)} %norm.1.own_ref.refs_12_), channel_id=1, source_target_pairs={{0,1},{1,0},{2,3},{3,2},{4,5},{5,4},{6,7},{7,6},{8,9},{9,8},{10,11... | collective-permute-start | bytes 28311560 | tf_op jit(solution)/shard_map/ppermute | solution.py:699
  238.3 1059.7 %reduce-scatter.3.cloned.1.call-start = ((), (), s32[]{:S(2)}) async-start(), calls=%async_computation.4 | async-start | bytes 25878528 | tf_op jit(solution)/shard_map/reduce_scatter | solution.py:778
  244.3 5.2 copy-start.3
  244.3 62.9 %collective-permute-start.8 = (bf16[1152,1536]{1,0:T(8,128)(2,1)S(1)}, bf16[1152,1536]{1,0:T(8,128)(2,1)}, u32[]{:S(2)}, u32[]{:S(2)}) collective-permute-start(bf16[1152,1536]{1,0:T(8,128)(2,1)S(1)} %slice.194.own_ref), channel_id=1, source_target_pairs={{0,1},{1,0},{2,3},{3,2},{4,5},{5,4},{6,7},{7,6},{8,9},{9,8},{10,11... | collective-permute-start | bytes 10616840 | tf_op jit(solution)/shard_map/ppermute | solution.py:699
  249.4 56.4 %collective-permute-start.2 = (bf16[1,512,1152]{2,1,0:T(8,128)(2,1)}, bf16[1,512,1152]{2,1,0:T(8,128)(2,1)}, u32[]{:S(2)}, u32[]{:S(2)}) collective-permute-start(bf16[1,512,1152]{2,1,0:T(8,128)(2,1)} %get-tuple-element.113), channel_id=1, source_target_pairs={{0,4},{4,0},{8,12},{12,8},{1,5},{5,1},{9,13},{13,9},{2,6},{6,2},{1... | collective-permute-start | bytes 3538952 | tf_op jit(solution)/shard_map/ppermute | solution.py:716
  252.4 49.7 %collective-permute-start.9 = (s32[1,2,512]{2,0,1:T(1,128)S(1)}, s32[1,2,512]{2,0,1:T(1,128)S(1)}, u32[]{:S(2)}, u32[]{:S(2)}) collective-permute-start(s32[1,2,512]{2,0,1:T(1,128)S(1)} %get-tuple-element.134), channel_id=1, source_target_pairs={{0,4},{4,0},{8,12},{12,8},{1,5},{5,1},{9,13},{13,9},{2,6},{6,2},{1... | collective-permute-start | bytes 12296 | tf_op jit(solution)/shard_map/ppermute | solution.py:716
  252.9 50.7 %collective-permute-start.10 = (s32[1,2,512]{2,0,1:T(1,128)S(1)}, s32[1,2,512]{2,0,1:T(1,128)S(1)}, u32[]{:S(2)}, u32[]{:S(2)}) collective-permute-start(s32[1,2,512]{2,0,1:T(1,128)S(1)} %get-tuple-element.135), channel_id=1, source_target_pairs={{0,8},{4,12},{8,0},{12,4},{1,9},{5,13},{9,1},{13,5},{2,10},{6,14},... | collective-permute-start | bytes 12296 | tf_op jit(solution)/shard_map/ppermute | solution.py:716
  254.4 51.5 %collective-permute-start.11 = (s32[1,2,512]{2,0,1:T(1,128)S(1)}, s32[1,2,512]{2,0,1:T(1,128)S(1)}, u32[]{:S(2)}, u32[]{:S(2)}) collective-permute-start(s32[1,2,512]{2,0,1:T(1,128)S(1)} %get-tuple-element.132), channel_id=1, source_target_pairs={{0,12},{4,8},{8,4},{12,0},{1,13},{5,9},{9,5},{13,1},{2,14},{6,10},... | collective-permute-start | bytes 12296 | tf_op jit(solution)/shard_map/ppermute | solution.py:716
  302.1 7.2 copy-start.16
  302.1 79.2 %collective-permute-start.3 = (bf16[1,512,1152]{2,1,0:T(8,128)(2,1)}, bf16[1,512,1152]{2,1,0:T(8,128)(2,1)}, u32[]{:S(2)}, u32[]{:S(2)}) collective-permute-start(bf16[1,512,1152]{2,1,0:T(8,128)(2,1)} %get-tuple-element.112), channel_id=1, source_target_pairs={{0,8},{4,12},{8,0},{12,4},{1,9},{5,13},{9,1},{13,5},{2,10},{6,14},... | collective-permute-start | bytes 3538952 | tf_op jit(solution)/shard_map/ppermute | solution.py:716
  303.6 5.8 copy-start.17
  303.6 77.7 %collective-permute-start.4 = (bf16[1,512,1152]{2,1,0:T(8,128)(2,1)}, bf16[1,512,1152]{2,1,0:T(8,128)(2,1)}, u32[]{:S(2)}, u32[]{:S(2)}) collective-permute-start(bf16[1,512,1152]{2,1,0:T(8,128)(2,1)} %get-tuple-element.111), channel_id=1, source_target_pairs={{0,12},{4,8},{8,4},{12,0},{1,13},{5,9},{9,5},{13,1},{2,14},{6,10},... | collective-permute-start | bytes 3538952 | tf_op jit(solution)/shard_map/ppermute | solution.py:716
  305.8 3.5 copy-start.18
  305.8 80.3 %collective-permute-start.5 = (bf16[1,512,1152]{2,1,0:T(8,128)(2,1)}, bf16[1,512,1152]{2,1,0:T(8,128)(2,1)}, u32[]{:S(2)}, u32[]{:S(2)}) collective-permute-start(bf16[1,512,1152]{2,1,0:T(8,128)(2,1)} %get-tuple-element.115), channel_id=1, source_target_pairs={{0,4},{4,0},{8,12},{12,8},{1,5},{5,1},{9,13},{13,9},{2,6},{6,2},{1... | collective-permute-start | bytes 3538952 | tf_op jit(solution)/shard_map/ppermute | solution.py:716
  305.8 148.3 %collective-permute-start.6 = (bf16[1,512,1152]{2,1,0:T(8,128)(2,1)}, bf16[1,512,1152]{2,1,0:T(8,128)(2,1)}, u32[]{:S(2)}, u32[]{:S(2)}) collective-permute-start(bf16[1,512,1152]{2,1,0:T(8,128)(2,1)} %get-tuple-element.116), channel_id=1, source_target_pairs={{0,8},{4,12},{8,0},{12,4},{1,9},{5,13},{9,1},{13,5},{2,10},{6,14},... | collective-permute-start | bytes 3538952 | tf_op jit(solution)/shard_map/ppermute | solution.py:716
  307.2 146.9 %collective-permute-start.7 = (bf16[1,512,1152]{2,1,0:T(8,128)(2,1)}, bf16[1,512,1152]{2,1,0:T(8,128)(2,1)S(1)}, u32[]{:S(2)}, u32[]{:S(2)}) collective-permute-start(bf16[1,512,1152]{2,1,0:T(8,128)(2,1)} %get-tuple-element.114), channel_id=1, source_target_pairs={{0,12},{4,8},{8,4},{12,0},{1,13},{5,9},{9,5},{13,1},{2,14},{6,10},... | collective-permute-start | bytes 3538952 | tf_op jit(solution)/shard_map/ppermute | solution.py:716
  454.1 2.0 copy-start.4
  563.6 11.1 collective-permute-start.12
  670.1 0.7 copy-start.14
  670.1 1.4 copy-start.15
  766.6 232.5 %collective-permute-start.18 = (f32[4,144,3456]{2,1,0:T(8,128)}, f32[4,144,3456]{2,1,0:T(8,128)}, u32[]{:S(2)}, u32[]{:S(2)}) collective-permute-start(f32[4,144,3456]{2,1,0:T(8,128)} %get-tuple-element.87), channel_id=1, source_target_pairs={{0,2},{2,0},{1,3},{3,1},{4,6},{6,4},{5,7},{7,5},{8,10},{10,8},{9,1... | collective-permute-start | bytes 23887880 | tf_op jit(solution)/shard_map/ppermute | solution.py:703
  794.1 403.4 %collective-permute-start.16 = (f32[2048,1152]{1,0:T(8,128)}, f32[2048,1152]{1,0:T(8,128)}, u32[]{:S(2)}, u32[]{:S(2)}) collective-permute-start(f32[2048,1152]{1,0:T(8,128)} %shard_map.263), channel_id=1, source_target_pairs={{0,1},{1,0},{2,3},{3,2},{4,5},{5,4},{6,7},{7,6},{8,9},{9,8},{10,11... | collective-permute-start | bytes 28311560 | tf_op jit(solution)/shard_map/ppermute | solution.py:699
  843.6 389.1 %collective-permute-start.17 = (f32[2048,1152]{1,0:T(8,128)}, f32[2048,1152]{1,0:T(8,128)}, u32[]{:S(2)}, u32[]{:S(2)}) collective-permute-start(f32[2048,1152]{1,0:T(8,128)} %shard_map.264), channel_id=1, source_target_pairs={{0,1},{1,0},{2,3},{3,2},{4,5},{5,4},{6,7},{7,6},{8,9},{9,8},{10,11... | collective-permute-start | bytes 28311560 | tf_op jit(solution)/shard_map/ppermute | solution.py:699
  999.1 64.2 %slice-start = ((s8[10485760]{0:T(1024)(128)(4,1)}), s8[4194304]{0:T(1024)(128)(4,1)S(1)}, s32[]{:S(2)}) async-start(s8[10485760]{0:T(1024)(128)(4,1)} %bitcast.58), calls=%async_computation.6 | async-start | bytes 8388608
  999.1 64.2 %slice-start.1 = ((s8[10485760]{0:T(1024)(128)(4,1)}), s8[2097152]{0:T(1024)(128)(4,1)S(1)}, s32[]{:S(2)}) async-start(s8[10485760]{0:T(1024)(128)(4,1)} %bitcast.58), calls=%async_computation.7 | async-start | bytes 4194304
  1007.5 1.3 copy-start.2
  1008.8 46.9 %collective-permute-start.19 = (f32[2,144,1792]{2,1,0:T(8,128)}, f32[2,144,1792]{2,1,0:T(8,128)S(1)}, u32[]{:S(2)}, u32[]{:S(2)}) collective-permute-start(f32[2,144,1792]{2,1,0:T(8,128)} %get-tuple-element.89), channel_id=1, source_target_pairs={{0,8},{8,0},{1,9},{9,1},{2,10},{10,2},{3,11},{11,3},{4,12},{12,4},... | collective-permute-start | bytes 6193160 | tf_op jit(solution)/shard_map/ppermute | solution.py:703
  1010.3 43.3 %collective-permute-start.20 = (f32[2,144,1664]{2,1,0:T(8,128)S(1)}, f32[2,144,1664]{2,1,0:T(8,128)S(1)}, u32[]{:S(2)}, u32[]{:S(2)}) collective-permute-start(f32[2,144,1664]{2,1,0:T(8,128)S(1)} %get-tuple-element.91), channel_id=1, source_target_pairs={{0,4},{4,0},{1,5},{5,1},{2,6},{6,2},{3,7},{7,3},{8,12},{12,8},{9,1... | collective-permute-start | bytes 5750792 | tf_op jit(solution)/shard_map/ppermute | solution.py:703
  1053.5 2.2 copy-start.21
  1055.7 1.3 copy-start.20
  1057.0 6.2 slice-start.2
  1060.4 6.4 copy-start
  1060.4 6.4 copy-start.1
  1060.4 25.7 %collective-permute-start.21 = (f32[144,1792]{1,0:T(8,128)S(1)}, f32[144,1792]{1,0:T(8,128)S(1)}, u32[]{:S(2)}, u32[]{:S(2)}) collective-permute-start(f32[144,1792]{1,0:T(8,128)S(1)} %get-tuple-element.93), channel_id=1, source_target_pairs={{0,4},{4,0},{1,5},{5,1},{2,6},{6,2},{3,7},{7,3},{8,12},{12,8},{9,1... | collective-permute-start | bytes 3096584 | tf_op jit(solution)/shard_map/ppermute | solution.py:703
  1061.9 21.9 %collective-permute-start.22 = (f32[144,1664]{1,0:T(8,128)S(1)}, f32[144,1664]{1,0:T(8,128)S(1)}, u32[]{:S(2)}, u32[]{:S(2)}) collective-permute-start(f32[144,1664]{1,0:T(8,128)S(1)} %get-tuple-element.95), channel_id=1, source_target_pairs={{0,8},{8,0},{1,9},{9,1},{2,10},{10,2},{3,11},{11,3},{4,12},{12,4},... | collective-permute-start | bytes 2875400 | tf_op jit(solution)/shard_map/ppermute | solution.py:703
  1063.3 26.1 %copy-start.12 = (bf16[16,1,72]{2,1,0:T(2,128)(2,1)S(1)}, bf16[16,1,72]{2,1,0:T(2,128)(2,1)}, u32[]{:S(2)}) copy-start(bf16[16,1,72]{2,1,0:T(2,128)(2,1)} %get-tuple-element.119) | copy-start | bytes 6916
  1063.3 26.1 %copy-start.13 = (bf16[16,1,72]{2,1,0:T(2,128)(2,1)S(1)}, bf16[16,1,72]{2,1,0:T(2,128)(2,1)}, u32[]{:S(2)}) copy-start(bf16[16,1,72]{2,1,0:T(2,128)(2,1)} %get-tuple-element.121) | copy-start | bytes 6916
  1063.3 26.7 %copy-start.11 = (f32[16,1152]{1,0:T(8,128)S(1)}, f32[16,1152]{1,0:T(8,128)}, u32[]{:S(2)}) copy-start(f32[16,1152]{1,0:T(8,128)} %get-tuple-element.82) | copy-start | bytes 221188
  1063.3 26.9 %copy-start.9 = (f32[16,1152]{1,0:T(8,128)S(1)}, f32[16,1152]{1,0:T(8,128)}, u32[]{:S(2)}) copy-start(f32[16,1152]{1,0:T(8,128)} %get-tuple-element.83) | copy-start | bytes 221188
  1063.3 27.0 %copy-start.10 = (f32[16,1152]{1,0:T(8,128)S(1)}, f32[16,1152]{1,0:T(8,128)}, u32[]{:S(2)}) copy-start(f32[16,1152]{1,0:T(8,128)} %get-tuple-element.84) | copy-start | bytes 221188
  1066.7 75.6 %collective-permute-start.13 = (bf16[1,512,2560]{2,1,0:T(8,128)(2,1)}, bf16[1,512,2560]{2,1,0:T(8,128)(2,1)}, u32[]{:S(2)}, u32[]{:S(2)}) collective-permute-start(bf16[1,512,2560]{2,1,0:T(8,128)(2,1)} %get-tuple-element.110), channel_id=1, source_target_pairs={{0,4},{4,0},{8,12},{12,8},{1,5},{5,1},{9,13},{13,9},{2,6},{6,2},{1... | collective-permute-start | bytes 7864328 | tf_op jit(solution)/shard_map/ppermute | solution.py:716
  1083.8 3.3 copy-start.23
  1083.8 58.6 %collective-permute-start.14 = (bf16[1,512,2560]{2,1,0:T(8,128)(2,1)}, bf16[1,512,2560]{2,1,0:T(8,128)(2,1)}, u32[]{:S(2)}, u32[]{:S(2)}) collective-permute-start(bf16[1,512,2560]{2,1,0:T(8,128)(2,1)} %get-tuple-element.109), channel_id=1, source_target_pairs={{0,8},{4,12},{8,0},{12,4},{1,9},{5,13},{9,1},{13,5},{2,10},{6,14},... | collective-permute-start | bytes 7864328 | tf_op jit(solution)/shard_map/ppermute | solution.py:716
  1086.1 1.0 copy-start.22
  1087.1 110.4 %collective-permute-start.15 = (bf16[1,512,2560]{2,1,0:T(8,128)(2,1)}, bf16[1,512,2560]{2,1,0:T(8,128)(2,1)}, u32[]{:S(2)}, u32[]{:S(2)}) collective-permute-start(bf16[1,512,2560]{2,1,0:T(8,128)(2,1)} %get-tuple-element.108), channel_id=1, source_target_pairs={{0,12},{4,8},{8,4},{12,0},{1,13},{5,9},{9,5},{13,1},{2,14},{6,10},... | collective-permute-start | bytes 7864328 | tf_op jit(solution)/shard_map/ppermute | solution.py:716
  1142.4 196.1 %collective-permute-start.23 = (f32[72,2304]{1,0:T(8,128)S(1)}, f32[72,2304]{1,0:T(8,128)S(1)}, u32[]{:S(2)}, u32[]{:S(2)}) collective-permute-start(f32[72,2304]{1,0:T(8,128)S(1)} %slice_select_fusion.2), channel_id=1, source_target_pairs={{0,1},{1,0},{2,3},{3,2},{4,5},{5,4},{6,7},{7,6},{8,9},{9,8},{10,11... | collective-permute-start | bytes 1990664 | tf_op jit(solution)/shard_map/ppermute | solution.py:699
  1295.6 4.5 copy-start.8
  1298.0 40.5 %collective-permute-start.24 = (f32[72,2304]{1,0:T(8,128)S(1)}, f32[72,2304]{1,0:T(8,128)S(1)}, u32[]{:S(2)}, u32[]{:S(2)}) collective-permute-start(f32[72,2304]{1,0:T(8,128)S(1)} %slice_select_fusion.1), channel_id=1, source_target_pairs={{0,1},{1,0},{2,3},{3,2},{4,5},{5,4},{6,7},{7,6},{8,9},{9,8},{10,11... | collective-permute-start | bytes 1990664 | tf_op jit(solution)/shard_map/ppermute | solution.py:699
  1299.4 39.1 %collective-permute-start.25 = (f32[72,2304]{1,0:T(8,128)S(1)}, f32[72,2304]{1,0:T(8,128)}, u32[]{:S(2)}, u32[]{:S(2)}) collective-permute-start(f32[72,2304]{1,0:T(8,128)S(1)} %slice_select_fusion), channel_id=1, source_target_pairs={{0,1},{1,0},{2,3},{3,2},{4,5},{5,4},{6,7},{7,6},{8,9},{9,8},{10,11... | collective-permute-start | bytes 1990664 | tf_op jit(solution)/shard_map/ppermute | solution.py:699
  1332.8 14.5 %copy-start.19 = (f32[72]{0:T(128)}, f32[72]{0:T(128)S(1)}, u32[]{:S(2)}) copy-start(f32[72]{0:T(128)S(1)} %get-tuple-element.170) | copy-start | bytes 868
  1338.4 0.9 copy-start.6
  1338.4 1.1 copy-start.7
Sparse Core Ops, SparseCore 0:
  20.5 124.8 all-gather.5
  148.1 93.9 all-gather.3
  246.3 236.2 reduce-scatter.4
  670.3 227.9 reduce-scatter.2

commit v3 on v2

--- a/solution.py
+++ b/solution.py
@@ -320,6 +320,20 @@
         acc_s[...] = jnp.zeros_like(acc_s)
         db_ref[...] = jnp.zeros_like(db_ref)
 
+    def leave(which, act):
+        cols = slice(0, 2 * d_model) if which == 0 else slice(2 * d_model, 3 * d_model)
+        sem = sems.at[(0, 3)[which]]
+        if mode != 'halves':
+            pl.when(step == last)(lambda: act(pltpu.make_async_copy(acc_s.at[:, cols], dw_ref.at[:, cols], sem)))
+            return
+        x_index = lax.axis_index('x')
+        block = d_model // 8
+        for chip in range(8):
+            for ref, flip in zip(dw_refs, (0, 1)):
+                @pl.when((step == last) & ((x_index ^ flip) == chip % 2))
+                def _():
+                    act(pltpu.make_async_copy(acc_s.at[chip * block:(chip + 1) * block, cols], ref.at[chip // 2, :, cols], sem))
+
     n_sub = 2
     sub = rows // n_sub
     w12 = w_ref[:, :2 * d_model]
@@ -355,6 +369,8 @@
         db_ref[:8, :] += s1
         db_ref[8:, :] += s2
         acc_s[:, :2 * d_model] += dot_tn(ng_s[sl, :d_model], dh_ref[sl, :])
+        if i == n_sub - 1:
+            leave(0, lambda copy: copy.start())
         acc_s[:, 2 * d_model:] += dot_tn(act_ref[sl, :], ng_s[sl, d_model:])
 
     if extra_refs:
@@ -380,25 +396,9 @@
             side_copy(1 - slot, step - 1).wait()
             side_copy(slot, step).wait()
 
-    @pl.when(step == last)
-    def _():
-        if mode != 'halves':
-            copy = pltpu.make_async_copy(acc_s, dw_ref.at[:, :3 * d_model], sems.at[0])
-            copy.start()
-            copy.wait()
-            return
-        x_index = lax.axis_index('x')
-        block = d_model // 8
-
-        def each(act):
-            for chip in range(8):
-                for ref, flip in zip(dw_refs, (0, 1)):
-                    @pl.when((x_index ^ flip) == chip % 2)
-                    def _():
-                        act(pltpu.make_async_copy(acc_s.at[chip * block:(chip + 1) * block, :], ref.at[chip // 2], sems.at[0]))
-
-        each(lambda copy: copy.start())
-        each(lambda copy: copy.wait())
+    leave(1, lambda copy: copy.start())
+    leave(0, lambda copy: copy.wait())
+    leave(1, lambda copy: copy.wait())
 
 
 def hidden_part(ng_own, ng_oth, weight, b1, b2, extra=(), halves=False):
@@ -427,7 +427,7 @@
         out_shape=[jax.ShapeDtypeStruct((2 * t_len, d_model), BF16), jax.ShapeDtypeStruct((2 * t_len, 2 * d_model), BF16),
                    *grads, jax.ShapeDtypeStruct((16, d_model), F32)],
         scratch_shapes=[pltpu.VMEM((rows, 2 * d_model), F32), pltpu.VMEM((rows, d_model), F32), pltpu.VMEM((rows, both), BF16),
-                        pltpu.VMEM((d_model, 3 * d_model), F32), pltpu.VMEM(side, F32), pltpu.SemaphoreType.DMA((3,))],
+                        pltpu.VMEM((d_model, 3 * d_model), F32), pltpu.VMEM(side, F32), pltpu.SemaphoreType.DMA((4,))],
         compiler_params=pltpu.CompilerParams(vmem_limit_bytes=63 * 1024 * 1024, dimension_semantics=('arbitrary',)),
         cost_estimate=pl.CostEstimate(flops=65_000_000_000, bytes_accessed=70_000_000, transcendentals=4_700_000),
         name='hidden',
@@ -554,42 +554,92 @@
     )(cp_index[None], ng_blocks, *n_got, *g_got, od_seq, od_seq, od_seq)
 
 
-def fwd_product(act_refs, w_refs):
-    out = dot_nn(act_refs[0][...], w_refs[0][...])
-    for act_ref, w_ref in zip(act_refs[1:], w_refs[1:]):
-        out = out + dot_nn(act_ref[...], w_ref[...])
+def small_kernel(in_ref, out_ref, got_s, send_sems, recv_sems):
+    at = [lax.axis_index(axis) for axis in ALL_AXES]
+    me = ((at[0] * 2 + at[1]) * 2 + at[2]) * 2 + at[3]
+
+    def peer(flip):
+        return tuple(index ^ ((flip >> (3 - i)) & 1) for i, index in enumerate(at))
+
+    barrier = pltpu.get_barrier_semaphore()
+    for flip in range(1, 16):
+        pl.semaphore_signal(barrier, inc=1, device_id=peer(flip), device_id_type=pl.DeviceIdType.MESH)
+    pl.semaphore_wait(barrier, 15)
+    copies = []
+    for flip in range(1, 16):
+        copies.append(pltpu.make_async_remote_copy(
+            src_ref=in_ref.at[me ^ flip], dst_ref=got_s.at[flip], send_sem=send_sems.at[flip], recv_sem=recv_sems.at[flip],
+            device_id=peer(flip), device_id_type=pl.DeviceIdType.MESH))
+        copies[-1].start()
+    for copy in copies:
+        copy.wait()
+    total = in_ref[me]
+    for flip in range(1, 16):
+        total = total + got_s[flip]
+    out_ref[...] = total
+
+
+def small_sum(values):
+    return pl.pallas_call(
+        small_kernel, out_shape=jax.ShapeDtypeStruct(values.shape[1:], F32), name='small_sum',
+        in_specs=[pl.BlockSpec(memory_space=pltpu.VMEM)], out_specs=pl.BlockSpec(memory_space=pltpu.VMEM),
+        scratch_shapes=[pltpu.VMEM(values.shape, F32), pltpu.SemaphoreType.DMA((16,)), pltpu.SemaphoreType.DMA((16,))],
+        compiler_params=pltpu.CompilerParams(collective_id=0, has_side_effects=True),
+        cost_estimate=pl.CostEstimate(flops=8_000_000_000, bytes_accessed=130_000, transcendentals=0),
+    )(values)
+
+
+def fetch_weights(w_refs, cols, w_s, sems):
+    first = pl.program_id(0) == 0
+    copies = [pltpu.make_async_copy(ref.at[:, at:at + w_s.shape[2]], w_s.at[i], sems.at[i]) for i, (ref, at) in enumerate(zip(w_refs, cols))]
+    for copy in copies:
+        pl.when(first)(copy.start)
+    return lambda i: pl.when(first)(copies[i].wait)
+
+
+def fwd_product(act_refs, w_s, ready):
+    out = None
+    for i, act_ref in enumerate(act_refs):
+        ready(i)
+        part = dot_nn(act_ref[...], w_s[i])
+        out = part if out is None else out + part
     return out
 
 
-def bwd_product(dh_refs, w_refs):
-    out = dot_nt(dh_refs[0][...], w_refs[0][:, :dh_refs[0].shape[1]])
-    for dh_ref, w_ref in zip(dh_refs[1:], w_refs[1:]):
-        out = out + dot_nt(dh_ref[...], w_ref[:, :dh_ref.shape[1]])
+def bwd_product(dh_refs, w_s, ready):
+    out = None
+    for i, dh_ref in enumerate(dh_refs):
+        ready(i)
+        part = dot_nt(dh_ref[...], w_s[i])
+        out = part if out is None else out + part
     return out
 
 
-def other_kernel(product, *refs):
-    refs[-1][...] = product(refs[:N_PART], refs[N_PART:2 * N_PART])
+def other_kernel(product, cols, *refs):
+    out_ref, w_s, sems = refs[-3:]
+    out_ref[...] = product(refs[:N_PART], w_s, fetch_weights(refs[N_PART:2 * N_PART], cols, w_s, sems))
 
 
 OUT_ROWS = 256
 
 
-def out_specs_of(width, weights, w_width, w_off, first_block):
+def out_specs_of(width, first_block):
     tile = pl.BlockSpec((OUT_ROWS, width), lambda i, *_: (i + first_block, 0))
-    specs = [tile] * N_PART
-    for array, col in weights:
-        specs.append(pl.BlockSpec((array.shape[0], w_width), lambda i, *_, at=w_off(col): (0, at), pipeline_mode=pl.Buffered(1)))
-    return specs
+    return [tile] * N_PART + [pl.BlockSpec(memory_space=pl.ANY)] * N_PART
+
+
+def weight_scratch(weights, w_width):
+    return [pltpu.VMEM((N_PART, weights[0][0].shape[0], w_width), BF16), pltpu.SemaphoreType.DMA((N_PART,))]
 
 
 def out_other(parts, weights, product, w_width, w_off):
     t_len, width = parts[0].shape[0] // 2, parts[0].shape[1]
     d_model = weights[0][0].shape[0]
     return pl.pallas_call(
-        functools.partial(other_kernel, product),
+        functools.partial(other_kernel, product, [w_off(col) for _, col in weights]),
         grid=(t_len // OUT_ROWS,),
-        in_specs=out_specs_of(width, weights, w_width, w_off, t_len // OUT_ROWS),
+        scratch_shapes=weight_scratch(weights, w_width),
+        in_specs=out_specs_of(width, t_len // OUT_ROWS),
         out_specs=pl.BlockSpec((OUT_ROWS, d_model), lambda i: (i, 0)),
         out_shape=jax.ShapeDtypeStruct((t_len, d_model), F32),
         compiler_params=pltpu.CompilerParams(vmem_limit_bytes=60 * 1024 * 1024, dimension_semantics=('arbitrary',)),
@@ -597,9 +647,10 @@
     )(*parts, *[array for array, _ in weights])
 
 
-def fwd_own_kernel(cp_ref, *refs):
+def fwd_own_kernel(cols, cp_ref, *refs):
     o_refs = refs[2 * N_PART:2 * N_PART + 8]
-    wo_ref, x_ref, got_ref, bias_ref, out_ref, o_s = refs[2 * N_PART + 8:]
+    wo_ref, x_ref, got_ref, bias_ref, out_ref, o_s, w_s, sems = refs[2 * N_PART + 8:]
+    ready = fetch_weights(refs[N_PART:2 * N_PART], cols, w_s, sems)
     flip = (pl.program_id(0) // 2) ^ cp_ref[0]
     half = o_s.shape[1] // 2
     for i in range(4):
@@ -607,13 +658,14 @@
         def _():
             o_s[:, :half] = o_refs[2 * i][0]
             o_s[:, half:] = o_refs[2 * i + 1][0]
-    out = fwd_product(refs[:N_PART], refs[N_PART:2 * N_PART]) + dot_nn(o_s[...], wo_ref[...])
+    out = dot_nn(o_s[...], wo_ref[...]) + fwd_product(refs[:N_PART], w_s, ready)
     out_ref[...] = (x_ref[...].astype(F32) + out + got_ref[...] + bias_ref[...]).astype(BF16)
 
 
-def bwd_own_kernel(cp_ref, *refs):
+def bwd_own_kernel(cols, cp_ref, *refs):
     d_refs = refs[2 * N_PART:2 * N_PART + 4]
-    wqkv_ref, x_ref, g_ref, got_ref, scale_ref, d_x_ref, sums_ref, d_s = refs[2 * N_PART + 4:]
+    wqkv_ref, x_ref, g_ref, got_ref, scale_ref, d_x_ref, sums_ref, d_s, w_s, sems = refs[2 * N_PART + 4:]
+    ready = fetch_weights(refs[N_PART:2 * N_PART], cols, w_s, sems)
     flip = (pl.program_id(0) // 2) ^ cp_ref[0]
     for i in range(4):
         @pl.when(flip == i)
@@ -624,7 +676,7 @@
     def _():
         sums_ref[...] = jnp.zeros_like(sums_ref)
 
-    d_n = bwd_product(refs[:N_PART], refs[N_PART:2 * N_PART]) + dot_nt(d_s[...], wqkv_ref[...]) + got_ref[...]
+    d_n = dot_nt(d_s[...], wqkv_ref[...]) + got_ref[...] + bwd_product(refs[:N_PART], w_s, ready)
     x_f = x_ref[...].astype(F32)
     g_f = g_ref[...].astype(F32)
     inv = lax.rsqrt(jnp.mean(x_f * x_f, axis=1, keepdims=True) + 1e-6)
@@ -639,7 +691,7 @@
 
 def own_call(kernel, cp_index, parts, weights, w_width, w_off, od_blocks, od_got, od_cols, od_width, rest, rest_specs, out_specs, out_shape, scratch):
     t_len, width = parts[0].shape[0] // 2, parts[0].shape[1]
-    specs = out_specs_of(width, weights, w_width, w_off, 0)
+    specs = out_specs_of(width, 0)
     args = list(parts) + [array for array, _ in weights]
     for i, source in enumerate([od_blocks] + od_got):
         for col in od_cols:
@@ -649,9 +701,9 @@
                 specs.append(pl.BlockSpec((1, OUT_ROWS, od_width), lambda j, cp, col=col, i=i: (0, jnp.clip(j - 2 * (cp[0] ^ i), 0, 1), col)))
             args.append(source)
     return pl.pallas_call(
-        kernel,
+        functools.partial(kernel, [w_off(col) for _, col in weights]),
         grid_spec=pltpu.PrefetchScalarGridSpec(
-            num_scalar_prefetch=1, grid=(t_len // OUT_ROWS,), in_specs=specs + rest_specs, out_specs=out_specs, scratch_shapes=scratch),
+            num_scalar_prefetch=1, grid=(t_len // OUT_ROWS,), in_specs=specs + rest_specs, out_specs=out_specs, scratch_shapes=scratch + weight_scratch(weights, w_width)),
         out_shape=out_shape,
         compiler_params=pltpu.CompilerParams(vmem_limit_bytes=62 * 1024 * 1024, dimension_semantics=('arbitrary',)),
         cost_estimate=pl.CostEstimate(flops=2 * t_len * weights[0][0].shape[0] * (width * N_PART + 1024), bytes_accessed=80_000_000, transcendentals=0),
@@ -792,17 +844,17 @@
         od_got = send_blocks(od_blocks, cp_index)
         third(2, ng_own, (d_keep, swap_core(d_send)))
 
-        wd_off = lambda col: 3 * col + 2
-        w12_off = lambda col: col
+        wd_off = lambda col: (3 * col + 2) * d_model
+        w12_off = lambda col: 3 * col * d_model
         tile = lambda width, col=0: pl.BlockSpec((OUT_ROWS, width), lambda i, *_: (i, col))
         full = lambda a: pl.BlockSpec(a.shape, lambda i, *_: (0, 0), pipeline_mode=pl.Buffered(1))
         out_oth = out_other(acts, weights, fwd_product, d_model, wd_off)
-        dn_oth = out_other(after(tuple(dhs), out_oth), weights, bwd_product, 3 * d_model, w12_off)
+        dn_oth = out_other(after(tuple(dhs), out_oth), weights, bwd_product, 2 * d_model, w12_off)
         bias_f = bo_f + bd_f
         x_out = own_call(fwd_own_kernel, cp_index, after(tuple(acts), dn_oth), weights, d_model, wd_off, od_blocks, od_got, (3, 4), 512,
                          [wo, x_loc, swap_core(out_oth), bias_f], [full(wo), tile(d_model), tile(d_model), full(bias_f)],
                          tile(d_model), jax.ShapeDtypeStruct((t_len, d_model), BF16), [pltpu.VMEM((OUT_ROWS, qk), BF16)])
-        d_x, sums = own_call(bwd_own_kernel, cp_index, after(tuple(dhs), x_out), weights, 3 * d_model, w12_off, od_blocks, od_got, (0,), qk + 2 * HEAD_DIM,
+        d_x, sums = own_call(bwd_own_kernel, cp_index, after(tuple(dhs), x_out), weights, 2 * d_model, w12_off, od_blocks, od_got, (0,), qk + 2 * HEAD_DIM,
                              [wqkv, x_loc, ng_own, swap_core(dn_oth), scale_f],
                              [full(wqkv), tile(d_model), tile(d_model, 1), tile(d_model), full(scale_f)],
                              [tile(d_model), pl.BlockSpec((16, d_model), lambda i, *_: (0, 0))],
@@ -816,9 +868,9 @@
         zero = jnp.zeros_like(db)
         db = jnp.where(first, jnp.stack([db, zero], axis=2), jnp.stack([zero, db], axis=2)).reshape(2, 16, f_blk)
         small = jnp.concatenate([sums[0], sums[1], db[0], db[1]], axis=1)
-        small = lax.psum(small, ALL_AXES)
-        small = lax.dynamic_index_in_dim(small, lax.axis_index(ALL_AXES), 0, keepdims=False)
-        g_scale, g_bias, g_b1, g_b2 = small[:r_in], small[r_in:2 * r_in], small[2 * r_in:2 * r_in + f_blk], small[2 * r_in + f_blk:]
+        small = jnp.pad(small, ((0, 0), (0, 1024 - small.shape[1]))).reshape(16, 8, 128)
+        small = small_sum(small).reshape(1024)
+        g_scale, g_bias, g_b1, g_b2 = small[:r_in], small[r_in:2 * r_in], small[2 * r_in:2 * r_in + f_blk], small[2 * r_in + f_blk:2 * r_in + 2 * f_blk]
 
         g_w1, g_w2, g_wd = join_up(owns, recvs)
         g_attn = owns[2][:r_o + r_in, 3 * d_model:]

time: 1360 us -> 1360 us (level)
  Pallas kernels: 615 us -> 655 us
  blocking collectives: 47.1 us -> 15.1 us
    pallas_call x4 -> x5, Pallas kernels: 175 us -> 212 us  [the longest x2 120 us: own_call(): pl.pallas_call(functools.partial(kernel, [w_off(col) for _, col in weight...]
    psum x1 -> x0, blocking collectives: 32.1 us -> none  [local_step(): small = lax.psum(small, ALL_AXES)]
  transfers between devices with their start and end apart: 30 -> 30, of which waited for: 16 -> 17; matrix products, arithmetic and copies ran while one was open for 3% -> 3% of each run, Pallas kernels for 44% -> 47%
where the time goes in v3:
time: 1360 us; the launch traced here: 1350 us
  Pallas kernels  655 us (48%)
  waiting for transfers between devices  590 us (43%)
  local copies, waits for them, and re-layouts  40.5 us (3%)
  starting transfers between devices  25.5 us (2%)
  blocking collectives  15.1 us (1%)
  between operations  14.5 us (1%)
    pallas_call x3, Pallas kernels, hidden_part(): pl.pallas_call(functools.partial(hidden_kernel, mode), grid=(steps,), in_...  286 us
    ppermute x12, waiting for transfers between devices, send_blocks(): lax.ppermute(sent, ('z', 'y'), [(i, i ^ flip) for i in range(4)])  275 us
    ppermute x5, waiting for transfers between devices, shift(): return lax.ppermute(values, axis, [(0, 1), (1, 0)])  207 us
    pallas_call x2, Pallas kernels, own_call(): pl.pallas_call(functools.partial(kernel, [w_off(col) for _, col in weight...  120 us
    all_gather x2, waiting for transfers between devices, gather(): return lax.all_gather(shard, CHIPS, axis=0, tiled=True)  85.3 us
    pallas_call x2, Pallas kernels, out_other(): pl.pallas_call(functools.partial(other_kernel, product, [w_off(col) for _...  84.7 us
    pallas_call x1, Pallas kernels, attention(): pl.pallas_call(attn_kernel, grid_spec=pltpu.PrefetchScalarGridSpec(num_sc...  84.3 us
  transfers between devices with their start and end apart: 30, of which 17 were waited for; matrix products, arithmetic and copies ran while one was open for 3% of the time, Pallas kernels for 47%

profile of v3, /device:TPU:0, one launch (start us, length us, event | category | flops | bytes accessed | tf_op | source)
XLA Modules:
  0.0 1353.3 jit_solution(15313666694500772362)
XLA Ops:
  7.2 4.8 split_up.1
  12.8 1.9 pack.1.extra_ref
  16.1 4.2 stack_up.1
  21.1 1.4 vectors.1
  22.5 15.1 %all-gather = bf16[128,512]{1,0:T(8,128)(2,1)S(1)} all-gather(bf16[8,512]{1,0:T(8,128)(2,1)} %vectors.1), channel_id=2, replica_groups=mesh['z'=2,'y'=2,'x'=2,'core'=2] {'z','y','x','core'}, dimensions={0}, use_global_device_ids=true | all-gather | bytes 139264 | tf_op jit(solution)/shard_map/all_gather | solution.py:796
  38.9 8.5 norm.1.own_ref.refs_12_
  50.8 11.7 collective-permute-done.oth_ref
  62.4 82.9 %all-gather.6.cloned.1.call-done.w_ref.refs_4_.refs_5_ = bf16[1152,6912]{1,0:T(8,128)(2,1)} async-done(((bf16[144,6912]{1,0:T(8,128)(2,1)}), bf16[1152,6912]{1,0:T(8,128)(2,1)}) %all-gather.6.cloned.1.call-update) | async-done | bytes 15925264 | tf_op jit(solution)/shard_map/all_gather | solution.py:791
  145.3 93.7 %hidden.4 = (bf16[4096,1152]{1,0:T(8,128)(2,1)}, bf16[4096,2304]{1,0:T(8,128)(2,1)}, f32[1152,3456]{1,0:T(8,128)}, f32[16,1152]{1,0:T(8,128)}) custom-call(bf16[2048,2304]{1,0:T(8,128)(2,1)} %norm.1.own_ref.refs_12_, bf16[2048,2304]{1,0:T(8,128)(2,1)} %collective-permute-done.oth_ref, bf16[1152,6912]{1,0:T(8,128)(2,1)} %all-gather.6.cloned.1.call-done.w_ref.refs_4_.refs_5_, ...), custom_call_target="tpu_custom_call" | custom-call | flops 65000001536 | bytes 70000000 | tf_op jit(solution)/shard_map/hidden/pallas_call | solution.py:422
  239.7 2.4 all-gather.4.cloned.1.call-done.w_ref.refs_3_
  242.0 2.2 slice.178.own_ref
  244.3 5.1 constant_dynamic-slice_fusion.6
  249.4 1.5 collective-permute-start.2
  250.9 1.5 fusion.7
  252.9 1.5 collective-permute-start.10
  254.4 1.6 collective-permute-start.11
  255.9 3.9 constant_dynamic-slice_fusion.3
  259.8 42.3 %collective-permute-done.9 = s32[1,2,512]{2,0,1:T(1,128)S(1)} collective-permute-done((s32[1,2,512]{2,0,1:T(1,128)S(1)}, s32[1,2,512]{2,0,1:T(1,128)S(1)}, u32[]{:S(2)}, u32[]{:S(2)}) %collective-permute-start.9) | collective-permute-done | bytes 4128 | tf_op jit(solution)/shard_map/ppermute | solution.py:768
  302.1 1.4 collective-permute-start.3
  303.6 2.3 collective-permute-start.4
  305.8 1.3 collective-permute-start.6
  307.2 2.1 collective-permute-start.7
  312.4 3.7 fusion
  316.1 1.9 pad_maximum_fusion
  318.0 6.0 unpack.1
  324.1 57.2 %collective-permute-done.3.n2_ref = bf16[1,512,1152]{2,1,0:T(8,128)(2,1)} collective-permute-done((bf16[1,512,1152]{2,1,0:T(8,128)(2,1)}, bf16[1,512,1152]{2,1,0:T(8,128)(2,1)}, u32[]{:S(2)}, u32[]{:S(2)}) %collective-permute-start.3) | collective-permute-done | bytes 1179680 | tf_op jit(solution)/shard_map/ppermute | solution.py:768
  381.3 4.8 collective-permute-done.5.g1_ref
  386.1 68.0 %collective-permute-done.6.g2_ref = bf16[1,512,1152]{2,1,0:T(8,128)(2,1)} collective-permute-done((bf16[1,512,1152]{2,1,0:T(8,128)(2,1)}, bf16[1,512,1152]{2,1,0:T(8,128)(2,1)}, u32[]{:S(2)}, u32[]{:S(2)}) %collective-permute-start.6) | collective-permute-done | bytes 1179680 | tf_op jit(solution)/shard_map/ppermute | solution.py:768
  454.1 1.4 broadcast_in_dim.46.segq_ref
  456.1 84.3 %attn.1.dqkv_ref.o_lo_ref.o_hi_ref = bf16[2048,2560]{1,0:T(8,128)(2,1)} custom-call(s32[1]{0:T(128)} %bitcast.cp_ref, bf16[4,512,2304]{2,1,0:T(8,128)(2,1)} %bitcast.60, bf16[1,512,1152]{2,1,0:T(8,128)(2,1)} %collective-permute-done.2.n1_ref, bf16[1,512,1152]{2,1,0:T(8,128)(2,1)} %collective-permute-done.3.n2_ref, ...), custom_call_target="tpu_custom_call" | custom-call | flops 44999999488 | bytes 40000000 | tf_op jit(solution)/shard_map/attn/pallas_call | solution.py:157
  540.5 23.1 %attn_grad.1 = (f32[8,136,1536]{2,1,0:T(8,128)}, f32[8,136,1536]{2,1,0:T(8,128)}) custom-call(s32[1]{0:T(128)} %bitcast.cp_ref, bf16[4,512,2304]{2,1,0:T(8,128)(2,1)} %bitcast.61, bf16[1,512,1152]{2,1,0:T(8,128)(2,1)} %collective-permute-done.2.n1_ref, bf16[1,512,1152]{2,1,0:T(8,128)(2,1)} %collective-permute-done.3.n2_ref, ...), custom_call_target="tpu_custom_call" | custom-call | flops 12000000000 | bytes 33000000 | tf_op jit(solution)/shard_map/attn_grad/pallas_call | solution.py:540
  565.0 9.7 collective-permute-done.12.refs_1_
  574.7 96.3 %hidden.5 = (bf16[4096,1152]{1,0:T(8,128)(2,1)}, bf16[4096,2304]{1,0:T(8,128)(2,1)}, f32[1152,4992]{1,0:T(8,128)}, f32[16,1152]{1,0:T(8,128)}) custom-call(bf16[2048,2304]{1,0:T(8,128)(2,1)} %norm.1.own_ref.refs_12_, bf16[2048,2304]{1,0:T(8,128)(2,1)} %collective-permute-done.oth_ref, bf16[1152,6912]{1,0:T(8,128)(2,1)} %all-gather.6.cloned.1.call-done.w_ref.refs_4_.refs_5_, ...), custom_call_target="tpu_custom_call" | custom-call | flops 65000001536 | bytes 70000000 | tf_op jit(solution)/shard_map/hidden/pallas_call | solution.py:422
  673.1 95.7 %hidden.3 = (bf16[4096,1152]{1,0:T(8,128)(2,1)}, bf16[4096,2304]{1,0:T(8,128)(2,1)}, f32[4,144,3456]{2,1,0:T(8,128)}, f32[4,144,3456]{2,1,0:T(8,128)}, f32[16,1152]{1,0:T(8,128)}) custom-call(bf16[2048,2304]{1,0:T(8,128)(2,1)} %norm.1.own_ref.refs_12_, bf16[2048,2304]{1,0:T(8,128)(2,1)} %collective-permute-done.oth_ref, ...), custom_call_target="tpu_custom_call" | custom-call | flops 65000001536 | bytes 70000000 | tf_op jit(solution)/shard_map/hidden/pallas_call | solution.py:422
  768.8 30.8 %shard_map.263 = f32[2048,1152]{1,0:T(8,128)} custom-call(bf16[4096,1152]{1,0:T(8,128)(2,1)} %get-tuple-element.74.refs_0_, bf16[4096,1152]{1,0:T(8,128)(2,1)} %get-tuple-element.75.refs_1_, bf16[4096,1152]{1,0:T(8,128)(2,1)} %get-tuple-element.76.refs_2_, bf16[1152,4992]{1,0:T(8,128)(2,1)} %all-gather.4.cloned.1.call-done.w_ref.refs_3_, ...), custom_call_target="tpu_custom_call" | custom-call | flops 16307453952 | bytes 50000000 | tf_op jit(solution)/shard_map/pallas_call | solution.py:638
  799.7 53.9 %shard_map.264 = f32[2048,1152]{1,0:T(8,128)} custom-call(bf16[4096,2304]{1,0:T(8,128)(2,1)} %get-tuple-element.77.refs_0_, bf16[4096,2304]{1,0:T(8,128)(2,1)} %get-tuple-element.78.refs_1_, bf16[4096,2304]{1,0:T(8,128)(2,1)} %get-tuple-element.79.refs_2_, bf16[1152,4992]{1,0:T(8,128)(2,1)} %all-gather.4.cloned.1.call-done.w_ref.refs_3_, ...), custom_call_target="tpu_custom_call" | custom-call | flops 32614907904 | bytes 50000000 | tf_op jit(solution)/shard_map/pallas_call | solution.py:638
  854.1 145.8 %collective-permute-done.18.got_ref = f32[4,144,3456]{2,1,0:T(8,128)} collective-permute-done((f32[4,144,3456]{2,1,0:T(8,128)}, f32[4,144,3456]{2,1,0:T(8,128)}, u32[]{:S(2)}, u32[]{:S(2)}) %collective-permute-start.18) | collective-permute-done | bytes 7962656 | tf_op jit(solution)/shard_map/ppermute | solution.py:755
  999.9 8.4 fold_first.1
  1008.4 1.3 copy-done.2
  1009.7 1.5 collective-permute-start.19
  1011.2 1.5 collective-permute-start.20
  1012.6 41.8 %collective-permute-done.20.got_b_ref = f32[2,144,1664]{2,1,0:T(8,128)S(1)} collective-permute-done((f32[2,144,1664]{2,1,0:T(8,128)S(1)}, f32[2,144,1664]{2,1,0:T(8,128)S(1)}, u32[]{:S(2)}, u32[]{:S(2)}) %collective-permute-start.20) | collective-permute-done | bytes 1916960 | tf_op jit(solution)/shard_map/ppermute | solution.py:755
  1054.4 2.2 collective-permute-done.19.got_a_ref
  1057.9 3.3 fold_second.1
  1061.2 1.5 collective-permute-start.21
  1062.7 1.5 collective-permute-start.22
  1064.3 3.4 constant_dynamic-slice_fusion
  1068.3 16.3 %collective-permute-done.22.got_b_ref = f32[144,1664]{1,0:T(8,128)S(1)} collective-permute-done((f32[144,1664]{1,0:T(8,128)S(1)}, f32[144,1664]{1,0:T(8,128)S(1)}, u32[]{:S(2)}, u32[]{:S(2)}) %collective-permute-start.22) | collective-permute-done | bytes 958496 | tf_op jit(solution)/shard_map/ppermute | solution.py:755
  1084.6 1.5 collective-permute-start.14
  1087.0 2.4 collective-permute-start.15
  1090.8 3.6 fold_third.1.refs_0_
  1094.4 1.4 slice_select_fusion.2
  1095.8 47.4 %collective-permute-done.13.refs_8_.refs_9_.refs_7_ = bf16[1,512,2560]{2,1,0:T(8,128)(2,1)} collective-permute-done((bf16[1,512,2560]{2,1,0:T(8,128)(2,1)}, bf16[1,512,2560]{2,1,0:T(8,128)(2,1)}, u32[]{:S(2)}, u32[]{:S(2)}) %collective-permute-start.13) | collective-permute-done | bytes 2621472 | tf_op jit(solution)/shard_map/ppermute | solution.py:768
  1143.2 53.5 %collective-permute-done.14.refs_10_.refs_11_.refs_8_ = bf16[1,512,2560]{2,1,0:T(8,128)(2,1)} collective-permute-done((bf16[1,512,2560]{2,1,0:T(8,128)(2,1)}, bf16[1,512,2560]{2,1,0:T(8,128)(2,1)}, u32[]{:S(2)}, u32[]{:S(2)}) %collective-permute-start.14) | collective-permute-done | bytes 2621472 | tf_op jit(solution)/shard_map/ppermute | solution.py:768
  1196.8 1.6 collective-permute-done.15.refs_12_.refs_13_.refs_9_
  1198.4 40.8 %shard_map.265 = bf16[2048,1152]{1,0:T(8,128)(2,1)} custom-call(s32[1]{0:T(128)} %bitcast.cp_ref, bf16[4096,1152]{1,0:T(8,128)(2,1)} %get-tuple-element.74.refs_0_, bf16[4096,1152]{1,0:T(8,128)(2,1)} %get-tuple-element.75.refs_1_, bf16[4096,1152]{1,0:T(8,128)(2,1)} %get-tuple-element.76.refs_2_, ...), custom_call_target="tpu_custom_call" | custom-call | flops 21139292160 | bytes 80000000 | tf_op jit(solution)/shard_map/pallas_call | solution.py:703
  1239.2 79.2 %shard_map.266 = (bf16[2048,1152]{1,0:T(8,128)(2,1)}, f32[16,1152]{1,0:T(8,128)}) custom-call(s32[1]{0:T(128)} %bitcast.cp_ref, bf16[4096,2304]{1,0:T(8,128)(2,1)} %get-tuple-element.77.refs_0_, bf16[4096,2304]{1,0:T(8,128)(2,1)} %get-tuple-element.78.refs_1_, bf16[4096,2304]{1,0:T(8,128)(2,1)} %get-tuple-element.79.refs_2_, ...), custom_call_target="tpu_custom_call" | custom-call | flops 37446746112 | bytes 80000000 | tf_op jit(solution)/shard_map/pallas_call | solution.py:703
  1320.3 7.4 small_sum.1
  1327.8 1.4 slice_select_fusion.1
  1329.3 1.4 slice_select_fusion
  1332.2 1.7 slice.187
  1333.9 1.7 slice.190
  1335.6 1.6 fusion.11
  1338.3 7.8 join_up.1
  (142 shorter events, 25.9 us)
Async XLA Ops:
  7.2 138.2 %all-gather.6.cloned.1.call-start = ((), (), s32[]{:S(2)}) async-start(), calls=%async_computation.3 | async-start | bytes 17915904 | tf_op jit(solution)/shard_map/all_gather | solution.py:791
  12.0 3.2 collective-permute-start.1
  15.2 0.9 copy-start.5
  20.3 221.7 %all-gather.4.cloned.1.call-start = ((), (), s32[]{:S(2)}) async-start(), calls=%async_computation.2 | async-start | bytes 12939264 | tf_op jit(solution)/shard_map/all_gather | solution.py:791
  21.1 1306.7 %reduce-scatter.5.cloned.1.call-start = ((), (), s32[]{:S(2)}) async-start(), calls=%async_computation.5 | async-start | bytes 17915904 | tf_op jit(solution)/shard_map/reduce_scatter | solution.py:830
  47.4 15.0 %collective-permute-start = (bf16[2048,2304]{1,0:T(8,128)(2,1)}, bf16[2048,2304]{1,0:T(8,128)(2,1)}, u32[]{:S(2)}, u32[]{:S(2)}) collective-permute-start(bf16[2048,2304]{1,0:T(8,128)(2,1)} %norm.1.own_ref.refs_12_), channel_id=1, source_target_pairs={{0,1},{1,0},{2,3},{3,2},{4,5},{5,4},{6,7},{7,6},{8,9},{9,8},{10,11... | collective-permute-start | bytes 28311560 | tf_op jit(solution)/shard_map/ppermute | solution.py:751
  239.0 1090.3 %reduce-scatter.3.cloned.1.call-start = ((), (), s32[]{:S(2)}) async-start(), calls=%async_computation.4 | async-start | bytes 25878528 | tf_op jit(solution)/shard_map/reduce_scatter | solution.py:830
  244.3 5.2 copy-start.3
  244.3 62.9 %collective-permute-start.8 = (bf16[1152,1536]{1,0:T(8,128)(2,1)S(1)}, bf16[1152,1536]{1,0:T(8,128)(2,1)}, u32[]{:S(2)}, u32[]{:S(2)}) collective-permute-start(bf16[1152,1536]{1,0:T(8,128)(2,1)S(1)} %slice.178.own_ref), channel_id=1, source_target_pairs={{0,1},{1,0},{2,3},{3,2},{4,5},{5,4},{6,7},{7,6},{8,9},{9,8},{10,11... | collective-permute-start | bytes 10616840 | tf_op jit(solution)/shard_map/ppermute | solution.py:751
  249.4 56.4 %collective-permute-start.2 = (bf16[1,512,1152]{2,1,0:T(8,128)(2,1)}, bf16[1,512,1152]{2,1,0:T(8,128)(2,1)}, u32[]{:S(2)}, u32[]{:S(2)}) collective-permute-start(bf16[1,512,1152]{2,1,0:T(8,128)(2,1)} %get-tuple-element.113), channel_id=1, source_target_pairs={{0,4},{4,0},{8,12},{12,8},{1,5},{5,1},{9,13},{13,9},{2,6},{6,2},{1... | collective-permute-start | bytes 3538952 | tf_op jit(solution)/shard_map/ppermute | solution.py:768
  252.4 49.7 %collective-permute-start.9 = (s32[1,2,512]{2,0,1:T(1,128)S(1)}, s32[1,2,512]{2,0,1:T(1,128)S(1)}, u32[]{:S(2)}, u32[]{:S(2)}) collective-permute-start(s32[1,2,512]{2,0,1:T(1,128)S(1)} %get-tuple-element.130), channel_id=1, source_target_pairs={{0,4},{4,0},{8,12},{12,8},{1,5},{5,1},{9,13},{13,9},{2,6},{6,2},{1... | collective-permute-start | bytes 12296 | tf_op jit(solution)/shard_map/ppermute | solution.py:768
  252.9 50.7 %collective-permute-start.10 = (s32[1,2,512]{2,0,1:T(1,128)S(1)}, s32[1,2,512]{2,0,1:T(1,128)S(1)}, u32[]{:S(2)}, u32[]{:S(2)}) collective-permute-start(s32[1,2,512]{2,0,1:T(1,128)S(1)} %get-tuple-element.131), channel_id=1, source_target_pairs={{0,8},{4,12},{8,0},{12,4},{1,9},{5,13},{9,1},{13,5},{2,10},{6,14},... | collective-permute-start | bytes 12296 | tf_op jit(solution)/shard_map/ppermute | solution.py:768
  254.4 51.5 %collective-permute-start.11 = (s32[1,2,512]{2,0,1:T(1,128)S(1)}, s32[1,2,512]{2,0,1:T(1,128)S(1)}, u32[]{:S(2)}, u32[]{:S(2)}) collective-permute-start(s32[1,2,512]{2,0,1:T(1,128)S(1)} %get-tuple-element.128), channel_id=1, source_target_pairs={{0,12},{4,8},{8,4},{12,0},{1,13},{5,9},{9,5},{13,1},{2,14},{6,10},... | collective-permute-start | bytes 12296 | tf_op jit(solution)/shard_map/ppermute | solution.py:768
  302.1 7.2 copy-start.16
  302.1 79.2 %collective-permute-start.3 = (bf16[1,512,1152]{2,1,0:T(8,128)(2,1)}, bf16[1,512,1152]{2,1,0:T(8,128)(2,1)}, u32[]{:S(2)}, u32[]{:S(2)}) collective-permute-start(bf16[1,512,1152]{2,1,0:T(8,128)(2,1)} %get-tuple-element.112), channel_id=1, source_target_pairs={{0,8},{4,12},{8,0},{12,4},{1,9},{5,13},{9,1},{13,5},{2,10},{6,14},... | collective-permute-start | bytes 3538952 | tf_op jit(solution)/shard_map/ppermute | solution.py:768
  303.6 5.8 copy-start.17
  303.6 77.7 %collective-permute-start.4 = (bf16[1,512,1152]{2,1,0:T(8,128)(2,1)}, bf16[1,512,1152]{2,1,0:T(8,128)(2,1)}, u32[]{:S(2)}, u32[]{:S(2)}) collective-permute-start(bf16[1,512,1152]{2,1,0:T(8,128)(2,1)} %get-tuple-element.111), channel_id=1, source_target_pairs={{0,12},{4,8},{8,4},{12,0},{1,13},{5,9},{9,5},{13,1},{2,14},{6,10},... | collective-permute-start | bytes 3538952 | tf_op jit(solution)/shard_map/ppermute | solution.py:768
  305.8 3.5 copy-start.18
  305.8 80.3 %collective-permute-start.5 = (bf16[1,512,1152]{2,1,0:T(8,128)(2,1)}, bf16[1,512,1152]{2,1,0:T(8,128)(2,1)}, u32[]{:S(2)}, u32[]{:S(2)}) collective-permute-start(bf16[1,512,1152]{2,1,0:T(8,128)(2,1)} %get-tuple-element.115), channel_id=1, source_target_pairs={{0,4},{4,0},{8,12},{12,8},{1,5},{5,1},{9,13},{13,9},{2,6},{6,2},{1... | collective-permute-start | bytes 3538952 | tf_op jit(solution)/shard_map/ppermute | solution.py:768
  305.8 148.3 %collective-permute-start.6 = (bf16[1,512,1152]{2,1,0:T(8,128)(2,1)}, bf16[1,512,1152]{2,1,0:T(8,128)(2,1)}, u32[]{:S(2)}, u32[]{:S(2)}) collective-permute-start(bf16[1,512,1152]{2,1,0:T(8,128)(2,1)} %get-tuple-element.116), channel_id=1, source_target_pairs={{0,8},{4,12},{8,0},{12,4},{1,9},{5,13},{9,1},{13,5},{2,10},{6,14},... | collective-permute-start | bytes 3538952 | tf_op jit(solution)/shard_map/ppermute | solution.py:768
  307.2 146.9 %collective-permute-start.7 = (bf16[1,512,1152]{2,1,0:T(8,128)(2,1)}, bf16[1,512,1152]{2,1,0:T(8,128)(2,1)S(1)}, u32[]{:S(2)}, u32[]{:S(2)}) collective-permute-start(bf16[1,512,1152]{2,1,0:T(8,128)(2,1)} %get-tuple-element.114), channel_id=1, source_target_pairs={{0,12},{4,8},{8,4},{12,0},{1,13},{5,9},{9,5},{13,1},{2,14},{6,10},... | collective-permute-start | bytes 3538952 | tf_op jit(solution)/shard_map/ppermute | solution.py:768
  454.1 2.0 copy-start.4
  563.6 11.1 collective-permute-start.12
  671.0 0.7 copy-start.13
  671.0 1.4 copy-start.14
  768.8 231.1 %collective-permute-start.18 = (f32[4,144,3456]{2,1,0:T(8,128)}, f32[4,144,3456]{2,1,0:T(8,128)}, u32[]{:S(2)}, u32[]{:S(2)}) collective-permute-start(f32[4,144,3456]{2,1,0:T(8,128)} %get-tuple-element.87), channel_id=1, source_target_pairs={{0,2},{2,0},{1,3},{3,1},{4,6},{6,4},{5,7},{7,5},{8,10},{10,8},{9,1... | collective-permute-start | bytes 23887880 | tf_op jit(solution)/shard_map/ppermute | solution.py:755
  799.6 398.8 %collective-permute-start.16 = (f32[2048,1152]{1,0:T(8,128)}, f32[2048,1152]{1,0:T(8,128)}, u32[]{:S(2)}, u32[]{:S(2)}) collective-permute-start(f32[2048,1152]{1,0:T(8,128)} %shard_map.263), channel_id=1, source_target_pairs={{0,1},{1,0},{2,3},{3,2},{4,5},{5,4},{6,7},{7,6},{8,9},{9,8},{10,11... | collective-permute-start | bytes 28311560 | tf_op jit(solution)/shard_map/ppermute | solution.py:751
  853.6 385.6 %collective-permute-start.17 = (f32[2048,1152]{1,0:T(8,128)}, f32[2048,1152]{1,0:T(8,128)}, u32[]{:S(2)}, u32[]{:S(2)}) collective-permute-start(f32[2048,1152]{1,0:T(8,128)} %shard_map.264), channel_id=1, source_target_pairs={{0,1},{1,0},{2,3},{3,2},{4,5},{5,4},{6,7},{7,6},{8,9},{9,8},{10,11... | collective-permute-start | bytes 28311560 | tf_op jit(solution)/shard_map/ppermute | solution.py:751
  999.9 64.3 %slice-start = ((s8[10485760]{0:T(1024)(128)(4,1)}), s8[4194304]{0:T(1024)(128)(4,1)S(1)}, s32[]{:S(2)}) async-start(s8[10485760]{0:T(1024)(128)(4,1)} %bitcast.56), calls=%async_computation.6 | async-start | bytes 8388608
  999.9 64.3 %slice-start.1 = ((s8[10485760]{0:T(1024)(128)(4,1)}), s8[2097152]{0:T(1024)(128)(4,1)S(1)}, s32[]{:S(2)}) async-start(s8[10485760]{0:T(1024)(128)(4,1)} %bitcast.56), calls=%async_computation.7 | async-start | bytes 4194304
  1008.4 1.3 copy-start.2
  1009.7 46.9 %collective-permute-start.19 = (f32[2,144,1792]{2,1,0:T(8,128)}, f32[2,144,1792]{2,1,0:T(8,128)S(1)}, u32[]{:S(2)}, u32[]{:S(2)}) collective-permute-start(f32[2,144,1792]{2,1,0:T(8,128)} %get-tuple-element.89), channel_id=1, source_target_pairs={{0,8},{8,0},{1,9},{9,1},{2,10},{10,2},{3,11},{11,3},{4,12},{12,4},... | collective-permute-start | bytes 6193160 | tf_op jit(solution)/shard_map/ppermute | solution.py:755
  1011.2 43.3 %collective-permute-start.20 = (f32[2,144,1664]{2,1,0:T(8,128)S(1)}, f32[2,144,1664]{2,1,0:T(8,128)S(1)}, u32[]{:S(2)}, u32[]{:S(2)}) collective-permute-start(f32[2,144,1664]{2,1,0:T(8,128)S(1)} %get-tuple-element.91), channel_id=1, source_target_pairs={{0,4},{4,0},{1,5},{5,1},{2,6},{6,2},{3,7},{7,3},{8,12},{12,8},{9,1... | collective-permute-start | bytes 5750792 | tf_op jit(solution)/shard_map/ppermute | solution.py:755
  1054.4 2.2 copy-start.21
  1056.6 1.3 copy-start.20
  1057.9 6.3 slice-start.2
  1061.2 6.5 copy-start
  1061.2 6.5 copy-start.1
  1061.2 25.7 %collective-permute-start.21 = (f32[144,1792]{1,0:T(8,128)S(1)}, f32[144,1792]{1,0:T(8,128)S(1)}, u32[]{:S(2)}, u32[]{:S(2)}) collective-permute-start(f32[144,1792]{1,0:T(8,128)S(1)} %get-tuple-element.93), channel_id=1, source_target_pairs={{0,4},{4,0},{1,5},{5,1},{2,6},{6,2},{3,7},{7,3},{8,12},{12,8},{9,1... | collective-permute-start | bytes 3096584 | tf_op jit(solution)/shard_map/ppermute | solution.py:755
  1062.7 21.9 %collective-permute-start.22 = (f32[144,1664]{1,0:T(8,128)S(1)}, f32[144,1664]{1,0:T(8,128)S(1)}, u32[]{:S(2)}, u32[]{:S(2)}) collective-permute-start(f32[144,1664]{1,0:T(8,128)S(1)} %get-tuple-element.95), channel_id=1, source_target_pairs={{0,8},{8,0},{1,9},{9,1},{2,10},{10,2},{3,11},{11,3},{4,12},{12,4},... | collective-permute-start | bytes 2875400 | tf_op jit(solution)/shard_map/ppermute | solution.py:755
  1064.2 25.1 %copy-start.11 = (bf16[16,1,72]{2,1,0:T(2,128)(2,1)S(1)}, bf16[16,1,72]{2,1,0:T(2,128)(2,1)}, u32[]{:S(2)}) copy-start(bf16[16,1,72]{2,1,0:T(2,128)(2,1)} %get-tuple-element.119) | copy-start | bytes 6916
  1064.2 25.1 %copy-start.12 = (bf16[16,1,72]{2,1,0:T(2,128)(2,1)S(1)}, bf16[16,1,72]{2,1,0:T(2,128)(2,1)}, u32[]{:S(2)}) copy-start(bf16[16,1,72]{2,1,0:T(2,128)(2,1)} %get-tuple-element.121) | copy-start | bytes 6916
  1064.2 25.8 %copy-start.10 = (f32[16,1152]{1,0:T(8,128)S(1)}, f32[16,1152]{1,0:T(8,128)}, u32[]{:S(2)}) copy-start(f32[16,1152]{1,0:T(8,128)} %get-tuple-element.82) | copy-start | bytes 221188
  1064.3 25.9 %copy-start.8 = (f32[16,1152]{1,0:T(8,128)S(1)}, f32[16,1152]{1,0:T(8,128)}, u32[]{:S(2)}) copy-start(f32[16,1152]{1,0:T(8,128)} %get-tuple-element.83) | copy-start | bytes 221188
  1064.3 26.1 %copy-start.9 = (f32[16,1152]{1,0:T(8,128)S(1)}, f32[16,1152]{1,0:T(8,128)}, u32[]{:S(2)}) copy-start(f32[16,1152]{1,0:T(8,128)} %get-tuple-element.84) | copy-start | bytes 221188
  1067.7 75.5 %collective-permute-start.13 = (bf16[1,512,2560]{2,1,0:T(8,128)(2,1)}, bf16[1,512,2560]{2,1,0:T(8,128)(2,1)}, u32[]{:S(2)}, u32[]{:S(2)}) collective-permute-start(bf16[1,512,2560]{2,1,0:T(8,128)(2,1)} %get-tuple-element.110), channel_id=1, source_target_pairs={{0,4},{4,0},{8,12},{12,8},{1,5},{5,1},{9,13},{13,9},{2,6},{6,2},{1... | collective-permute-start | bytes 7864328 | tf_op jit(solution)/shard_map/ppermute | solution.py:768
  1084.6 4.7 copy-start.23
  1084.6 112.2 %collective-permute-start.14 = (bf16[1,512,2560]{2,1,0:T(8,128)(2,1)}, bf16[1,512,2560]{2,1,0:T(8,128)(2,1)}, u32[]{:S(2)}, u32[]{:S(2)}) collective-permute-start(bf16[1,512,2560]{2,1,0:T(8,128)(2,1)} %get-tuple-element.109), channel_id=1, source_target_pairs={{0,8},{4,12},{8,0},{12,4},{1,9},{5,13},{9,1},{13,5},{2,10},{6,14},... | collective-permute-start | bytes 7864328 | tf_op jit(solution)/shard_map/ppermute | solution.py:768
  1087.0 2.4 copy-start.22
  1087.0 111.4 %collective-permute-start.15 = (bf16[1,512,2560]{2,1,0:T(8,128)(2,1)}, bf16[1,512,2560]{2,1,0:T(8,128)(2,1)}, u32[]{:S(2)}, u32[]{:S(2)}) collective-permute-start(bf16[1,512,2560]{2,1,0:T(8,128)(2,1)} %get-tuple-element.108), channel_id=1, source_target_pairs={{0,12},{4,8},{8,4},{12,0},{1,13},{5,9},{9,5},{13,1},{2,14},{6,10},... | collective-permute-start | bytes 7864328 | tf_op jit(solution)/shard_map/ppermute | solution.py:768
  1143.2 194.0 %collective-permute-start.23 = (f32[72,2304]{1,0:T(8,128)S(1)}, f32[72,2304]{1,0:T(8,128)S(1)}, u32[]{:S(2)}, u32[]{:S(2)}) collective-permute-start(f32[72,2304]{1,0:T(8,128)S(1)} %slice_select_fusion.2), channel_id=1, source_target_pairs={{0,1},{1,0},{2,3},{3,2},{4,5},{5,4},{6,7},{7,6},{8,9},{9,8},{10,11... | collective-permute-start | bytes 1990664 | tf_op jit(solution)/shard_map/ppermute | solution.py:751
  1327.7 3.4 copy-start.15
  1329.1 8.1 collective-permute-start.24
  1330.6 6.6 collective-permute-start.25
  1331.6 14.5 %copy-start.19 = (f32[72]{0:T(128)}, f32[72]{0:T(128)S(1)}, u32[]{:S(2)}) copy-start(f32[72]{0:T(128)S(1)} %get-tuple-element.170) | copy-start | bytes 868
  1337.2 0.8 copy-start.6
  1337.2 1.0 copy-start.7
Sparse Core Ops, SparseCore 0:
  20.5 124.8 all-gather.5
  148.1 93.9 all-gather.3
  246.3 236.2 reduce-scatter.4
  671.2 226.5 reduce-scatter.2

commit v4 on v1

--- a/solution.py
+++ b/solution.py
@@ -35,29 +35,33 @@
 
 
 def attn_kernel(cp_ref, own_ref, n1_ref, n2_ref, n3_ref, g1_ref, g2_ref, g3_ref, wqkv_ref, wo_ref, cos_ref, sin_ref, cosk_ref, sink_ref, segq_ref, segk_ref, out_ref,
-                n_s, g_s, q_s, do_s, k_s, v_s, kt_s, vt_s, mask_s, s_s, p_s, dk_s, dv_s):
+                n_buf, g_buf, sems, q_s, do_s, k_s, v_s, kt_s, vt_s, mask_s, s_s, p_s, dk_s, dv_s):
     step = pl.program_id(0)
     n_blocks = pl.num_programs(0)
-    rows, d_model = n_s.shape
+    rows, d_model = n_buf.shape[1:]
     qk = N_HEADS * HEAD_DIM
     base = pl.multiple_of(step * rows, rows)
     cos_b = cos_ref[...]
     sin_b = sin_ref[...]
-    flip = step ^ cp_ref[0]
-
-    @pl.when(flip == 0)
-    def _():
-        n_s[...] = own_ref[0, :, :d_model]
-        g_s[...] = own_ref[0, :, d_model:]
-
-    for i, (n_ref, g_ref) in enumerate(((n1_ref, g1_ref), (n2_ref, g2_ref), (n3_ref, g3_ref))):
-        @pl.when(flip == i + 1)
-        def _():
-            n_s[...] = n_ref[0]
-            g_s[...] = g_ref[0]
-
-    n_blk = n_s[...]
-    g_blk = g_s[...]
+    slot = lax.rem(step, 2)
+
+    def fetch(at_step):
+        flip = at_step ^ cp_ref[0]
+        to = lax.rem(at_step, 2)
+        own = own_ref.at[cp_ref[0]]
+        sources = ((own.at[:, :d_model], own.at[:, d_model:]), (n1_ref.at[0], g1_ref.at[0]), (n2_ref.at[0], g2_ref.at[0]), (n3_ref.at[0], g3_ref.at[0]))
+        for i, (n_src, g_src) in enumerate(sources):
+            @pl.when(flip == i)
+            def _():
+                pltpu.make_async_copy(n_src, n_buf.at[to], sems.at[0, to]).start()
+                pltpu.make_async_copy(g_src, g_buf.at[to], sems.at[1, to]).start()
+
+    pl.when(step == 0)(lambda: fetch(step))
+    pl.when(step + 1 < n_blocks)(lambda: fetch(step + 1))
+    pltpu.make_async_copy(n1_ref.at[0], n_buf.at[slot], sems.at[0, slot]).wait()
+    pltpu.make_async_copy(g1_ref.at[0], g_buf.at[slot], sems.at[1, slot]).wait()
+    n_blk = n_buf[slot]
+    g_blk = g_buf[slot]
 
     @pl.when(step == 0)
     def _():
@@ -148,17 +152,17 @@
     segk = jnp.broadcast_to(seg_own[None, :], (8, t_len))
     row_spec = lambda width: pl.BlockSpec((rows, width), lambda i, cp: (i, 0))
     full = lambda a: pl.BlockSpec(a.shape, lambda i, cp: (0,) * a.ndim, pipeline_mode=pl.Buffered(1))
-    own_spec = pl.BlockSpec((1, rows, both), lambda i, cp: (cp[0], 0, 0), pipeline_mode=pl.Buffered(1))
+    anywhere = pl.BlockSpec(memory_space=pl.ANY)
     width = 2 * (qk + HEAD_DIM)
     return pl.pallas_call(
         attn_kernel,
         grid_spec=pltpu.PrefetchScalarGridSpec(
             num_scalar_prefetch=1,
             grid=(4,),
-            in_specs=[own_spec] + [full(a) for a in n_got + g_got] + [full(wqkv), full(wo), row_spec(ROPE_DIMS), row_spec(ROPE_DIMS), full(cos_b), full(sin_b), row_spec(128), full(segk)],
+            in_specs=[anywhere] * 7 + [full(wqkv), full(wo), row_spec(ROPE_DIMS), row_spec(ROPE_DIMS), full(cos_b), full(sin_b), row_spec(128), full(segk)],
             out_specs=pl.BlockSpec((t_len, width), lambda i, cp: (0, 0)),
             scratch_shapes=[
-                pltpu.VMEM((rows, both // 2), BF16), pltpu.VMEM((rows, both // 2), BF16),
+                pltpu.VMEM((2, rows, both // 2), BF16), pltpu.VMEM((2, rows, both // 2), BF16), pltpu.SemaphoreType.DMA((2, 2)),
                 pltpu.VMEM((N_HEADS, rows, HEAD_DIM), BF16), pltpu.VMEM((N_HEADS, rows, HEAD_DIM), BF16),
                 pltpu.VMEM((t_len, HEAD_DIM), BF16), pltpu.VMEM((t_len, HEAD_DIM), BF16),
                 pltpu.VMEM((HEAD_DIM, t_len), BF16), pltpu.VMEM((HEAD_DIM, t_len), BF16),
@@ -472,6 +476,41 @@
     )(cp_index[None], ng_blocks, *n_got, *g_got, od_seq, od_seq, od_seq)
 
 
+def small_kernel(in_ref, out_ref, got_s, send_sems, recv_sems):
+    at = [lax.axis_index(axis) for axis in ALL_AXES]
+    me = ((at[0] * 2 + at[1]) * 2 + at[2]) * 2 + at[3]
+
+    def peer(flip):
+        return tuple(index ^ ((flip >> (3 - i)) & 1) for i, index in enumerate(at))
+
+    barrier = pltpu.get_barrier_semaphore()
+    for flip in range(1, 16):
+        pl.semaphore_signal(barrier, inc=1, device_id=peer(flip), device_id_type=pl.DeviceIdType.MESH)
+    pl.semaphore_wait(barrier, 15)
+    copies = []
+    for flip in range(1, 16):
+        copies.append(pltpu.make_async_remote_copy(
+            src_ref=in_ref.at[me ^ flip], dst_ref=got_s.at[flip], send_sem=send_sems.at[flip], recv_sem=recv_sems.at[flip],
+            device_id=peer(flip), device_id_type=pl.DeviceIdType.MESH))
+        copies[-1].start()
+    for copy in copies:
+        copy.wait()
+    total = in_ref[me]
+    for flip in range(1, 16):
+        total = total + got_s[flip]
+    out_ref[...] = total
+
+
+def small_sum(values):
+    return pl.pallas_call(
+        small_kernel, out_shape=jax.ShapeDtypeStruct(values.shape[1:], F32), name='small_sum',
+        in_specs=[pl.BlockSpec(memory_space=pltpu.VMEM)], out_specs=pl.BlockSpec(memory_space=pltpu.VMEM),
+        scratch_shapes=[pltpu.VMEM(values.shape, F32), pltpu.SemaphoreType.DMA((16,)), pltpu.SemaphoreType.DMA((16,))],
+        compiler_params=pltpu.CompilerParams(collective_id=0, has_side_effects=True),
+        cost_estimate=pl.CostEstimate(flops=8_000_000_000, bytes_accessed=130_000, transcendentals=0),
+    )(values)
+
+
 def fwd_product(act_refs, w_refs):
     out = dot_nn(act_refs[0][...], w_refs[0][...])
     for act_ref, w_ref in zip(act_refs[1:], w_refs[1:]):
@@ -562,9 +601,9 @@
     for i, source in enumerate([od_blocks] + od_got):
         for col in od_cols:
             if i == 0:
-                specs.append(pl.BlockSpec((1, OUT_ROWS, od_width), lambda j, cp, col=col: (cp[0], j % 2, col)))
+                specs.append(pl.BlockSpec((1, OUT_ROWS, od_width), lambda j, cp, col=col: (cp[0], jnp.clip(j - 2 * cp[0], 0, 1), col)))
             else:
-                specs.append(pl.BlockSpec((1, OUT_ROWS, od_width), lambda j, cp, col=col: (0, j % 2, col)))
+                specs.append(pl.BlockSpec((1, OUT_ROWS, od_width), lambda j, cp, col=col, i=i: (0, jnp.clip(j - 2 * (cp[0] ^ i), 0, 1), col)))
             args.append(source)
     return pl.pallas_call(
         kernel,
@@ -615,6 +654,9 @@
 
     def swap_core(values):
         return lax.ppermute(values, 'core', [(0, 1), (1, 0)])
+
+    def after(value, *deps):
+        return lax.optimization_barrier((value,) + deps)[0]
 
     def send_blocks(values, cp_index, width=None):
         got = []
@@ -634,9 +676,6 @@
         f_blk = b_up1.shape[0]
         sub = f_blk // N_PART
         qk = N_HEADS * HEAD_DIM
-
-        def after(value, *deps):
-            return lax.optimization_barrier((value,) + deps)[0]
 
         seg_pack = jnp.stack([seg_id, seg_pos], axis=1)
         seg_got = send_blocks(seg_pack, cp_index)
@@ -692,12 +731,12 @@
         third(0, ng_own)
         extra_own = whole[0][:, 3 * d_model:]
         wqkv, wo = unpack(extra_own, swap_core(extra_own), r_o, r_in, d_model)
-        od_seq = attention(cp_index, after(ng_blocks, dbs[0]), n_got, g_got, wqkv, wo, cos_b, sin_b, seg_own)
+        od_seq = attention(cp_index, ng_blocks, n_got, g_got, wqkv, wo, cos_b, sin_b, seg_own)
         d_keep, d_send = attn_grad(cp_index, ng_blocks, n_got, g_got, od_seq, r_o, r_in)
         od_blocks = od_seq.reshape(n_seq, piece, -1)
         od_got = send_blocks(od_blocks, cp_index)
         third(1, ng_own, (d_keep, swap_core(d_send)))
-        third(2, after(ng_own, dbs[1]))
+        third(2, ng_own)
 
         wd_off = lambda col: 3 * col + 2
         w12_off = lambda col: col
@@ -723,9 +762,9 @@
         zero = jnp.zeros_like(db)
         db = jnp.where(first, jnp.stack([db, zero], axis=2), jnp.stack([zero, db], axis=2)).reshape(2, 16, f_blk)
         small = jnp.concatenate([sums[0], sums[1], db[0], db[1]], axis=1)
-        small = lax.psum(small, ALL_AXES)
-        small = lax.dynamic_index_in_dim(small, lax.axis_index(ALL_AXES), 0, keepdims=False)
-        g_scale, g_bias, g_b1, g_b2 = small[:r_in], small[r_in:2 * r_in], small[2 * r_in:2 * r_in + f_blk], small[2 * r_in + f_blk:]
+        small = jnp.pad(small, ((0, 0), (0, 1024 - small.shape[1]))).reshape(16, 8, 128)
+        small = small_sum(small).reshape(1024)
+        g_scale, g_bias, g_b1, g_b2 = small[:r_in], small[r_in:2 * r_in], small[2 * r_in:2 * r_in + f_blk], small[2 * r_in + f_blk:2 * r_in + 2 * f_blk]
 
         g_w1, g_w2, g_wd = join_up(owns, recvs)
         g_attn = owns[1][:r_o + r_in, 3 * d_model:]

time: 1180 us -> 1160 us (0.983)
  blocking collectives: 47.3 us -> 15.1 us
    psum x1 -> x0, blocking collectives: 32.2 us -> none  [local_step(): small = lax.psum(small, ALL_AXES)]
  transfers between devices with their start and end apart: 26 -> 26, of which waited for: 11 -> 11; matrix products, arithmetic and copies ran while one was open for 4% -> 4% of each run, Pallas kernels for 49% -> 51%
where the time goes in v4:
time: 1160 us
  Pallas kernels  607 us (52%)
  waiting for transfers between devices  450 us (39%)
  local copies, waits for them, and re-layouts  39.6 us (3%)
  starting transfers between devices  17.7 us (2%)
  blocking collectives  15.1 us (1%)
  between operations  14.5 us (1%)
  other arithmetic  11.8 us (1%)
    ppermute x12, waiting for transfers between devices, send_blocks(): lax.ppermute(sent, ('z', 'y'), [(i, i ^ flip) for i in range(4)])  342 us
    pallas_call x3, Pallas kernels, hidden_part(): pl.pallas_call(hidden_kernel, grid=(steps,), in_specs=[own_spec, oth_spec...  282 us
    pallas_call x2, Pallas kernels, own_call(): pl.pallas_call(kernel, grid_spec=pltpu.PrefetchScalarGridSpec(num_scalar_...  98.2 us
    all_gather x2, waiting for transfers between devices, gather(): return lax.all_gather(shard, CHIPS, axis=0, tiled=True)  85.5 us
    pallas_call x1, Pallas kernels, attention(): pl.pallas_call(attn_kernel, grid_spec=pltpu.PrefetchScalarGridSpec(num_sc...  84.5 us
    pallas_call x2, Pallas kernels, out_other(): pl.pallas_call(functools.partial(other_kernel, product), grid=(t_len // O...  76.8 us
  transfers between devices with their start and end apart: 26, of which 11 were waited for; matrix products, arithmetic and copies ran while one was open for 4% of the time, Pallas kernels for 51%

profile of v4, /device:TPU:0, one launch (start us, length us, event | category | flops | bytes accessed | tf_op | source)
XLA Modules:
  0.0 1155.9 jit_solution(16863139587519931881)
XLA Ops:
  7.2 4.8 split_up.1
  12.0 0.7 collective-permute-start.1
  12.8 1.9 pack.1.extra_ref
  15.2 0.9 copy-done.2
  16.1 4.2 stack_up.1
  20.4 0.7 all-gather.6.cloned.1.call-update
  21.1 1.4 vectors.1
  22.5 15.1 %all-gather = bf16[128,512]{1,0:T(8,128)(2,1)S(1)} all-gather(bf16[8,512]{1,0:T(8,128)(2,1)} %vectors.1), channel_id=2, replica_groups=mesh['z'=2,'y'=2,'x'=2,'core'=2] {'z','y','x','core'}, dimensions={0}, use_global_device_ids=true | all-gather | bytes 139264 | tf_op jit(solution)/shard_map/all_gather | solution.py:693
  38.2 0.7 reshape.153.scale_ref.refs_14_
  38.9 8.4 norm.1.own_ref.refs_12_
  48.6 0.7 reshape_squeeze.29.b1_ref
  49.9 0.7 reshape_squeeze.31.b2_ref
  50.6 11.7 %collective-permute-done.oth_ref = bf16[2048,2304]{1,0:T(8,128)(2,1)} collective-permute-done((bf16[2048,2304]{1,0:T(8,128)(2,1)}, bf16[2048,2304]{1,0:T(8,128)(2,1)}, u32[]{:S(2)}, u32[]{:S(2)}) %collective-permute-start) | collective-permute-done | bytes 9437216 | tf_op jit(solution)/shard_map/ppermute | solution.py:656
  62.3 54.9 %all-gather.4.cloned.1.call-done.w_ref.refs_3_ = bf16[1152,4992]{1,0:T(8,128)(2,1)} async-done(((bf16[144,4992]{1,0:T(8,128)(2,1)}), bf16[1152,4992]{1,0:T(8,128)(2,1)}) %all-gather.4.cloned.1.call-update) | async-done | bytes 11501584 | tf_op jit(solution)/shard_map/all_gather | solution.py:688
  117.2 92.9 %hidden.3 = (bf16[4096,1152]{1,0:T(8,128)(2,1)}, bf16[4096,2304]{1,0:T(8,128)(2,1)}, f32[1152,3456]{1,0:T(8,128)}, f32[16,1152]{1,0:T(8,128)}) custom-call(bf16[2048,2304]{1,0:T(8,128)(2,1)} %norm.1.own_ref.refs_12_, bf16[2048,2304]{1,0:T(8,128)(2,1)} %collective-permute-done.oth_ref, bf16[1152,4992]{1,0:T(8,128)(2,1)} %all-gather.4.cloned.1.call-done.w_ref.refs_3_, ...), custom_call_target="tpu_custom_call" | custom-call | flops 65000001536 | bytes 70000000 | tf_op jit(solution)/shard_map/hidden/pallas_call | solution.py:402
  210.3 0.7 reshape_squeeze.34.b1_ref
  211.6 30.6 %all-gather.6.cloned.1.call-done.w_ref.refs_4_.refs_5_ = bf16[1152,6912]{1,0:T(8,128)(2,1)} async-done(((bf16[144,6912]{1,0:T(8,128)(2,1)}), bf16[1152,6912]{1,0:T(8,128)(2,1)}) %all-gather.6.cloned.1.call-update) | async-done | bytes 15925264 | tf_op jit(solution)/shard_map/all_gather | solution.py:688
  242.2 94.0 %hidden.5 = (bf16[4096,1152]{1,0:T(8,128)(2,1)}, bf16[4096,2304]{1,0:T(8,128)(2,1)}, f32[1152,3456]{1,0:T(8,128)}, f32[16,1152]{1,0:T(8,128)}) custom-call(bf16[2048,2304]{1,0:T(8,128)(2,1)} %norm.1.own_ref.refs_12_, bf16[2048,2304]{1,0:T(8,128)(2,1)} %collective-permute-done.oth_ref, bf16[1152,6912]{1,0:T(8,128)(2,1)} %all-gather.6.cloned.1.call-done.w_ref.refs_4_.refs_5_, ...), custom_call_target="tpu_custom_call" | custom-call | flops 65000001536 | bytes 70000000 | tf_op jit(solution)/shard_map/hidden/pallas_call | solution.py:402
  336.3 2.5 slice.176.own_ref
  338.9 5.2 constant_dynamic-slice_fusion.6
  344.1 1.5 collective-permute-start.2
  345.6 0.9 fusion.7
  347.0 1.5 collective-permute-start.10
  348.5 1.5 collective-permute-start.11
  350.0 4.5 constant_dynamic-slice_fusion.3
  354.5 31.7 %collective-permute-done.9 = s32[1,2,512]{2,0,1:T(1,128)S(1)} collective-permute-done((s32[1,2,512]{2,0,1:T(1,128)S(1)}, s32[1,2,512]{2,0,1:T(1,128)S(1)}, u32[]{:S(2)}, u32[]{:S(2)}) %collective-permute-start.9) | collective-permute-done | bytes 4128 | tf_op jit(solution)/shard_map/ppermute | solution.py:665
  386.2 1.5 collective-permute-start.3
  387.6 1.5 collective-permute-start.4
  389.7 1.5 collective-permute-start.6
  391.1 1.5 collective-permute-start.7
  392.9 3.7 fusion
  396.6 1.9 pad_maximum_fusion
  398.5 6.0 unpack.1
  404.6 61.2 %collective-permute-done.3.n2_ref = bf16[1,512,1152]{2,1,0:T(8,128)(2,1)} collective-permute-done((bf16[1,512,1152]{2,1,0:T(8,128)(2,1)}, bf16[1,512,1152]{2,1,0:T(8,128)(2,1)}, u32[]{:S(2)}, u32[]{:S(2)}) %collective-permute-start.3) | collective-permute-done | bytes 1179680 | tf_op jit(solution)/shard_map/ppermute | solution.py:665
  465.8 10.0 collective-permute-done.5.g1_ref
  475.8 63.6 %collective-permute-done.6.g2_ref = bf16[1,512,1152]{2,1,0:T(8,128)(2,1)} collective-permute-done((bf16[1,512,1152]{2,1,0:T(8,128)(2,1)}, bf16[1,512,1152]{2,1,0:T(8,128)(2,1)}, u32[]{:S(2)}, u32[]{:S(2)}) %collective-permute-start.6) | collective-permute-done | bytes 1179680 | tf_op jit(solution)/shard_map/ppermute | solution.py:665
  539.5 1.4 broadcast_in_dim.46.segq_ref
  541.4 84.5 %attn.1.dqkv_ref.o_lo_ref.o_hi_ref = bf16[2048,2560]{1,0:T(8,128)(2,1)} custom-call(s32[1]{0:T(128)} %bitcast.cp_ref, bf16[4,512,2304]{2,1,0:T(8,128)(2,1)} %bitcast.58, bf16[1,512,1152]{2,1,0:T(8,128)(2,1)} %collective-permute-done.2.n1_ref, bf16[1,512,1152]{2,1,0:T(8,128)(2,1)} %collective-permute-done.3.n2_ref, ...), custom_call_target="tpu_custom_call" | custom-call | flops 44999999488 | bytes 40000000 | tf_op jit(solution)/shard_map/attn/pallas_call | solution.py:157
  626.0 23.2 %attn_grad.1 = (f32[8,136,1536]{2,1,0:T(8,128)}, f32[8,136,1536]{2,1,0:T(8,128)}) custom-call(s32[1]{0:T(128)} %bitcast.cp_ref, bf16[4,512,2304]{2,1,0:T(8,128)(2,1)} %bitcast.59, bf16[1,512,1152]{2,1,0:T(8,128)(2,1)} %collective-permute-done.2.n1_ref, bf16[1,512,1152]{2,1,0:T(8,128)(2,1)} %collective-permute-done.3.n2_ref, ...), custom_call_target="tpu_custom_call" | custom-call | flops 12000000000 | bytes 33000000 | tf_op jit(solution)/shard_map/attn_grad/pallas_call | solution.py:462
  649.1 0.7 reshape_squeeze.32.b1_ref
  649.8 0.7 reshape_squeeze.33.b2_ref
  650.5 9.7 collective-permute-done.12.refs_1_
  660.2 95.4 %hidden.4 = (bf16[4096,1152]{1,0:T(8,128)(2,1)}, bf16[4096,2304]{1,0:T(8,128)(2,1)}, f32[1152,4992]{1,0:T(8,128)}, f32[16,1152]{1,0:T(8,128)}) custom-call(bf16[2048,2304]{1,0:T(8,128)(2,1)} %norm.1.own_ref.refs_12_, bf16[2048,2304]{1,0:T(8,128)(2,1)} %collective-permute-done.oth_ref, bf16[1152,6912]{1,0:T(8,128)(2,1)} %all-gather.6.cloned.1.call-done.w_ref.refs_4_.refs_5_, ...), custom_call_target="tpu_custom_call" | custom-call | flops 65000001536 | bytes 70000000 | tf_op jit(solution)/shard_map/hidden/pallas_call | solution.py:402
  755.6 26.9 %shard_map.263 = f32[2048,1152]{1,0:T(8,128)} custom-call(bf16[4096,1152]{1,0:T(8,128)(2,1)} %get-tuple-element.65.refs_0_, bf16[4096,1152]{1,0:T(8,128)(2,1)} %get-tuple-element.66.refs_1_, bf16[4096,1152]{1,0:T(8,128)(2,1)} %get-tuple-element.67.refs_2_, bf16[1152,4992]{1,0:T(8,128)(2,1)} %all-gather.4.cloned.1.call-done.w_ref.refs_3_, ...), custom_call_target="tpu_custom_call" | custom-call | flops 16307453952 | bytes 50000000 | tf_op jit(solution)/shard_map/pallas_call | solution.py:546
  782.7 49.8 %shard_map.264 = f32[2048,1152]{1,0:T(8,128)} custom-call(bf16[4096,2304]{1,0:T(8,128)(2,1)} %get-tuple-element.68.refs_0_, bf16[4096,2304]{1,0:T(8,128)(2,1)} %get-tuple-element.69.refs_1_, bf16[4096,2304]{1,0:T(8,128)(2,1)} %get-tuple-element.70.refs_2_, bf16[1152,4992]{1,0:T(8,128)(2,1)} %all-gather.4.cloned.1.call-done.w_ref.refs_3_, ...), custom_call_target="tpu_custom_call" | custom-call | flops 32614907904 | bytes 50000000 | tf_op jit(solution)/shard_map/pallas_call | solution.py:546
  833.2 6.6 constant_dynamic-slice_fusion
  839.8 1.5 collective-permute-start.13
  841.3 1.4 collective-permute-start.14
  843.3 0.7 add.55.refs_17_
  844.8 98.0 %collective-permute-done.13.refs_8_.refs_9_.refs_7_ = bf16[1,512,2560]{2,1,0:T(8,128)(2,1)} collective-permute-done((bf16[1,512,2560]{2,1,0:T(8,128)(2,1)}, bf16[1,512,2560]{2,1,0:T(8,128)(2,1)}, u32[]{:S(2)}, u32[]{:S(2)}) %collective-permute-start.13) | collective-permute-done | bytes 2621472 | tf_op jit(solution)/shard_map/ppermute | solution.py:665
  942.8 77.4 %collective-permute-done.15.refs_12_.refs_13_.refs_9_ = bf16[1,512,2560]{2,1,0:T(8,128)(2,1)} collective-permute-done((bf16[1,512,2560]{2,1,0:T(8,128)(2,1)S(1)}, bf16[1,512,2560]{2,1,0:T(8,128)(2,1)}, u32[]{:S(2)}, u32[]{:S(2)}) %collective-permute-start.15) | collective-permute-done | bytes 2621472 | tf_op jit(solution)/shard_map/ppermute | solution.py:665
  1020.2 35.1 %shard_map.265 = bf16[2048,1152]{1,0:T(8,128)(2,1)} custom-call(s32[1]{0:T(128)} %bitcast.cp_ref, bf16[4096,1152]{1,0:T(8,128)(2,1)} %get-tuple-element.65.refs_0_, bf16[4096,1152]{1,0:T(8,128)(2,1)} %get-tuple-element.66.refs_1_, bf16[4096,1152]{1,0:T(8,128)(2,1)} %get-tuple-element.67.refs_2_, ...), custom_call_target="tpu_custom_call" | custom-call | flops 21139292160 | bytes 80000000 | tf_op jit(solution)/shard_map/pallas_call | solution.py:608
  1055.3 63.0 %shard_map.266 = (bf16[2048,1152]{1,0:T(8,128)(2,1)}, f32[16,1152]{1,0:T(8,128)}) custom-call(s32[1]{0:T(128)} %bitcast.cp_ref, bf16[4096,2304]{1,0:T(8,128)(2,1)} %get-tuple-element.68.refs_0_, bf16[4096,2304]{1,0:T(8,128)(2,1)} %get-tuple-element.69.refs_1_, bf16[4096,2304]{1,0:T(8,128)(2,1)} %get-tuple-element.70.refs_2_, ...), custom_call_target="tpu_custom_call" | custom-call | flops 37446746112 | bytes 80000000 | tf_op jit(solution)/shard_map/pallas_call | solution.py:608
  1118.4 0.9 bitcast_reduce_fusion.3
  1120.2 7.4 small_sum.1
  1127.7 1.4 slice_select_fusion.2
  1129.2 1.4 slice_select_fusion
  1131.0 1.4 slice_select_fusion.1
  1133.7 1.7 slice.187
  1135.4 1.7 slice.190
  1137.1 1.6 fusion.11
  1138.7 0.8 copy-done.3
  1139.8 0.9 copy-done.5
  1140.6 7.9 join_up.1
  (109 shorter events, 11.8 us)
Async XLA Ops:
  7.2 110.1 %all-gather.4.cloned.1.call-start = ((), (), s32[]{:S(2)}) async-start(), calls=%async_computation.3 | async-start | bytes 12939264 | tf_op jit(solution)/shard_map/all_gather | solution.py:688
  12.0 3.2 collective-permute-start.1
  15.2 0.9 copy-start.2
  20.3 221.9 %all-gather.6.cloned.1.call-start = ((), (), s32[]{:S(2)}) async-start(), calls=%async_computation.4 | async-start | bytes 17915904 | tf_op jit(solution)/shard_map/all_gather | solution.py:688
  21.1 1106.6 %reduce-scatter.6.cloned.1.call-start = ((), (), s32[]{:S(2)}) async-start(), calls=%async_computation.6 | async-start | bytes 17915904 | tf_op jit(solution)/shard_map/reduce_scatter | solution.py:724
  47.3 15.0 %collective-permute-start = (bf16[2048,2304]{1,0:T(8,128)(2,1)}, bf16[2048,2304]{1,0:T(8,128)(2,1)}, u32[]{:S(2)}, u32[]{:S(2)}) collective-permute-start(bf16[2048,2304]{1,0:T(8,128)(2,1)} %norm.1.own_ref.refs_12_), channel_id=1, source_target_pairs={{0,1},{1,0},{2,3},{3,2},{4,5},{5,4},{6,7},{7,6},{8,9},{9,8},{10,11... | collective-permute-start | bytes 28311560 | tf_op jit(solution)/shard_map/ppermute | solution.py:656
  210.2 919.0 %reduce-scatter.8.cloned.1.call-start = ((), (), s32[]{:S(2)}) async-start(), calls=%async_computation.7 | async-start | bytes 17915904 | tf_op jit(solution)/shard_map/reduce_scatter | solution.py:724
  336.2 794.8 %reduce-scatter.4.cloned.1.call-start = ((), (), s32[]{:S(2)}) async-start(), calls=%async_computation.5 | async-start | bytes 25878528 | tf_op jit(solution)/shard_map/reduce_scatter | solution.py:724
  338.8 5.3 copy-start
  338.8 52.3 %collective-permute-start.8 = (bf16[1152,1536]{1,0:T(8,128)(2,1)S(1)}, bf16[1152,1536]{1,0:T(8,128)(2,1)}, u32[]{:S(2)}, u32[]{:S(2)}) collective-permute-start(bf16[1152,1536]{1,0:T(8,128)(2,1)S(1)} %slice.176.own_ref), channel_id=1, source_target_pairs={{0,1},{1,0},{2,3},{3,2},{4,5},{5,4},{6,7},{7,6},{8,9},{9,8},{10,11... | collective-permute-start | bytes 10616840 | tf_op jit(solution)/shard_map/ppermute | solution.py:656
  338.9 6.7 copy-start.13
  344.1 45.6 %collective-permute-start.2 = (bf16[1,512,1152]{2,1,0:T(8,128)(2,1)}, bf16[1,512,1152]{2,1,0:T(8,128)(2,1)}, u32[]{:S(2)}, u32[]{:S(2)}) collective-permute-start(bf16[1,512,1152]{2,1,0:T(8,128)(2,1)} %get-tuple-element.95), channel_id=1, source_target_pairs={{0,4},{4,0},{8,12},{12,8},{1,5},{5,1},{9,13},{13,9},{2,6},{6,2},{1... | collective-permute-start | bytes 3538952 | tf_op jit(solution)/shard_map/ppermute | solution.py:665
  346.4 39.7 %collective-permute-start.9 = (s32[1,2,512]{2,0,1:T(1,128)S(1)}, s32[1,2,512]{2,0,1:T(1,128)S(1)}, u32[]{:S(2)}, u32[]{:S(2)}) collective-permute-start(s32[1,2,512]{2,0,1:T(1,128)S(1)} %get-tuple-element.112), channel_id=1, source_target_pairs={{0,4},{4,0},{8,12},{12,8},{1,5},{5,1},{9,13},{13,9},{2,6},{6,2},{1... | collective-permute-start | bytes 12296 | tf_op jit(solution)/shard_map/ppermute | solution.py:665
  347.0 40.6 %collective-permute-start.10 = (s32[1,2,512]{2,0,1:T(1,128)S(1)}, s32[1,2,512]{2,0,1:T(1,128)S(1)}, u32[]{:S(2)}, u32[]{:S(2)}) collective-permute-start(s32[1,2,512]{2,0,1:T(1,128)S(1)} %get-tuple-element.113), channel_id=1, source_target_pairs={{0,8},{4,12},{8,0},{12,4},{1,9},{5,13},{9,1},{13,5},{2,10},{6,14},... | collective-permute-start | bytes 12296 | tf_op jit(solution)/shard_map/ppermute | solution.py:665
  348.5 40.6 %collective-permute-start.11 = (s32[1,2,512]{2,0,1:T(1,128)S(1)}, s32[1,2,512]{2,0,1:T(1,128)S(1)}, u32[]{:S(2)}, u32[]{:S(2)}) collective-permute-start(s32[1,2,512]{2,0,1:T(1,128)S(1)} %get-tuple-element.110), channel_id=1, source_target_pairs={{0,12},{4,8},{8,4},{12,0},{1,13},{5,9},{9,5},{13,1},{2,14},{6,10},... | collective-permute-start | bytes 12296 | tf_op jit(solution)/shard_map/ppermute | solution.py:665
  386.2 79.6 %collective-permute-start.3 = (bf16[1,512,1152]{2,1,0:T(8,128)(2,1)}, bf16[1,512,1152]{2,1,0:T(8,128)(2,1)}, u32[]{:S(2)}, u32[]{:S(2)}) collective-permute-start(bf16[1,512,1152]{2,1,0:T(8,128)(2,1)} %get-tuple-element.94), channel_id=1, source_target_pairs={{0,8},{4,12},{8,0},{12,4},{1,9},{5,13},{9,1},{13,5},{2,10},{6,14},... | collective-permute-start | bytes 3538952 | tf_op jit(solution)/shard_map/ppermute | solution.py:665
  387.6 78.2 %collective-permute-start.4 = (bf16[1,512,1152]{2,1,0:T(8,128)(2,1)}, bf16[1,512,1152]{2,1,0:T(8,128)(2,1)}, u32[]{:S(2)}, u32[]{:S(2)}) collective-permute-start(bf16[1,512,1152]{2,1,0:T(8,128)(2,1)} %get-tuple-element.93), channel_id=1, source_target_pairs={{0,12},{4,8},{8,4},{12,0},{1,13},{5,9},{9,5},{13,1},{2,14},{6,10},... | collective-permute-start | bytes 3538952 | tf_op jit(solution)/shard_map/ppermute | solution.py:665
  389.1 86.7 %collective-permute-start.5 = (bf16[1,512,1152]{2,1,0:T(8,128)(2,1)}, bf16[1,512,1152]{2,1,0:T(8,128)(2,1)}, u32[]{:S(2)}, u32[]{:S(2)}) collective-permute-start(bf16[1,512,1152]{2,1,0:T(8,128)(2,1)} %get-tuple-element.97), channel_id=1, source_target_pairs={{0,4},{4,0},{8,12},{12,8},{1,5},{5,1},{9,13},{13,9},{2,6},{6,2},{1... | collective-permute-start | bytes 3538952 | tf_op jit(solution)/shard_map/ppermute | solution.py:665
  389.7 149.8 %collective-permute-start.6 = (bf16[1,512,1152]{2,1,0:T(8,128)(2,1)}, bf16[1,512,1152]{2,1,0:T(8,128)(2,1)}, u32[]{:S(2)}, u32[]{:S(2)}) collective-permute-start(bf16[1,512,1152]{2,1,0:T(8,128)(2,1)} %get-tuple-element.98), channel_id=1, source_target_pairs={{0,8},{4,12},{8,0},{12,4},{1,9},{5,13},{9,1},{13,5},{2,10},{6,14},... | collective-permute-start | bytes 3538952 | tf_op jit(solution)/shard_map/ppermute | solution.py:665
  391.1 148.3 %collective-permute-start.7 = (bf16[1,512,1152]{2,1,0:T(8,128)(2,1)}, bf16[1,512,1152]{2,1,0:T(8,128)(2,1)S(1)}, u32[]{:S(2)}, u32[]{:S(2)}) collective-permute-start(bf16[1,512,1152]{2,1,0:T(8,128)(2,1)} %get-tuple-element.96), channel_id=1, source_target_pairs={{0,12},{4,8},{8,4},{12,0},{1,13},{5,9},{9,5},{13,1},{2,14},{6,10},... | collective-permute-start | bytes 3538952 | tf_op jit(solution)/shard_map/ppermute | solution.py:665
  539.4 2.0 copy-start.1
  625.9 23.2 %copy-start.11 = (f32[8,144]{1,0:T(8,128)S(1)}, f32[8,144]{1,0:T(8,128)}, u32[]{:S(2)}) copy-start(f32[8,144]{1,0:T(8,128)} %get-tuple-element.86) | copy-start | bytes 13828
  626.0 23.9 %copy-start.12 = (f32[8,144]{1,0:T(8,128)S(1)}, f32[8,144]{1,0:T(8,128)}, u32[]{:S(2)}) copy-start(f32[8,144]{1,0:T(8,128)} %get-tuple-element.83) | copy-start | bytes 13828
  649.1 11.1 collective-permute-start.12
  782.6 237.6 %collective-permute-start.16 = (f32[2048,1152]{1,0:T(8,128)}, f32[2048,1152]{1,0:T(8,128)}, u32[]{:S(2)}, u32[]{:S(2)}) collective-permute-start(f32[2048,1152]{1,0:T(8,128)} %shard_map.263), channel_id=1, source_target_pairs={{0,1},{1,0},{2,3},{3,2},{4,5},{5,4},{6,7},{7,6},{8,9},{9,8},{10,11... | collective-permute-start | bytes 28311560 | tf_op jit(solution)/shard_map/ppermute | solution.py:656
  832.5 222.8 %collective-permute-start.17 = (f32[2048,1152]{1,0:T(8,128)}, f32[2048,1152]{1,0:T(8,128)}, u32[]{:S(2)}, u32[]{:S(2)}) collective-permute-start(f32[2048,1152]{1,0:T(8,128)} %shard_map.264), channel_id=1, source_target_pairs={{0,1},{1,0},{2,3},{3,2},{4,5},{5,4},{6,7},{7,6},{8,9},{9,8},{10,11... | collective-permute-start | bytes 28311560 | tf_op jit(solution)/shard_map/ppermute | solution.py:656
  833.2 10.1 copy-start.9
  833.2 10.1 copy-start.10
  833.2 10.8 copy-start.6
  833.2 11.0 copy-start.7
  833.2 11.1 copy-start.8
  839.8 103.0 %collective-permute-start.13 = (bf16[1,512,2560]{2,1,0:T(8,128)(2,1)}, bf16[1,512,2560]{2,1,0:T(8,128)(2,1)}, u32[]{:S(2)}, u32[]{:S(2)}) collective-permute-start(bf16[1,512,2560]{2,1,0:T(8,128)(2,1)} %get-tuple-element.92), channel_id=1, source_target_pairs={{0,4},{4,0},{8,12},{12,8},{1,5},{5,1},{9,13},{13,9},{2,6},{6,2},{1... | collective-permute-start | bytes 7864328 | tf_op jit(solution)/shard_map/ppermute | solution.py:665
  841.3 101.5 %collective-permute-start.14 = (bf16[1,512,2560]{2,1,0:T(8,128)(2,1)}, bf16[1,512,2560]{2,1,0:T(8,128)(2,1)}, u32[]{:S(2)}, u32[]{:S(2)}) collective-permute-start(bf16[1,512,2560]{2,1,0:T(8,128)(2,1)} %get-tuple-element.91), channel_id=1, source_target_pairs={{0,8},{4,12},{8,0},{12,4},{1,9},{5,13},{9,1},{13,5},{2,10},{6,14},... | collective-permute-start | bytes 7864328 | tf_op jit(solution)/shard_map/ppermute | solution.py:665
  842.7 177.5 %collective-permute-start.15 = (bf16[1,512,2560]{2,1,0:T(8,128)(2,1)S(1)}, bf16[1,512,2560]{2,1,0:T(8,128)(2,1)}, u32[]{:S(2)}, u32[]{:S(2)}) collective-permute-start(bf16[1,512,2560]{2,1,0:T(8,128)(2,1)S(1)} %get-tuple-element.90), channel_id=1, source_target_pairs={{0,12},{4,8},{8,4},{12,0},{1,13},{5,9},{9,5},{13,1},{2,14},{6,10},... | collective-permute-start | bytes 7864328 | tf_op jit(solution)/shard_map/ppermute | solution.py:665
  1127.7 4.9 copy-start.14
  1129.1 9.6 collective-permute-start.18
  1130.6 8.1 collective-permute-start.20
  1132.4 6.3 collective-permute-start.19
  1133.1 15.5 %copy-start.15 = (f32[72]{0:T(128)}, f32[72]{0:T(128)S(1)}, u32[]{:S(2)}) copy-start(f32[72]{0:T(128)S(1)} %get-tuple-element.152) | copy-start | bytes 868
  1138.7 0.8 copy-start.3
  1138.7 1.1 copy-start.4
  1139.8 0.9 copy-start.5
Sparse Core Ops, SparseCore 0:
  20.5 96.7 all-gather.3
  120.0 122.2 all-gather.5
  246.5 136.6 reduce-scatter.5
  387.4 216.4 reduce-scatter.7
  755.8 232.3 reduce-scatter.3

commit v5 on v4

--- a/solution.py
+++ b/solution.py
@@ -271,10 +271,10 @@
 
 
 def join_kernel(*refs):
-    own_refs, recv_refs, (w1_ref, w2_ref, wd_ref) = refs[:N_PART], refs[N_PART:2 * N_PART], refs[2 * N_PART:]
+    own_refs, recv_refs, (w1_ref, w2_ref) = refs[:N_PART], refs[N_PART:2 * N_PART], refs[2 * N_PART:]
     core = lax.axis_index('core')
     rows = w1_ref.shape[0]
-    d_model = wd_ref.shape[1]
+    d_model = recv_refs[0].shape[1] // 2
     sub = d_model // 8
 
     def put(even_of, odd_of):
@@ -288,16 +288,16 @@
 
     pl.when(core == 0)(lambda: put(lambda p: own_refs[p][:rows, :2 * d_model], lambda p: recv_refs[p][...]))
     pl.when(core == 1)(lambda: put(lambda p: recv_refs[p][...], lambda p: own_refs[p][rows:, :2 * d_model]))
-    for part in range(N_PART):
-        wd_ref[part * 2 * rows:(part + 1) * 2 * rows, :] = own_refs[part][:, 2 * d_model:3 * d_model]
 
 
 def join_up(owns, recvs):
     rows, cols = recvs[0].shape
-    d_model = cols // 2
     up = jax.ShapeDtypeStruct((rows, N_PART * cols), F32)
-    return pl.pallas_call(
-        join_kernel, out_shape=[up, up, jax.ShapeDtypeStruct((N_PART * 2 * rows, d_model), F32)], name='join_up',
+    first_cols = pl.BlockSpec((2 * rows, cols), lambda i: (0, 0))
+    whole = lambda width: pl.BlockSpec((rows, width), lambda i: (0, 0))
+    return pl.pallas_call(
+        join_kernel, out_shape=[up, up], name='join_up', grid=(1,),
+        in_specs=[first_cols] * N_PART + [whole(cols)] * N_PART, out_specs=[whole(N_PART * cols)] * 2,
     )(*owns, *recvs)
 
 
@@ -766,7 +766,8 @@
         small = small_sum(small).reshape(1024)
         g_scale, g_bias, g_b1, g_b2 = small[:r_in], small[r_in:2 * r_in], small[2 * r_in:2 * r_in + f_blk], small[2 * r_in + f_blk:2 * r_in + 2 * f_blk]
 
-        g_w1, g_w2, g_wd = join_up(owns, recvs)
+        g_w1, g_w2 = join_up(owns, recvs)
+        g_wd = jnp.concatenate([own[:, 2 * d_model:3 * d_model] for own in owns], axis=0)
         g_attn = owns[1][:r_o + r_in, 3 * d_model:]
         g_wo, g_wq, g_wk, g_wv = g_attn[:r_o, :d_model], g_attn[r_o:, :qk], g_attn[r_o:, qk:qk + HEAD_DIM], g_attn[r_o:, qk + HEAD_DIM:]
         return (x_out, d_x, g_scale, g_wq, g_wk, g_wv, g_wo, g_bias, g_w1, g_b1, g_w2, g_b2, g_wd, g_bias)

time: 1160 us -> 1160 us (level)
  no operation moved by 1% of the time
where the time goes in v5:
time: 1160 us; the launch traced here: 1150 us
  Pallas kernels  605 us (52%)
  waiting for transfers between devices  450 us (39%)
  local copies, waits for them, and re-layouts  35.6 us (3%)
  starting transfers between devices  17.7 us (2%)
  blocking collectives  15.1 us (1%)
  other arithmetic  15 us (1%)
  between operations  14.5 us (1%)
    ppermute x12, waiting for transfers between devices, send_blocks(): lax.ppermute(sent, ('z', 'y'), [(i, i ^ flip) for i in range(4)])  342 us
    pallas_call x3, Pallas kernels, hidden_part(): pl.pallas_call(hidden_kernel, grid=(steps,), in_specs=[own_spec, oth_spec...  282 us
    pallas_call x2, Pallas kernels, own_call(): pl.pallas_call(kernel, grid_spec=pltpu.PrefetchScalarGridSpec(num_scalar_...  98.2 us
    all_gather x2, waiting for transfers between devices, gather(): return lax.all_gather(shard, CHIPS, axis=0, tiled=True)  85.6 us
    pallas_call x1, Pallas kernels, attention(): pl.pallas_call(attn_kernel, grid_spec=pltpu.PrefetchScalarGridSpec(num_sc...  84.5 us
    pallas_call x2, Pallas kernels, out_other(): pl.pallas_call(functools.partial(other_kernel, product), grid=(t_len // O...  76.8 us
  transfers between devices with their start and end apart: 26, of which 11 were waited for; matrix products, arithmetic and copies ran while one was open for 4% of the time, Pallas kernels for 51%

profile of v5, /device:TPU:0, one launch (start us, length us, event | category | flops | bytes accessed | tf_op | source)
XLA Modules:
  0.0 1153.4 jit_solution(4947145612602054901)
XLA Ops:
  7.2 4.8 split_up.1
  12.0 0.7 collective-permute-start.1
  12.8 1.9 pack.1.extra_ref
  15.2 0.9 copy-done.3
  16.1 4.2 stack_up.1
  20.4 0.7 all-gather.6.cloned.1.call-update
  21.1 1.4 vectors.1
  22.5 15.1 %all-gather = bf16[128,512]{1,0:T(8,128)(2,1)S(1)} all-gather(bf16[8,512]{1,0:T(8,128)(2,1)} %vectors.1), channel_id=2, replica_groups=mesh['z'=2,'y'=2,'x'=2,'core'=2] {'z','y','x','core'}, dimensions={0}, use_global_device_ids=true | all-gather | bytes 139264 | tf_op jit(solution)/shard_map/all_gather | solution.py:693
  38.2 0.7 reshape.153.scale_ref.refs_14_
  38.9 8.4 norm.1.own_ref.refs_12_
  48.6 0.7 reshape_squeeze.29.b1_ref
  49.9 0.7 reshape_squeeze.31.b2_ref
  50.6 11.7 %collective-permute-done.oth_ref = bf16[2048,2304]{1,0:T(8,128)(2,1)} collective-permute-done((bf16[2048,2304]{1,0:T(8,128)(2,1)}, bf16[2048,2304]{1,0:T(8,128)(2,1)}, u32[]{:S(2)}, u32[]{:S(2)}) %collective-permute-start) | collective-permute-done | bytes 9437216 | tf_op jit(solution)/shard_map/ppermute | solution.py:656
  62.3 54.9 %all-gather.4.cloned.1.call-done.w_ref.refs_3_ = bf16[1152,4992]{1,0:T(8,128)(2,1)} async-done(((bf16[144,4992]{1,0:T(8,128)(2,1)}), bf16[1152,4992]{1,0:T(8,128)(2,1)}) %all-gather.4.cloned.1.call-update) | async-done | bytes 11501584 | tf_op jit(solution)/shard_map/all_gather | solution.py:688
  117.2 92.9 %hidden.3 = (bf16[4096,1152]{1,0:T(8,128)(2,1)}, bf16[4096,2304]{1,0:T(8,128)(2,1)}, f32[1152,3456]{1,0:T(8,128)}, f32[16,1152]{1,0:T(8,128)}) custom-call(bf16[2048,2304]{1,0:T(8,128)(2,1)} %norm.1.own_ref.refs_12_, bf16[2048,2304]{1,0:T(8,128)(2,1)} %collective-permute-done.oth_ref, bf16[1152,4992]{1,0:T(8,128)(2,1)} %all-gather.4.cloned.1.call-done.w_ref.refs_3_, ...), custom_call_target="tpu_custom_call" | custom-call | flops 65000001536 | bytes 70000000 | tf_op jit(solution)/shard_map/hidden/pallas_call | solution.py:402
  210.2 0.7 reshape_squeeze.34.b1_ref
  211.6 30.6 %all-gather.6.cloned.1.call-done.w_ref.refs_4_.refs_5_ = bf16[1152,6912]{1,0:T(8,128)(2,1)} async-done(((bf16[144,6912]{1,0:T(8,128)(2,1)}), bf16[1152,6912]{1,0:T(8,128)(2,1)}) %all-gather.6.cloned.1.call-update) | async-done | bytes 15925264 | tf_op jit(solution)/shard_map/all_gather | solution.py:688
  242.2 94.0 %hidden.5 = (bf16[4096,1152]{1,0:T(8,128)(2,1)}, bf16[4096,2304]{1,0:T(8,128)(2,1)}, f32[1152,3456]{1,0:T(8,128)}, f32[16,1152]{1,0:T(8,128)}) custom-call(bf16[2048,2304]{1,0:T(8,128)(2,1)} %norm.1.own_ref.refs_12_, bf16[2048,2304]{1,0:T(8,128)(2,1)} %collective-permute-done.oth_ref, bf16[1152,6912]{1,0:T(8,128)(2,1)} %all-gather.6.cloned.1.call-done.w_ref.refs_4_.refs_5_, ...), custom_call_target="tpu_custom_call" | custom-call | flops 65000001536 | bytes 70000000 | tf_op jit(solution)/shard_map/hidden/pallas_call | solution.py:402
  336.3 2.5 slice.188.own_ref
  338.9 5.2 constant_dynamic-slice_fusion.6
  344.1 1.5 collective-permute-start.2
  345.5 0.9 fusion.7
  347.0 1.5 collective-permute-start.10
  348.5 1.5 collective-permute-start.11
  349.9 4.5 constant_dynamic-slice_fusion.3
  354.5 31.7 %collective-permute-done.9 = s32[1,2,512]{2,0,1:T(1,128)S(1)} collective-permute-done((s32[1,2,512]{2,0,1:T(1,128)S(1)}, s32[1,2,512]{2,0,1:T(1,128)S(1)}, u32[]{:S(2)}, u32[]{:S(2)}) %collective-permute-start.9) | collective-permute-done | bytes 4128 | tf_op jit(solution)/shard_map/ppermute | solution.py:665
  386.1 1.5 collective-permute-start.3
  387.6 1.5 collective-permute-start.4
  389.6 1.5 collective-permute-start.6
  391.1 1.5 collective-permute-start.7
  392.9 3.7 fusion
  396.6 1.9 pad_maximum_fusion.1
  398.5 6.1 unpack.1
  404.6 61.2 %collective-permute-done.3.n2_ref = bf16[1,512,1152]{2,1,0:T(8,128)(2,1)} collective-permute-done((bf16[1,512,1152]{2,1,0:T(8,128)(2,1)}, bf16[1,512,1152]{2,1,0:T(8,128)(2,1)}, u32[]{:S(2)}, u32[]{:S(2)}) %collective-permute-start.3) | collective-permute-done | bytes 1179680 | tf_op jit(solution)/shard_map/ppermute | solution.py:665
  465.8 10.0 collective-permute-done.5.g1_ref
  475.8 63.6 %collective-permute-done.6.g2_ref = bf16[1,512,1152]{2,1,0:T(8,128)(2,1)} collective-permute-done((bf16[1,512,1152]{2,1,0:T(8,128)(2,1)}, bf16[1,512,1152]{2,1,0:T(8,128)(2,1)}, u32[]{:S(2)}, u32[]{:S(2)}) %collective-permute-start.6) | collective-permute-done | bytes 1179680 | tf_op jit(solution)/shard_map/ppermute | solution.py:665
  539.4 1.4 broadcast_in_dim.46.segq_ref
  541.4 84.5 %attn.1.dqkv_ref.o_lo_ref.o_hi_ref = bf16[2048,2560]{1,0:T(8,128)(2,1)} custom-call(s32[1]{0:T(128)} %bitcast.cp_ref, bf16[4,512,2304]{2,1,0:T(8,128)(2,1)} %bitcast.58, bf16[1,512,1152]{2,1,0:T(8,128)(2,1)} %collective-permute-done.2.n1_ref, bf16[1,512,1152]{2,1,0:T(8,128)(2,1)} %collective-permute-done.3.n2_ref, ...), custom_call_target="tpu_custom_call" | custom-call | flops 44999999488 | bytes 40000000 | tf_op jit(solution)/shard_map/attn/pallas_call | solution.py:157
  625.9 23.1 %attn_grad.1 = (f32[8,136,1536]{2,1,0:T(8,128)}, f32[8,136,1536]{2,1,0:T(8,128)}) custom-call(s32[1]{0:T(128)} %bitcast.cp_ref, bf16[4,512,2304]{2,1,0:T(8,128)(2,1)} %bitcast.59, bf16[1,512,1152]{2,1,0:T(8,128)(2,1)} %collective-permute-done.2.n1_ref, bf16[1,512,1152]{2,1,0:T(8,128)(2,1)} %collective-permute-done.3.n2_ref, ...), custom_call_target="tpu_custom_call" | custom-call | flops 12000000000 | bytes 33000000 | tf_op jit(solution)/shard_map/attn_grad/pallas_call | solution.py:462
  649.1 0.7 reshape_squeeze.32.b1_ref
  649.8 0.7 reshape_squeeze.33.b2_ref
  650.4 9.7 collective-permute-done.12.refs_1_
  660.1 95.5 %hidden.4 = (bf16[4096,1152]{1,0:T(8,128)(2,1)}, bf16[4096,2304]{1,0:T(8,128)(2,1)}, f32[1152,4992]{1,0:T(8,128)}, f32[16,1152]{1,0:T(8,128)}) custom-call(bf16[2048,2304]{1,0:T(8,128)(2,1)} %norm.1.own_ref.refs_12_, bf16[2048,2304]{1,0:T(8,128)(2,1)} %collective-permute-done.oth_ref, bf16[1152,6912]{1,0:T(8,128)(2,1)} %all-gather.6.cloned.1.call-done.w_ref.refs_4_.refs_5_, ...), custom_call_target="tpu_custom_call" | custom-call | flops 65000001536 | bytes 70000000 | tf_op jit(solution)/shard_map/hidden/pallas_call | solution.py:402
  755.7 27.1 %shard_map.263 = f32[2048,1152]{1,0:T(8,128)} custom-call(bf16[4096,1152]{1,0:T(8,128)(2,1)} %get-tuple-element.64.refs_0_, bf16[4096,1152]{1,0:T(8,128)(2,1)} %get-tuple-element.65.refs_1_, bf16[4096,1152]{1,0:T(8,128)(2,1)} %get-tuple-element.66.refs_2_, bf16[1152,4992]{1,0:T(8,128)(2,1)} %all-gather.4.cloned.1.call-done.w_ref.refs_3_, ...), custom_call_target="tpu_custom_call" | custom-call | flops 16307453952 | bytes 50000000 | tf_op jit(solution)/shard_map/pallas_call | solution.py:546
  782.9 49.7 %shard_map.264 = f32[2048,1152]{1,0:T(8,128)} custom-call(bf16[4096,2304]{1,0:T(8,128)(2,1)} %get-tuple-element.67.refs_0_, bf16[4096,2304]{1,0:T(8,128)(2,1)} %get-tuple-element.68.refs_1_, bf16[4096,2304]{1,0:T(8,128)(2,1)} %get-tuple-element.69.refs_2_, bf16[1152,4992]{1,0:T(8,128)(2,1)} %all-gather.4.cloned.1.call-done.w_ref.refs_3_, ...), custom_call_target="tpu_custom_call" | custom-call | flops 32614907904 | bytes 50000000 | tf_op jit(solution)/shard_map/pallas_call | solution.py:546
  832.6 0.7 collective-permute-start.17
  833.3 6.6 constant_dynamic-slice_fusion
  840.0 1.5 collective-permute-start.13
  841.4 1.4 collective-permute-start.14
  843.5 0.7 add.55.refs_17_
  844.9 97.9 %collective-permute-done.13.refs_8_.refs_9_.refs_7_ = bf16[1,512,2560]{2,1,0:T(8,128)(2,1)} collective-permute-done((bf16[1,512,2560]{2,1,0:T(8,128)(2,1)}, bf16[1,512,2560]{2,1,0:T(8,128)(2,1)}, u32[]{:S(2)}, u32[]{:S(2)}) %collective-permute-start.13) | collective-permute-done | bytes 2621472 | tf_op jit(solution)/shard_map/ppermute | solution.py:665
  942.8 77.4 %collective-permute-done.15.refs_12_.refs_13_.refs_9_ = bf16[1,512,2560]{2,1,0:T(8,128)(2,1)} collective-permute-done((bf16[1,512,2560]{2,1,0:T(8,128)(2,1)S(1)}, bf16[1,512,2560]{2,1,0:T(8,128)(2,1)}, u32[]{:S(2)}, u32[]{:S(2)}) %collective-permute-start.15) | collective-permute-done | bytes 2621472 | tf_op jit(solution)/shard_map/ppermute | solution.py:665
  1020.2 35.1 %shard_map.265 = bf16[2048,1152]{1,0:T(8,128)(2,1)} custom-call(s32[1]{0:T(128)} %bitcast.cp_ref, bf16[4096,1152]{1,0:T(8,128)(2,1)} %get-tuple-element.64.refs_0_, bf16[4096,1152]{1,0:T(8,128)(2,1)} %get-tuple-element.65.refs_1_, bf16[4096,1152]{1,0:T(8,128)(2,1)} %get-tuple-element.66.refs_2_, ...), custom_call_target="tpu_custom_call" | custom-call | flops 21139292160 | bytes 80000000 | tf_op jit(solution)/shard_map/pallas_call | solution.py:608
  1055.4 63.1 %shard_map.266 = (bf16[2048,1152]{1,0:T(8,128)(2,1)}, f32[16,1152]{1,0:T(8,128)}) custom-call(s32[1]{0:T(128)} %bitcast.cp_ref, bf16[4096,2304]{1,0:T(8,128)(2,1)} %get-tuple-element.67.refs_0_, bf16[4096,2304]{1,0:T(8,128)(2,1)} %get-tuple-element.68.refs_1_, bf16[4096,2304]{1,0:T(8,128)(2,1)} %get-tuple-element.69.refs_2_, ...), custom_call_target="tpu_custom_call" | custom-call | flops 37446746112 | bytes 80000000 | tf_op jit(solution)/shard_map/pallas_call | solution.py:608
  1118.5 0.9 bitcast_reduce_fusion.3
  1120.3 7.4 small_sum.1
  1127.7 1.3 fusion.16
  1129.0 2.2 slice_select_fusion.2
  1131.3 2.2 slice_select_fusion
  1133.9 1.5 slice_select_fusion.1
  1136.2 0.7 slice.199
  1137.0 0.7 slice.202
  1138.4 1.4 pad_maximum_fusion
  1139.8 6.3 join_up.1
  (112 shorter events, 11.0 us)
Async XLA Ops:
  7.2 110.1 %all-gather.4.cloned.1.call-start = ((), (), s32[]{:S(2)}) async-start(), calls=%async_computation.3 | async-start | bytes 12939264 | tf_op jit(solution)/shard_map/all_gather | solution.py:688
  12.0 3.2 collective-permute-start.1
  15.2 0.9 copy-start.3
  20.3 221.9 %all-gather.6.cloned.1.call-start = ((), (), s32[]{:S(2)}) async-start(), calls=%async_computation.4 | async-start | bytes 17915904 | tf_op jit(solution)/shard_map/all_gather | solution.py:688
  21.1 1107.9 %reduce-scatter.6.cloned.1.call-start = ((), (), s32[]{:S(2)}) async-start(), calls=%async_computation.6 | async-start | bytes 17915904 | tf_op jit(solution)/shard_map/reduce_scatter | solution.py:724
  47.3 15.0 %collective-permute-start = (bf16[2048,2304]{1,0:T(8,128)(2,1)}, bf16[2048,2304]{1,0:T(8,128)(2,1)}, u32[]{:S(2)}, u32[]{:S(2)}) collective-permute-start(bf16[2048,2304]{1,0:T(8,128)(2,1)} %norm.1.own_ref.refs_12_), channel_id=1, source_target_pairs={{0,1},{1,0},{2,3},{3,2},{4,5},{5,4},{6,7},{7,6},{8,9},{9,8},{10,11... | collective-permute-start | bytes 28311560 | tf_op jit(solution)/shard_map/ppermute | solution.py:656
  210.2 921.1 %reduce-scatter.8.cloned.1.call-start = ((), (), s32[]{:S(2)}) async-start(), calls=%async_computation.7 | async-start | bytes 17915904 | tf_op jit(solution)/shard_map/reduce_scatter | solution.py:724
  336.2 797.7 %reduce-scatter.4.cloned.1.call-start = ((), (), s32[]{:S(2)}) async-start(), calls=%async_computation.5 | async-start | bytes 25878528 | tf_op jit(solution)/shard_map/reduce_scatter | solution.py:724
  338.8 5.3 copy-start
  338.8 52.3 %collective-permute-start.8 = (bf16[1152,1536]{1,0:T(8,128)(2,1)S(1)}, bf16[1152,1536]{1,0:T(8,128)(2,1)}, u32[]{:S(2)}, u32[]{:S(2)}) collective-permute-start(bf16[1152,1536]{1,0:T(8,128)(2,1)S(1)} %slice.188.own_ref), channel_id=1, source_target_pairs={{0,1},{1,0},{2,3},{3,2},{4,5},{5,4},{6,7},{7,6},{8,9},{9,8},{10,11... | collective-permute-start | bytes 10616840 | tf_op jit(solution)/shard_map/ppermute | solution.py:656
  338.8 6.7 copy-start.11
  344.1 45.6 %collective-permute-start.2 = (bf16[1,512,1152]{2,1,0:T(8,128)(2,1)}, bf16[1,512,1152]{2,1,0:T(8,128)(2,1)}, u32[]{:S(2)}, u32[]{:S(2)}) collective-permute-start(bf16[1,512,1152]{2,1,0:T(8,128)(2,1)} %get-tuple-element.93), channel_id=1, source_target_pairs={{0,4},{4,0},{8,12},{12,8},{1,5},{5,1},{9,13},{13,9},{2,6},{6,2},{1... | collective-permute-start | bytes 3538952 | tf_op jit(solution)/shard_map/ppermute | solution.py:665
  346.4 39.7 %collective-permute-start.9 = (s32[1,2,512]{2,0,1:T(1,128)S(1)}, s32[1,2,512]{2,0,1:T(1,128)S(1)}, u32[]{:S(2)}, u32[]{:S(2)}) collective-permute-start(s32[1,2,512]{2,0,1:T(1,128)S(1)} %get-tuple-element.110), channel_id=1, source_target_pairs={{0,4},{4,0},{8,12},{12,8},{1,5},{5,1},{9,13},{13,9},{2,6},{6,2},{1... | collective-permute-start | bytes 12296 | tf_op jit(solution)/shard_map/ppermute | solution.py:665
  347.0 40.6 %collective-permute-start.10 = (s32[1,2,512]{2,0,1:T(1,128)S(1)}, s32[1,2,512]{2,0,1:T(1,128)S(1)}, u32[]{:S(2)}, u32[]{:S(2)}) collective-permute-start(s32[1,2,512]{2,0,1:T(1,128)S(1)} %get-tuple-element.111), channel_id=1, source_target_pairs={{0,8},{4,12},{8,0},{12,4},{1,9},{5,13},{9,1},{13,5},{2,10},{6,14},... | collective-permute-start | bytes 12296 | tf_op jit(solution)/shard_map/ppermute | solution.py:665
  348.5 40.6 %collective-permute-start.11 = (s32[1,2,512]{2,0,1:T(1,128)S(1)}, s32[1,2,512]{2,0,1:T(1,128)S(1)}, u32[]{:S(2)}, u32[]{:S(2)}) collective-permute-start(s32[1,2,512]{2,0,1:T(1,128)S(1)} %get-tuple-element.108), channel_id=1, source_target_pairs={{0,12},{4,8},{8,4},{12,0},{1,13},{5,9},{9,5},{13,1},{2,14},{6,10},... | collective-permute-start | bytes 12296 | tf_op jit(solution)/shard_map/ppermute | solution.py:665
  386.1 79.6 %collective-permute-start.3 = (bf16[1,512,1152]{2,1,0:T(8,128)(2,1)}, bf16[1,512,1152]{2,1,0:T(8,128)(2,1)}, u32[]{:S(2)}, u32[]{:S(2)}) collective-permute-start(bf16[1,512,1152]{2,1,0:T(8,128)(2,1)} %get-tuple-element.92), channel_id=1, source_target_pairs={{0,8},{4,12},{8,0},{12,4},{1,9},{5,13},{9,1},{13,5},{2,10},{6,14},... | collective-permute-start | bytes 3538952 | tf_op jit(solution)/shard_map/ppermute | solution.py:665
  387.6 78.2 %collective-permute-start.4 = (bf16[1,512,1152]{2,1,0:T(8,128)(2,1)}, bf16[1,512,1152]{2,1,0:T(8,128)(2,1)}, u32[]{:S(2)}, u32[]{:S(2)}) collective-permute-start(bf16[1,512,1152]{2,1,0:T(8,128)(2,1)} %get-tuple-element.91), channel_id=1, source_target_pairs={{0,12},{4,8},{8,4},{12,0},{1,13},{5,9},{9,5},{13,1},{2,14},{6,10},... | collective-permute-start | bytes 3538952 | tf_op jit(solution)/shard_map/ppermute | solution.py:665
  389.1 86.7 %collective-permute-start.5 = (bf16[1,512,1152]{2,1,0:T(8,128)(2,1)}, bf16[1,512,1152]{2,1,0:T(8,128)(2,1)}, u32[]{:S(2)}, u32[]{:S(2)}) collective-permute-start(bf16[1,512,1152]{2,1,0:T(8,128)(2,1)} %get-tuple-element.95), channel_id=1, source_target_pairs={{0,4},{4,0},{8,12},{12,8},{1,5},{5,1},{9,13},{13,9},{2,6},{6,2},{1... | collective-permute-start | bytes 3538952 | tf_op jit(solution)/shard_map/ppermute | solution.py:665
  389.6 149.8 %collective-permute-start.6 = (bf16[1,512,1152]{2,1,0:T(8,128)(2,1)}, bf16[1,512,1152]{2,1,0:T(8,128)(2,1)}, u32[]{:S(2)}, u32[]{:S(2)}) collective-permute-start(bf16[1,512,1152]{2,1,0:T(8,128)(2,1)} %get-tuple-element.96), channel_id=1, source_target_pairs={{0,8},{4,12},{8,0},{12,4},{1,9},{5,13},{9,1},{13,5},{2,10},{6,14},... | collective-permute-start | bytes 3538952 | tf_op jit(solution)/shard_map/ppermute | solution.py:665
  391.1 148.3 %collective-permute-start.7 = (bf16[1,512,1152]{2,1,0:T(8,128)(2,1)}, bf16[1,512,1152]{2,1,0:T(8,128)(2,1)S(1)}, u32[]{:S(2)}, u32[]{:S(2)}) collective-permute-start(bf16[1,512,1152]{2,1,0:T(8,128)(2,1)} %get-tuple-element.94), channel_id=1, source_target_pairs={{0,12},{4,8},{8,4},{12,0},{1,13},{5,9},{9,5},{13,1},{2,14},{6,10},... | collective-permute-start | bytes 3538952 | tf_op jit(solution)/shard_map/ppermute | solution.py:665
  539.4 2.0 copy-start.2
  625.9 23.1 %copy-start.9 = (f32[8,144]{1,0:T(8,128)S(1)}, f32[8,144]{1,0:T(8,128)}, u32[]{:S(2)}) copy-start(f32[8,144]{1,0:T(8,128)} %get-tuple-element.84) | copy-start | bytes 13828
  625.9 23.8 %copy-start.10 = (f32[8,144]{1,0:T(8,128)S(1)}, f32[8,144]{1,0:T(8,128)}, u32[]{:S(2)}) copy-start(f32[8,144]{1,0:T(8,128)} %get-tuple-element.81) | copy-start | bytes 13828
  649.0 11.1 collective-permute-start.12
  782.7 237.5 %collective-permute-start.16 = (f32[2048,1152]{1,0:T(8,128)}, f32[2048,1152]{1,0:T(8,128)}, u32[]{:S(2)}, u32[]{:S(2)}) collective-permute-start(f32[2048,1152]{1,0:T(8,128)} %shard_map.263), channel_id=1, source_target_pairs={{0,1},{1,0},{2,3},{3,2},{4,5},{5,4},{6,7},{7,6},{8,9},{9,8},{10,11... | collective-permute-start | bytes 28311560 | tf_op jit(solution)/shard_map/ppermute | solution.py:656
  832.6 222.8 %collective-permute-start.17 = (f32[2048,1152]{1,0:T(8,128)}, f32[2048,1152]{1,0:T(8,128)}, u32[]{:S(2)}, u32[]{:S(2)}) collective-permute-start(f32[2048,1152]{1,0:T(8,128)} %shard_map.264), channel_id=1, source_target_pairs={{0,1},{1,0},{2,3},{3,2},{4,5},{5,4},{6,7},{7,6},{8,9},{9,8},{10,11... | collective-permute-start | bytes 28311560 | tf_op jit(solution)/shard_map/ppermute | solution.py:656
  833.3 10.2 copy-start.7
  833.3 10.2 copy-start.8
  833.3 10.9 copy-start.4
  833.3 11.0 copy-start.5
  833.3 11.1 copy-start.6
  840.0 102.8 %collective-permute-start.13 = (bf16[1,512,2560]{2,1,0:T(8,128)(2,1)}, bf16[1,512,2560]{2,1,0:T(8,128)(2,1)}, u32[]{:S(2)}, u32[]{:S(2)}) collective-permute-start(bf16[1,512,2560]{2,1,0:T(8,128)(2,1)} %get-tuple-element.90), channel_id=1, source_target_pairs={{0,4},{4,0},{8,12},{12,8},{1,5},{5,1},{9,13},{13,9},{2,6},{6,2},{1... | collective-permute-start | bytes 7864328 | tf_op jit(solution)/shard_map/ppermute | solution.py:665
  841.4 101.4 %collective-permute-start.14 = (bf16[1,512,2560]{2,1,0:T(8,128)(2,1)}, bf16[1,512,2560]{2,1,0:T(8,128)(2,1)}, u32[]{:S(2)}, u32[]{:S(2)}) collective-permute-start(bf16[1,512,2560]{2,1,0:T(8,128)(2,1)} %get-tuple-element.89), channel_id=1, source_target_pairs={{0,8},{4,12},{8,0},{12,4},{1,9},{5,13},{9,1},{13,5},{2,10},{6,14},... | collective-permute-start | bytes 7864328 | tf_op jit(solution)/shard_map/ppermute | solution.py:665
  842.8 177.4 %collective-permute-start.15 = (bf16[1,512,2560]{2,1,0:T(8,128)(2,1)S(1)}, bf16[1,512,2560]{2,1,0:T(8,128)(2,1)}, u32[]{:S(2)}, u32[]{:S(2)}) collective-permute-start(bf16[1,512,2560]{2,1,0:T(8,128)(2,1)S(1)} %get-tuple-element.88), channel_id=1, source_target_pairs={{0,12},{4,8},{8,4},{12,0},{1,13},{5,9},{9,5},{13,1},{2,14},{6,10},... | collective-permute-start | bytes 7864328 | tf_op jit(solution)/shard_map/ppermute | solution.py:665
  1129.0 17.1 %copy-start.13 = (f32[72]{0:T(128)}, f32[72]{0:T(128)S(1)}, u32[]{:S(2)}) copy-start(f32[72]{0:T(128)S(1)} %get-tuple-element.150) | copy-start | bytes 868
  1129.0 6.6 copy-start.12
  1131.2 8.6 collective-permute-start.18
  1133.5 6.3 collective-permute-start.20
  1133.9 2.3 copy-start.1
  1135.4 4.4 collective-permute-start.19
  1136.2 2.1 slice-start
  1136.2 2.1 slice-start.1
  1136.2 2.1 slice-start.2
Sparse Core Ops, SparseCore 0:
  20.5 96.7 all-gather.3
  120.0 122.2 all-gather.5
  246.5 136.6 reduce-scatter.5
  387.4 216.4 reduce-scatter.7
  755.8 232.2 reduce-scatter.3
